TPU v7x, 32 devices: a whole 2x2x4 slice. The times are simulated.
32 devices in a mesh: tensor: 4 (over z), replica: 2 (over y), fsdp: 4 (over x, core).
Axes of the slice: x: 2, y: 2, z: 4, core: 2. Of those that a mesh axis runs over, the one named last changes fastest.
Arguments:
- x_tokens: bfloat16 [2048, 2048], P(('replica', 'fsdp'))
- dy_tokens: bfloat16 [2048, 2048], P(('replica', 'fsdp'))
- w_gate: bfloat16 [2, 2048, 8192], P(None, 'fsdp', 'tensor')
- w_up: bfloat16 [2, 2048, 8192], P(None, 'fsdp', 'tensor')
- w_down: bfloat16 [2, 8192, 2048], P(None, ('tensor', 'fsdp'))
- norm_gain: float32 [2, 2048], replicated
Outputs:
- output 1: bfloat16 [2048, 2048], P(('replica', 'fsdp'))
- output 2: float32 [2, 2048, 8192], P(None, 'fsdp', 'tensor')
- output 3: float32 [2, 2048, 8192], P(None, 'fsdp', 'tensor')
- output 4: float32 [2, 8192, 2048], P(None, ('tensor', 'fsdp'))
- output 5: float32 [2, 2048], replicated
All inputs are finite; a program needn't handle non-finite values.
Results may differ from a plain program's by a relative error of at most 0.00785844.
Values are sent between devices in bfloat16 or wider.
A program may use at most 1 GiB of HBM per device.

v0:
```python
import jax
import jax.numpy as jnp
from jax import lax
from jax.sharding import PartitionSpec as P, NamedSharding


def norm_input(h_cur, gain_vec):
    h_f = h_cur.astype(jnp.float32)
    r_inv = lax.rsqrt(jnp.mean(h_f * h_f, axis=-1, keepdims=True) + 1e-6)
    return h_f, r_inv, (h_f * r_inv * gain_vec).astype(jnp.bfloat16)


def hidden_forward(normed, full_gate, full_up):
    gate_val = jnp.dot(normed, full_gate, preferred_element_type=jnp.float32).astype(jnp.bfloat16)
    up_val = jnp.dot(normed, full_up, preferred_element_type=jnp.float32).astype(jnp.bfloat16)
    act_val = (jax.nn.silu(gate_val.astype(jnp.float32)) * up_val.astype(jnp.float32)).astype(jnp.bfloat16)
    return gate_val, up_val, act_val


def hidden_backward(d_act, gate_val, up_val):
    gate_f = gate_val.astype(jnp.float32)
    sig_gate = jax.nn.sigmoid(gate_f)
    d_act_f = d_act.astype(jnp.float32)
    d_gate = (d_act_f * up_val.astype(jnp.float32) * sig_gate * (1.0 + gate_f * (1.0 - sig_gate))).astype(jnp.bfloat16)
    d_up = (d_act_f * gate_f * sig_gate).astype(jnp.bfloat16)
    return d_gate, d_up


def solution(mesh):
    tok_spec = P(("replica", "fsdp"), None)
    wide_spec = P(None, "fsdp", "tensor")
    down_spec = P(None, ("tensor", "fsdp"), None)
    gain_spec = P(None, None)

    def gather_layer(w_gate, w_up, w_down, layer_idx):
        full_gate = lax.all_gather(w_gate[layer_idx], "fsdp", axis=0, tiled=True)
        full_up = lax.all_gather(w_up[layer_idx], "fsdp", axis=0, tiled=True)
        full_down = lax.all_gather(w_down[layer_idx], "fsdp", axis=0, tiled=True)
        return full_gate, full_up, full_down

    def device_fn(x_loc, dy_loc, w_gate, w_up, w_down, norm_gain):
        layers = w_gate.shape[0]
        h_cur = x_loc
        saved_acts = []
        for layer_idx in range(layers):
            full_gate, full_up, full_down = gather_layer(w_gate, w_up, w_down, layer_idx)
            h_f, r_inv, normed = norm_input(h_cur, norm_gain[layer_idx])
            gate_val, up_val, act_val = hidden_forward(normed, full_gate, full_up)
            mlp_out = lax.psum(jnp.dot(act_val, full_down, preferred_element_type=jnp.float32), "tensor")
            saved_acts.append((h_cur, r_inv, normed, gate_val, up_val, act_val))
            h_cur = (h_f + mlp_out).astype(jnp.bfloat16)
        d_resid = dy_loc.astype(jnp.float32)
        part_gate = [None] * layers
        part_up = [None] * layers
        part_down = [None] * layers
        part_gain = [None] * layers
        for layer_idx in reversed(range(layers)):
            full_gate, full_up, full_down = gather_layer(w_gate, w_up, w_down, layer_idx)
            h_in, r_inv, normed, gate_val, up_val, act_val = saved_acts[layer_idx]
            d_out = d_resid.astype(jnp.bfloat16)
            d_act = jnp.einsum("td,fd->tf", d_out, full_down, preferred_element_type=jnp.float32).astype(jnp.bfloat16)
            part_down[layer_idx] = jnp.einsum("tf,td->fd", act_val, d_out, preferred_element_type=jnp.float32)
            d_gate, d_up = hidden_backward(d_act, gate_val, up_val)
            part_gate[layer_idx] = jnp.einsum("td,tf->df", normed, d_gate, preferred_element_type=jnp.float32)
            part_up[layer_idx] = jnp.einsum("td,tf->df", normed, d_up, preferred_element_type=jnp.float32)
            d_normed = lax.psum(jnp.einsum("tf,df->td", d_gate, full_gate, preferred_element_type=jnp.float32) + jnp.einsum("tf,df->td", d_up, full_up, preferred_element_type=jnp.float32), "tensor")
            x_hat = h_in.astype(jnp.float32) * r_inv
            part_gain[layer_idx] = jnp.sum(d_normed * x_hat, axis=0)
            if layer_idx > 0:
                v_term = d_normed * norm_gain[layer_idx]
                d_resid = d_resid + r_inv * (v_term - x_hat * jnp.mean(v_term * x_hat, axis=-1, keepdims=True))
        grad_gate = []
        grad_up = []
        grad_down = []
        for layer_idx in range(layers):
            grad_gate.append(lax.psum(lax.psum_scatter(part_gate[layer_idx], "fsdp", scatter_dimension=0, tiled=True), "replica"))
            grad_up.append(lax.psum(lax.psum_scatter(part_up[layer_idx], "fsdp", scatter_dimension=0, tiled=True), "replica"))
            grad_down.append(lax.psum(lax.psum_scatter(part_down[layer_idx], "fsdp", scatter_dimension=0, tiled=True), "replica"))
        d_gain = lax.psum(jnp.stack(part_gain), ("replica", "fsdp"))
        return h_cur, jnp.stack(grad_gate), jnp.stack(grad_up), jnp.stack(grad_down), d_gain

    return jax.shard_map(device_fn, mesh=mesh, in_specs=(tok_spec, tok_spec, wide_spec, wide_spec, down_spec, gain_spec), out_specs=(tok_spec, wide_spec, wide_spec, down_spec, gain_spec), check_vma=False)
```

profile of v0, /device:TPU:0, one launch (start us, length us, event | category | flops | bytes accessed | tf_op | source)
XLA Modules:
  0.0 2067.1 jit_solution(15566928663564076982)
XLA Ops:
  7.2 4.8 fusion.114
  12.1 4.9 fusion.115
  17.1 4.8 fusion.116
  23.4 50.0 %all-gather.13.cloned.1.call-done = bf16[1,2048,2048]{2,1,0:T(8,128)(2,1)} async-done(((bf16[1,512,2048]{2,1,0:T(8,128)(2,1)}), bf16[1,2048,2048]{2,1,0:T(8,128)(2,1)}) %all-gather.13.cloned.1.call-update) | async-done | bytes 8388624 | tf_op jit(solution)/shard_map/all_gather | solution.py:36
  73.5 5.8 fusion.34
  79.2 54.9 %all-gather.15.cloned.1.call-done = bf16[1,2048,2048]{2,1,0:T(8,128)(2,1)} async-done(((bf16[1,512,2048]{2,1,0:T(8,128)(2,1)}), bf16[1,2048,2048]{2,1,0:T(8,128)(2,1)}) %all-gather.15.cloned.1.call-update) | async-done | bytes 8388624 | tf_op jit(solution)/shard_map/all_gather | solution.py:37
  134.1 5.8 fusion.37
  139.9 54.9 %all-gather.17.cloned.1.call-done = bf16[1,2048,2048]{2,1,0:T(8,128)(2,1)} async-done(((bf16[1,512,2048]{2,1,0:T(8,128)(2,1)}), bf16[1,2048,2048]{2,1,0:T(8,128)(2,1)}) %all-gather.17.cloned.1.call-update) | async-done | bytes 8388624 | tf_op jit(solution)/shard_map/all_gather | solution.py:38
  194.8 7.2 fusion.14
  204.0 51.4 %all-gather.23.cloned.1.call-done = bf16[1,2048,2048]{2,1,0:T(8,128)(2,1)} async-done(((bf16[1,512,2048]{2,1,0:T(8,128)(2,1)}), bf16[1,2048,2048]{2,1,0:T(8,128)(2,1)}) %all-gather.23.cloned.1.call-update) | async-done | bytes 8388624 | tf_op jit(solution)/shard_map/all_gather | solution.py:38
  255.4 6.7 fusion.49
  262.1 81.7 %all-reduce.7.cloned.1.call-done = f32[256,2048]{1,0:T(8,128)} async-done(((f32[256,2048]{1,0:T(8,128)}), f32[256,2048]{1,0:T(8,128)}) %all-reduce.7.cloned.1.call-update) | async-done | bytes 2097168 | tf_op jit(solution)/shard_map/psum | solution.py:49
  343.8 2.0 fusion.73
  345.8 57.4 %all-gather.19.cloned.1.call-done = bf16[1,2048,2048]{2,1,0:T(8,128)(2,1)} async-done(((bf16[1,512,2048]{2,1,0:T(8,128)(2,1)}), bf16[1,2048,2048]{2,1,0:T(8,128)(2,1)}) %all-gather.19.cloned.1.call-update) | async-done | bytes 8388624 | tf_op jit(solution)/shard_map/all_gather | solution.py:36
  403.1 6.7 fusion.43
  409.9 53.4 %all-gather.21.cloned.1.call-done = bf16[1,2048,2048]{2,1,0:T(8,128)(2,1)} async-done(((bf16[1,512,2048]{2,1,0:T(8,128)(2,1)}), bf16[1,2048,2048]{2,1,0:T(8,128)(2,1)}) %all-gather.21.cloned.1.call-update) | async-done | bytes 8388624 | tf_op jit(solution)/shard_map/all_gather | solution.py:37
  463.2 5.9 fusion.46
  469.2 6.3 fusion.4
  475.5 4.2 fusion.31
  480.0 10.3 fusion.89
  490.4 9.8 fusion.87
  500.3 10.2 fusion.103
  510.5 55.0 %all-reduce.9.cloned.1.call-done = f32[256,2048]{1,0:T(8,128)} async-done(((f32[256,2048]{1,0:T(8,128)}), f32[256,2048]{1,0:T(8,128)}) %all-reduce.9.cloned.1.call-update) | async-done | bytes 2097168 | tf_op jit(solution)/shard_map/psum | solution.py:66
  565.6 2.4 fusion.72
  568.8 1.0 copy-done.13
  569.8 8.3 fusion.106
  578.4 6.1 fusion.40
  584.5 1.0 copy-done.11
  585.5 8.5 fusion.95
  594.1 9.6 fusion.93
  604.0 8.0 fusion.2
  612.0 6.0 fusion.16
  618.0 7.6 fusion.28
  625.7 66.2 %reduce-scatter.9.cloned.1.call-done = f32[512,2048]{1,0:T(8,128)} async-done(((f32[2048,2048]{1,0:T(8,128)}), f32[512,2048]{1,0:T(8,128)}) %reduce-scatter.9.cloned.1.call-update) | async-done | bytes 4194320 | tf_op jit(solution)/shard_map/reduce_scatter | solution.py:76
  691.9 126.8 %reduce-scatter.13.cloned.1.call-done = f32[512,2048]{1,0:T(8,128)} async-done(((f32[2048,2048]{1,0:T(8,128)}), f32[512,2048]{1,0:T(8,128)}) %reduce-scatter.13.cloned.1.call-update) | async-done | bytes 4194320 | tf_op jit(solution)/shard_map/reduce_scatter | solution.py:77
  818.6 126.9 %reduce-scatter.17.cloned.1.call-done = f32[512,2048]{1,0:T(8,128)} async-done(((f32[2048,2048]{1,0:T(8,128)}), f32[512,2048]{1,0:T(8,128)}) %reduce-scatter.17.cloned.1.call-update) | async-done | bytes 4194320 | tf_op jit(solution)/shard_map/reduce_scatter | solution.py:78
  945.5 126.8 %reduce-scatter.15.cloned.1.call-done = f32[512,2048]{1,0:T(8,128)} async-done(((f32[2048,2048]{1,0:T(8,128)}), f32[512,2048]{1,0:T(8,128)}) %reduce-scatter.15.cloned.1.call-update) | async-done | bytes 4194320 | tf_op jit(solution)/shard_map/reduce_scatter | solution.py:78
  1072.3 126.9 %reduce-scatter.7.cloned.1.call-done = f32[512,2048]{1,0:T(8,128)} async-done(((f32[2048,2048]{1,0:T(8,128)}), f32[512,2048]{1,0:T(8,128)}) %reduce-scatter.7.cloned.1.call-update) | async-done | bytes 4194320 | tf_op jit(solution)/shard_map/reduce_scatter | solution.py:76
  1199.2 126.8 %reduce-scatter.11.cloned.1.call-done = f32[512,2048]{1,0:T(8,128)} async-done(((f32[2048,2048]{1,0:T(8,128)}), f32[512,2048]{1,0:T(8,128)}) %reduce-scatter.11.cloned.1.call-update) | async-done | bytes 4194320 | tf_op jit(solution)/shard_map/reduce_scatter | solution.py:77
  1326.0 156.8 %all-reduce.11.cloned.1.call-done = (f32[256,2048]{1,0:T(8,128)}, f32[256,2048]{1,0:T(8,128)}) async-done(((f32[256,2048]{1,0:T(8,128)}, f32[256,2048]{1,0:T(8,128)}), (f32[256,2048]{1,0:T(8,128)}, f32[256,2048]{1,0:T(8,128)})) %all-reduce.11.cloned.1.call-update) | async-done | bytes 4194320 | tf_op jit(solution)/shard_map/psum | solution.py:49
  1482.7 1.9 fusion.55
  1484.7 24.2 %psum.87 = f32[2,2048]{1,0:T(2,128)} all-reduce(f32[2,2048]{1,0:T(2,128)S(1)} %pad_maximum_fusion.3), channel_id=1, replica_groups=mesh['tensor'=4,'replica'=2,'fsdp'=4] {'replica','fsdp'}, use_global_device_ids=true, to_apply=%region_21.22 | all-reduce | flops 4096 | bytes 32768 | tf_op jit(solution)/shard_map/psum | solution.py:79
  1508.9 2.8 fusion.74
  1511.7 530.6 %all-reduce.13.cloned.1.call-done = (f32[1,512,2048]{2,1,0:T(8,128)}, f32[1,512,2048]{2,1,0:T(8,128)}, f32[1,512,2048]{2,1,0:T(8,128)}, f32[1,512,2048]{2,1,0:T(...) async-done(((f32[1,512,2048]{2,1,0:T(8,128)}, f32[1,512,2048]{2,1,0:T(8,128)}, f32[1,512,2048]{2,1,0:T(8,128)}, f32[1,512,2048]{2,1,0:T(8,128)}, ...) | async-done | bytes 25165840 | tf_op jit(solution)/shard_map/psum | solution.py:76
  2042.3 9.0 pad_maximum_fusion.2
  2051.3 1.2 copy-done.16
  2052.5 1.2 copy-done.17
  2053.7 6.5 pad_maximum_fusion
  (75 shorter events, 5.6 us)
Async XLA Ops:
  7.2 66.3 %all-gather.13.cloned.1.call-start = ((), (), s32[]{:S(2)}) async-start(), calls=%async_computation.14 | async-start | bytes 10485760 | tf_op jit(solution)/shard_map/all_gather | solution.py:36
  12.1 122.1 %all-gather.15.cloned.1.call-start = ((), (), s32[]{:S(2)}) async-start(), calls=%async_computation.15 | async-start | bytes 10485760 | tf_op jit(solution)/shard_map/all_gather | solution.py:37
  17.0 177.8 %all-gather.17.cloned.1.call-start = ((), (), s32[]{:S(2)}) async-start(), calls=%async_computation.16 | async-start | bytes 10485760 | tf_op jit(solution)/shard_map/all_gather | solution.py:38
  21.9 1.2 copy-start
  21.9 1.5 copy-start.18
  21.9 233.4 %all-gather.23.cloned.1.call-start = ((), (), s32[]{:S(2)}) async-start(), calls=%async_computation.19 | async-start | bytes 10485760 | tf_op jit(solution)/shard_map/all_gather | solution.py:38
  22.5 321.3 %all-reduce.7.cloned.1.call-start = ((), (), s32[]{:S(2)}) async-start(), calls=%async_computation.6 | async-start | bytes 4194304 | tf_op jit(solution)/shard_map/psum | solution.py:49
  139.9 62.1 %copy-start.5 = (bf16[256,2048]{1,0:T(8,128)(2,1)}, bf16[256,2048]{1,0:T(8,128)(2,1)S(1)}, u32[]{:S(2)}) copy-start(bf16[256,2048]{1,0:T(8,128)(2,1)S(1)} %fusion.37) | copy-start | bytes 3145732
  202.1 201.1 %all-gather.19.cloned.1.call-start = ((), (), s32[]{:S(2)}) async-start(), calls=%async_computation.17 | async-start | bytes 10485760 | tf_op jit(solution)/shard_map/all_gather | solution.py:36
  202.1 53.2 %copy-start.3 = (bf16[256,2048]{1,0:T(8,128)(2,1)S(1)}, bf16[256,2048]{1,0:T(8,128)(2,1)}, u32[]{:S(2)}) copy-start(bf16[256,2048]{1,0:T(8,128)(2,1)} %param.7) | copy-start | bytes 3145732
  202.7 260.6 %all-gather.21.cloned.1.call-start = ((), (), s32[]{:S(2)}) async-start(), calls=%async_computation.18 | async-start | bytes 10485760 | tf_op jit(solution)/shard_map/all_gather | solution.py:37
  203.4 362.1 %all-reduce.9.cloned.1.call-start = ((), (), s32[]{:S(2)}) async-start(), calls=%async_computation.7 | async-start | bytes 4194304 | tf_op jit(solution)/shard_map/psum | solution.py:66
  463.2 5.9 copy-start.1
  463.2 5.9 copy-start.10
  469.2 6.4 copy-start.9
  469.2 6.4 copy-start.19
  479.8 212.1 %reduce-scatter.9.cloned.1.call-start = ((), (), s32[]{:S(2)}) async-start(), calls=%async_computation.9 | async-start | bytes 20971520 | tf_op jit(solution)/shard_map/reduce_scatter | solution.py:76
  490.3 328.3 %reduce-scatter.13.cloned.1.call-start = ((), (), s32[]{:S(2)}) async-start(), calls=%async_computation.11 | async-start | bytes 20971520 | tf_op jit(solution)/shard_map/reduce_scatter | solution.py:77
  500.2 445.3 %reduce-scatter.17.cloned.1.call-start = ((), (), s32[]{:S(2)}) async-start(), calls=%async_computation.13 | async-start | bytes 20971520 | tf_op jit(solution)/shard_map/reduce_scatter | solution.py:78
  510.5 561.8 %reduce-scatter.15.cloned.1.call-start = ((), (), s32[]{:S(2)}) async-start(), calls=%async_computation.12 | async-start | bytes 20971520 | tf_op jit(solution)/shard_map/reduce_scatter | solution.py:78
  565.6 2.4 copy-start.2
  565.6 2.5 copy-start.4
  568.0 1.7 copy-start.6
  568.8 1.0 copy-start.13
  578.1 621.1 %reduce-scatter.7.cloned.1.call-start = ((), (), s32[]{:S(2)}) async-start(), calls=%async_computation.8 | async-start | bytes 20971520 | tf_op jit(solution)/shard_map/reduce_scatter | solution.py:76
  578.4 7.1 copy-start.7
  584.5 1.0 copy-start.11
  594.0 731.9 %reduce-scatter.11.cloned.1.call-start = ((), (), s32[]{:S(2)}) async-start(), calls=%async_computation.10 | async-start | bytes 20971520 | tf_op jit(solution)/shard_map/reduce_scatter | solution.py:77
  603.7 879.0 %all-reduce.11.cloned.1.call-start = ((), (), s32[]{:S(2)}) async-start(), calls=%async_computation.20 | async-start | bytes 8388608 | tf_op jit(solution)/shard_map/psum | solution.py:49
  604.0 8.0 copy-start.12
  612.0 6.0 copy-start.8
  625.6 1416.7 %all-reduce.13.cloned.1.call-start = ((), (), s32[]{:S(2)}) async-start(), calls=%async_computation.21 | async-start | bytes 50331648 | tf_op jit(solution)/shard_map/psum | solution.py:76
  2042.3 9.0 copy-start.14
  2042.3 9.0 copy-start.15
  2042.3 10.1 copy-start.16
  2042.3 11.3 copy-start.17
Sparse Core Ops, SparseCore 0:
  12.2 61.2 all-gather.12
  75.6 58.4 all-gather.14
  136.3 58.4 all-gather.16
  196.8 58.4 all-gather.22
  258.1 85.5 all-reduce.6
  345.2 57.8 all-gather.18
  404.7 58.4 all-gather.20
  479.9 85.5 all-reduce.8
  568.1 123.6 reduce-scatter.8
  694.3 124.2 reduce-scatter.12
  821.2 124.2 reduce-scatter.16
  947.9 124.2 reduce-scatter.14
  1074.8 124.2 reduce-scatter.6
  1201.6 124.2 reduce-scatter.10
  1328.8 153.9 all-reduce.10
  1485.5 556.7 all-reduce.12
where the time goes:
time: 2070 us
  waiting for transfers between devices  1850 us (89%)
  matrix products  133 us (6%)
  other arithmetic  25.7 us (1%)
  blocking collectives  24.2 us (1%)
    psum x1, waiting for transfers between devices, device_fn(): lax.psum(lax.psum_scatter(part_gate[layer_idx], 'fsdp', scatter_dimension...  531 us
    reduce_scatter x2, waiting for transfers between devices, device_fn(): lax.psum_scatter(part_down[layer_idx], 'fsdp', scatter_dimension=0, tiled...  254 us
    reduce_scatter x2, waiting for transfers between devices, device_fn(): lax.psum_scatter(part_up[layer_idx], 'fsdp', scatter_dimension=0, tiled=T...  254 us
    psum x2, waiting for transfers between devices, device_fn(): lax.psum(jnp.dot(act_val, full_down, preferred_element_type=jnp.float32),...  238 us
    reduce_scatter x2, waiting for transfers between devices, device_fn(): lax.psum_scatter(part_gate[layer_idx], 'fsdp', scatter_dimension=0, tiled...  193 us
    all_gather x2, waiting for transfers between devices, gather_layer(): full_up = lax.all_gather(w_up[layer_idx], 'fsdp', axis=0, tiled=True)  108 us
    all_gather x2, waiting for transfers between devices, gather_layer(): full_gate = lax.all_gather(w_gate[layer_idx], 'fsdp', axis=0, tiled=True)  107 us
    all_gather x2, waiting for transfers between devices, gather_layer(): full_down = lax.all_gather(w_down[layer_idx], 'fsdp', axis=0, tiled=True)  106 us
  transfers between devices with their start and end apart: 16, of which 16 were waited for; matrix products, arithmetic and copies ran while one was open for 7% of the time, Pallas kernels for 0%

commit v1 on v0

v1 whole, which is shorter than its diff:
```python
import functools

import jax
import jax.numpy as jnp
from jax import lax
from jax.experimental import pallas as pl
from jax.experimental.pallas import tpu as pltpu
from jax.sharding import PartitionSpec as P

F32 = jnp.float32
BF16 = jnp.bfloat16
MESH = pl.DeviceIdType.MESH
NSEM = 160
NLOC = 48


def mm(lhs, rhs, ldim, rdim):
    return lax.dot_general(lhs, rhs, (((ldim,), (rdim,)), ((), ())), preferred_element_type=F32)


def kernel(
    x_in, dy_in, wg_in, wu_in, wd_in, gain,
    y_out, dwg_out, dwu_out, dwd_out, dgain_out, n0_buf, n1_buf, o1_buf, o0_buf, a_save, b_save, x_part,
    wg, wu, wd, acc_g, acc_u, acc_d, nb, ob, a_t, b_t, g_t, g_keep, part, from_core, from_z, n_own, o_own,
    x_ch, dy_ch, h1_ch, y_ch, r_own, dg, dg_core, dg_x, dg_y, dg_z, ssem, rsem, lsem,
):
    td, d = x_in.shape
    rb = wg_in.shape[1]
    fb = wg_in.shape[2] // 4
    hh = 2 * fb
    t2, ch, half = 2 * td, td // 4, td // 2
    tile = min(512, fb)
    z = lax.axis_index("tensor")
    y = lax.axis_index("replica")
    f = lax.axis_index("fsdp")
    x, c = f // 2, f % 2
    xo, yo, co = 1 - x, 1 - y, 1 - c
    q, qx, qy, qd = 2 * y + x, 2 * y + xo, 2 * yo + x, 2 * yo + xo
    cs = (c + y) % 2
    cso = 1 - cs
    to_c, to_x, to_xs, to_y = {"fsdp": 2 * x + co}, {"fsdp": 2 * xo + c}, {"fsdp": 2 * xo + cs}, {"replica": yo}

    def to_z(dz):
        return {"tensor": (z + dz) % 4}

    def rows(start, size):
        return pl.ds(pl.multiple_of(start, size if size % 16 == 0 else 8), size)

    def cols(start, size):
        return pl.ds(pl.multiple_of(start, 128), size)

    ids, lids, sent = {}, {}, {}

    def remote(key, src, dst, dev):
        i = ids.setdefault(key, len(ids))
        assert i < NSEM
        return pltpu.make_async_remote_copy(src_ref=src, dst_ref=dst, send_sem=ssem.at[i], recv_sem=rsem.at[i], device_id=dev, device_id_type=MESH)

    def push(key, src, dst, dev, again=None):
        copy = remote(key, src, dst, dev)
        copy.start()
        sent[key] = again or (lambda: copy)

    def got(key, dst):
        remote(key, dst, dst, to_c).wait_recv()

    def send_done(key):
        sent.pop(key)().wait_send()

    def local(key, src, dst):
        i = lids.setdefault(key, len(lids))
        assert i < NLOC
        return pltpu.make_async_copy(src, dst, lsem.at[i])

    def wview(ref, l, row, xb):
        return ref.at[l, rows(row * rb, rb), cols(xb * fb, fb)]

    def wsrc(ref, l, xb, core):
        return ref.at[l, :, cols((2 * xb + core) * fb, fb)]

    gu = ((wg_in, wg), (wu_in, wu))

    barrier = pltpu.get_barrier_semaphore()
    for dev in (to_c, to_x, {"fsdp": 2 * xo + co}, to_y, to_z(1), to_z(2), to_z(3)):
        pl.semaphore_signal(barrier, inc=1, device_id=dev, device_id_type=MESH)
    pl.semaphore_wait(barrier, 7)

    loads = [local("x", x_in, n_own.at[pl.ds(0, td)])]
    loads[0].start()
    for l in range(2):
        for m in range(2):
            for xb in range(2):
                push(("wx", l, m, xb), wsrc(gu[m][0], l, xb, cs), wview(gu[m][1], l, f, xb), to_xs)
        for k in range(2):
            r0 = y * (fb // 2) + k * (fb // 4)
            push(("wdx", l, k), wd_in.at[l, rows(r0, fb // 4)], wd.at[l, rows(x * fb + r0, fb // 4)], to_x)
        for m in range(2):
            for xb in range(2):
                push(("wc", l, m, xb), wsrc(gu[m][0], l, xb, co), wview(gu[m][1], l, f, xb), to_c)
                local(("w", l, m, xb), wsrc(gu[m][0], l, xb, c), wview(gu[m][1], l, f, xb)).start()
        local(("wd", l), wd_in.at[l], wd.at[l, rows(x * fb, fb)]).start()
    push("xp", x_in, x_part, to_c)
    push("dyp", dy_in, o1_buf.at[q, c], to_c)
    local("xc", x_in.at[rows(z * ch, ch)], x_ch).start()
    local("dyc", dy_in.at[rows(z * ch, ch)], dy_ch).start()
    local("dy_own", dy_in, ob.at[0, rows(c * td, td)]).start()

    def ag_x(a, buf, src, h):
        push((a, "x", h), src.at[pl.ds(h * half, half)], buf.at[q, c, pl.ds(h * half, half)], to_x)

    def ag_y(a, buf, src, h):
        push((a, "y", h), src.at[pl.ds(h * half, half)], buf.at[q, c, pl.ds(h * half, half)], to_y)

    def piece(buf, block, core, h):
        return buf.at[block, core, pl.ds(h * half, half)]

    def share(a, buf, j, block, h):
        key = (a, "c", j, h)
        push(key, piece(buf, block, c, h), piece(buf, block, c, h), to_c, lambda: remote(key, piece(buf, block, c, h), piece(buf, block, c, h), to_c))

    def ag_relay_x(a, buf):
        got((a, "y", 0), piece(buf, qy, c, 0))
        push((a, "dx"), piece(buf, qy, c, 0), piece(buf, qy, c, 0), to_x)
        share(a, buf, 1, qy, 0)

    def ag_relay_y(a, buf):
        got((a, "x", 1), piece(buf, qx, c, 1))
        push((a, "dy"), piece(buf, qx, c, 1), piece(buf, qx, c, 1), to_y)
        share(a, buf, 0, qx, 1)

    def ag_share_rest(a, buf):
        got((a, "x", 0), piece(buf, qx, c, 0))
        share(a, buf, 0, qx, 0)
        got((a, "y", 1), piece(buf, qy, c, 1))
        share(a, buf, 1, qy, 1)

    def ag_share_diag(a, buf):
        got((a, "dx"), piece(buf, qd, c, 0))
        share(a, buf, 2, qd, 0)
        got((a, "dy"), piece(buf, qd, c, 1))
        share(a, buf, 2, qd, 1)

    def block_of(j):
        return 2 * ((y + (j + 1) // 2) % 2) + (x + (j + 1) % 2) % 2

    def ag_wait_partner(a, buf, j):
        base = ids.setdefault((a, "c", 0, 0), len(ids))
        for jj in range(3):
            for h in range(2):
                assert ids.setdefault((a, "c", jj, h), len(ids)) == base + 2 * jj + h
        for h in range(2):
            ref = piece(buf, block_of(j), co, h)
            i = base + 2 * j + h
            pltpu.make_async_remote_copy(src_ref=ref, dst_ref=ref, send_sem=ssem.at[i], recv_sem=rsem.at[i], device_id=to_c, device_id_type=MESH).wait_recv()

    for a in ("n0", "o1", "n1", "o0"):
        for j in range(3):
            for h in range(2):
                ids.setdefault((a, "c", j, h), len(ids))

    def fwd(l, n_ref, g_ref):
        def step(i, carry):
            w = cols(i * tile, tile)
            a = mm(n_ref[...], wg[l, :, w], 1, 0).astype(BF16)
            b = mm(n_ref[...], wu[l, :, w], 1, 0).astype(BF16)
            a_t[:, w] = a
            b_t[:, w] = b
            if g_ref is not None:
                a_f = a.astype(F32)
                g_ref[:, w] = (a_f * jax.nn.sigmoid(a_f) * b.astype(F32)).astype(BF16)
            return carry

        lax.fori_loop(0, hh // tile, step, 0)

    def down(l, g_ref):
        def step(i, carry):
            w = cols(i * tile, tile)
            part[:, w] = mm(g_ref[...], wd[l, :, w], 1, 0)
            return carry

        lax.fori_loop(0, d // tile, step, 0)

    def bwd_hidden(l, o_ref):
        tile = min(512, fb)

        def step(i, carry):
            w = cols(i * tile, tile)
            q_f = mm(o_ref[...], wd[l, rows(i * tile, tile)], 1, 1).astype(BF16).astype(F32)
            a_f = a_t[:, w].astype(F32)
            b_f = b_t[:, w].astype(F32)
            s = jax.nn.sigmoid(a_f)
            g_t[:, w] = (a_f * s * b_f).astype(BF16)
            a_t[:, w] = (q_f * b_f * s * (1.0 + a_f * (1.0 - s))).astype(BF16)
            b_t[:, w] = (q_f * a_f * s).astype(BF16)
            return carry

        lax.fori_loop(0, hh // tile, step, 0)

    def m_tile(l, i):
        return mm(a_t[...], wg[l, rows(i * tile, tile)], 1, 1) + mm(b_t[...], wu[l, rows(i * tile, tile)], 1, 1)

    def m_part(l):
        def step(i, carry):
            part[:, cols(i * tile, tile)] = m_tile(l, i)
            return carry

        lax.fori_loop(0, d // tile, step, 0)

    def weight_grads(n_ref, o_ref):
        def step(i, carry):
            w = rows(i * tile, tile)
            n_rows = n_ref[:, cols(x * hh_rows + i * tile, tile)]
            acc_g[w, :] += mm(n_rows, a_t[...], 0, 0)
            acc_u[w, :] += mm(n_rows, b_t[...], 0, 0)
            return carry

        hh_rows = 2 * rb
        lax.fori_loop(0, hh_rows // tile, step, 0)

        def step_d(i, carry):
            acc_d[rows(i * tile_d, tile_d), :] += mm(g_t[:, cols(x * fb + i * tile_d, tile_d)], o_ref[...], 0, 0)
            return carry

        tile_d = min(256, fb)
        lax.fori_loop(0, fb // tile_d, step_d, 0)

    def zero_acc():
        for ref in (acc_g, acc_u, acc_d):
            def step(i, carry, ref=ref):
                ref[rows(i * 16, 16), :] = jnp.zeros((16, ref.shape[1]), F32)
                return carry

            lax.fori_loop(0, ref.shape[0] // 16, step, 0)

    def rinv(h_f):
        return lax.rsqrt(jnp.mean(h_f * h_f, axis=-1, keepdims=True) + 1e-6)

    def core_sum(key):
        push(key, part.at[rows(co * td, td)], from_core, to_c)
        got(key, from_core)

        def step(i, carry):
            r = rows(c * td + i * 16, 16)
            part[r, :] = part[r, :] + from_core[rows(i * 16, 16), :]
            return carry

        lax.fori_loop(0, td // 16, step, 0)

    def z_send(key):
        for dz in (2, 1, 3):
            zt = (z + dz) % 4
            push((key, dz), part.at[rows(c * td + zt * ch, ch)], from_z.at[dz - 1], to_z(dz))

    def z_got(key):
        for dz in (1, 3, 2):
            got((key, dz), from_z.at[dz - 1])

    def z_sum(i):
        r = rows(i * 16, 16)
        return part[rows(c * td + z * ch + i * 16, 16), :] + from_z[0, r, :] + from_z[1, r, :] + from_z[2, r, :]

    def sum_sends_done(ckey, zkey):
        send_done(ckey)
        for dz in (1, 2, 3):
            send_done((zkey, dz))

    def z_gather(key, ref):
        for dz in (2, 1, 3):
            own = ref.at[rows(c * td + z * ch, ch)]
            push((key, dz), own, own, to_z(dz))

    def z_gathered(key, ref):
        for dz in (1, 3, 2):
            got((key, dz), ref.at[rows(c * td + ((z + 4 - dz) % 4) * ch, ch)])

    loads[0].wait()

    def n0_step(i, carry):
        h_f = n_own[rows(i * 16, 16), :].astype(F32)
        nb[0, rows(c * td + i * 16, 16), :] = (h_f * rinv(h_f) * gain[0:1, :]).astype(BF16)
        return carry

    lax.fori_loop(0, td // 16, n0_step, 0)
    n0_mine = nb.at[0, rows(c * td, td)]
    push("n0p", n0_mine, n0_mine, to_c)
    keep = local("n0k", n0_mine, n0_buf.at[q, c])
    keep.start()
    keep.wait()
    ag_y("n0", n0_buf, n0_buf.at[q, c], 0)
    for h in range(2):
        ag_x("n0", n0_buf, n0_buf.at[q, c], h)
    for h in range(2):
        ag_x("o1", o1_buf, dy_in, h)

    def relay_gu(l, m, xb):
        ref = wview(gu[m][1], l, 2 * xo + cs, xb)
        got(("wx", l, m, xb), ref)
        push(("wy", l, m, xb), ref, ref, to_y)

    def relay_d(l, k):
        ref = wd.at[l, rows(xo * fb + y * (fb // 2) + k * (fb // 4), fb // 4)]
        got(("wdx", l, k), ref)
        push(("wdy", l, k), ref, ref, to_y)

    def have_gu(l):
        for m in range(2):
            for xb in range(2):
                local(("w", l, m, xb), wsrc(gu[m][0], l, xb, c), wview(gu[m][1], l, f, xb)).wait()
                got(("wc", l, m, xb), wview(gu[m][1], l, 2 * x + co, xb))
                got(("wy", l, m, xb), wview(gu[m][1], l, 2 * xo + cso, xb))

    def have_d(l):
        local(("wd", l), wd_in.at[l], wd.at[l, rows(x * fb, fb)]).wait()
        for k in range(2):
            got(("wdy", l, k), wd.at[l, rows(xo * fb + yo * (fb // 2) + k * (fb // 4), fb // 4)])

    for m in range(2):
        for xb in range(2):
            relay_gu(0, m, xb)
    got("n0p", nb.at[0, rows(co * td, td)])
    keep2 = local("n0k2", nb.at[0, rows(co * td, td)], n0_buf.at[q, co])
    keep2.start()
    have_gu(0)
    fwd(0, nb.at[0], g_t)
    saves = [local("sa", a_t, a_save.at[q]), local("sb", b_t, b_save.at[q])]
    for s in saves:
        s.start()
    relay_d(0, 0)
    relay_d(0, 1)
    have_d(0)
    down(0, g_t)
    core_sum("d0")
    z_send("z0")
    for m in range(2):
        for xb in range(2):
            relay_gu(1, m, xb)
    for k in range(2):
        relay_d(1, k)
    ag_y("n0", n0_buf, n0_buf.at[q, c], 1)

    local("xc", x_in.at[rows(z * ch, ch)], x_ch).wait()
    z_got("z0")

    def h1_step(i, carry):
        r = rows(i * 16, 16)
        h1 = (x_ch[r, :].astype(F32) + z_sum(i)).astype(BF16)
        h1_ch[r, :] = h1
        h_f = h1.astype(F32)
        n_own[rows(c * td + z * ch + i * 16, 16), :] = (h_f * rinv(h_f) * gain[1:2, :]).astype(BF16)
        return carry

    lax.fori_loop(0, ch // 16, h1_step, 0)
    z_gather("n1z", n_own)
    ag_relay_y("n0", n0_buf)
    ag_relay_x("n0", n0_buf)
    for h in range(2):
        ag_y("o1", o1_buf, dy_in, h)
    z_gathered("n1z", n_own)
    n1_mine = n_own.at[rows(c * td, td)]
    push("n1p", n1_mine, n1_mine, to_c)
    for h in range(2):
        ag_x("n1", n1_buf, n1_mine, h)
        ag_y("n1", n1_buf, n1_mine, h)
    got("dyp", o1_buf.at[q, co])
    dy_other = local("dy_other", o1_buf.at[q, co], ob.at[0, rows(co * td, td)])
    dy_other.start()
    got("n1p", n_own.at[rows(co * td, td)])

    have_gu(1)
    for s in saves:
        s.wait()
    fwd(1, n_own, g_keep)
    local("dy_own", dy_in, ob.at[0, rows(c * td, td)]).wait()
    dy_other.wait()
    have_d(1)
    bwd_hidden(1, ob.at[0])
    sum_sends_done("d0", "z0")
    m_part(1)
    core_sum("d1")
    z_send("z1")
    zero_acc()
    weight_grads(n_own, ob.at[0])
    keep2.wait()
    send_done("n0p")

    ag_share_rest("n0", n0_buf)
    ag_share_diag("n0", n0_buf)

    def load_n(buf, j, s):
        return local("ln", buf.at[j], nb_block.at[s])

    nb_block = nb

    def stage(buf, block, slot_ref, key):
        for core in range(2):
            local((key, core), buf.at[block, core], slot_ref.at[pl.ds(core * td, td)]).start()

    def staged(buf, block, slot_ref, key):
        for core in range(2):
            local((key, core), buf.at[block, core], slot_ref.at[pl.ds(core * td, td)]).wait()

    def f0_step(j, carry):
        blk = block_of(j)
        ag_wait_partner("n0", n0_buf, j)
        stage(n0_buf, blk, nb.at[0], "sn")
        staged(n0_buf, blk, nb.at[0], "sn")
        fwd(0, nb.at[0], None)
        out = (local("sa", a_t, a_save.at[blk]), local("sb", b_t, b_save.at[blk]))
        for s in out:
            s.start()
        for s in out:
            s.wait()
        return carry

    lax.fori_loop(0, 3, f0_step, 0)
    ag_relay_x("o1", o1_buf)
    ag_relay_y("o1", o1_buf)
    ag_share_rest("o1", o1_buf)

    local("dyc", dy_in.at[rows(z * ch, ch)], dy_ch).wait()
    z_got("z1")

    def e_step(i, dg1):
        r = rows(i * 16, 16)
        m = z_sum(i)
        h_f = h1_ch[r, :].astype(F32)
        r_inv = rinv(h_f)
        xh = h_f * r_inv
        v = m * gain[1:2, :]
        e = dy_ch[r, :].astype(F32) + r_inv * (v - xh * jnp.mean(v * xh, axis=-1, keepdims=True))
        o_own[rows(c * td + z * ch + i * 16, 16), :] = e.astype(BF16)
        return dg1 + jnp.sum(m * xh, axis=0, keepdims=True)

    dg[1:2, :] = lax.fori_loop(0, ch // 16, e_step, jnp.zeros((1, d), F32))
    z_gather("o0z", o_own)
    sum_sends_done("d1", "z1")
    down(1, g_keep)
    core_sum("d2")
    ag_relay_x("n1", n1_buf)
    ag_relay_y("n1", n1_buf)
    ag_share_diag("o1", o1_buf)
    ag_share_rest("n1", n1_buf)
    z_gathered("o0z", o_own)
    o0_mine = o_own.at[rows(c * td, td)]
    push("o0p", o0_mine, o0_mine, to_c)
    for h in range(2):
        ag_x("o0", o0_buf, o0_mine, h)
        ag_y("o0", o0_buf, o0_mine, h)
    z_send("z2")

    def l1_step(j, carry):
        blk = block_of(j)

        @pl.when(j == 2)
        def _():
            ag_share_diag("n1", n1_buf)

        ag_wait_partner("n1", n1_buf, j)
        ag_wait_partner("o1", o1_buf, j)
        stage(n1_buf, blk, nb.at[0], "sn")
        stage(o1_buf, blk, ob.at[0], "so")
        staged(n1_buf, blk, nb.at[0], "sn")
        staged(o1_buf, blk, ob.at[0], "so")
        fwd(1, nb.at[0], None)
        bwd_hidden(1, ob.at[0])
        weight_grads(nb.at[0], ob.at[0])
        return carry

    lax.fori_loop(0, 3, l1_step, 0)

    def grads_out(l):
        for i, (acc, out) in enumerate(((acc_g, dwg_out), (acc_u, dwu_out))):
            for xb in range(2):
                dst = out.at[l, :, cols((2 * xb + c) * fb, fb)]
                push(("q", l, i, xb), acc.at[rows(co * rb, rb), cols(xb * fb, fb)], dst, to_c)
                local(("qo", l, i, xb), acc.at[rows(c * rb, rb), cols(xb * fb, fb)], dst).start()
        local(("qd", l), acc_d, dwd_out.at[l]).start()

    def grads_out_done(l):
        for i, (acc, out) in enumerate(((acc_g, dwg_out), (acc_u, dwu_out))):
            for xb in range(2):
                dst = out.at[l, :, cols((2 * xb + c) * fb, fb)]
                local(("qo", l, i, xb), acc.at[rows(c * rb, rb), cols(xb * fb, fb)], dst).wait()
                send_done(("q", l, i, xb))
                got(("q", l, i, xb), out.at[l, :, cols((2 * xb + co) * fb, fb)])
        local(("qd", l), acc_d, dwd_out.at[l]).wait()

    grads_out(1)
    got("o0p", o_own.at[rows(co * td, td)])
    o_keep = [local(("ok", k), o_own.at[pl.ds(k * td, td)], o0_buf.at[q, k]) for k in range(2)]
    for s in o_keep:
        s.start()
    ag_relay_x("o0", o0_buf)
    ag_relay_y("o0", o0_buf)
    ag_share_rest("o0", o0_buf)
    got("xp", x_part)
    for key in ["n1p"] + [("n1z", dz) for dz in (1, 2, 3)] + [("n1", axis, h) for axis in "xy" for h in range(2)]:
        send_done(key)
    xl = [local("xl0", x_in, n_own.at[rows(c * td, td)]), local("xl1", x_part, n_own.at[rows(co * td, td)])]
    for s in xl:
        s.start()
    for s in xl:
        s.wait()

    def r_step(i, carry):
        h_f = n_own[rows(i * 16, 16), :].astype(F32)
        r_own[rows(i * 16, 16), :] = jnp.broadcast_to(rinv(h_f), (16, 128))
        return carry

    lax.fori_loop(0, t2 // 16, r_step, 0)
    for s in o_keep:
        s.wait()
    grads_out_done(1)
    zero_acc()

    def l0_step(j, carry):
        blk = 2 * ((y + j // 2) % 2) + (x + j % 2) % 2

        @pl.when(j == 2)
        def _():
            ag_share_diag("o0", o0_buf)

        @pl.when(j > 0)
        def _():
            ag_wait_partner("o0", o0_buf, j - 1)

        stage(n0_buf, blk, nb.at[0], "sn")
        stage(o0_buf, blk, ob.at[0], "so")
        back = (local("sa", a_save.at[blk], a_t), local("sb", b_save.at[blk], b_t))
        for s in back:
            s.start()
        for s in back:
            s.wait()
        staged(n0_buf, blk, nb.at[0], "sn")
        staged(o0_buf, blk, ob.at[0], "so")
        bwd_hidden(0, ob.at[0])

        @pl.when(j == 0)
        def _():
            def dg_step(i, carry):
                w = cols(i * tile, tile)
                m = m_tile(0, i)
                xh = n_own[:, w].astype(F32) * r_own[:, 0:1]
                dg[0:1, w] = jnp.sum(m * xh, axis=0, keepdims=True)
                return carry

            lax.fori_loop(0, d // tile, dg_step, 0)
            push("gc", dg, dg_core, to_c, lambda: remote("gc", dg, dg_core, to_c))

        weight_grads(nb.at[0], ob.at[0])
        return carry

    lax.fori_loop(0, 4, l0_step, 0)
    grads_out(0)

    got("gc", dg_core)
    send_done("gc")
    dg[...] = dg[...] + dg_core[...]
    push("gx", dg, dg_x, to_x)
    got("gx", dg_x)
    send_done("gx")
    dg[...] = dg[...] + dg_x[...]
    push("gy", dg, dg_y, to_y)
    got("gy", dg_y)
    send_done("gy")
    dg_z[z] = dg[...] + dg_y[...]
    for dz in (1, 2, 3):
        push(("gz", dz), dg_z.at[z], dg_z.at[z], to_z(dz))

    z_got("z2")

    def y_step(i, carry):
        r = rows(i * 16, 16)
        y_ch[r, :] = (h1_ch[r, :].astype(F32) + z_sum(i)).astype(BF16)
        return carry

    lax.fori_loop(0, ch // 16, y_step, 0)
    y_keep = local("yk", y_ch, y_out.at[rows(z * ch, ch)])
    y_keep.start()
    for dz in (1, 2, 3):
        push(("yz", dz), y_ch, y_out.at[rows(z * ch, ch)], to_z(dz))
    for dz in (1, 2, 3):
        got(("gz", dz), dg_z.at[(z + 4 - dz) % 4])
    dgain_out[...] = dg_z[0] + dg_z[1] + dg_z[2] + dg_z[3]
    for dz in (1, 2, 3):
        got(("yz", dz), y_out.at[rows(((z + 4 - dz) % 4) * ch, ch)])
    y_keep.wait()
    grads_out_done(0)
    for key in list(sent):
        send_done(key)


def make_call(td, d, rb, hs):
    fb = hs // 4
    hh, t2, ch = 2 * fb, 2 * td, td // 4
    shape = jax.ShapeDtypeStruct
    hbm = pl.BlockSpec(memory_space=pl.ANY)
    vmem = pl.BlockSpec(memory_space=pltpu.VMEM)
    block = shape((4, 2, td, d), BF16)
    outs = [
        shape((td, d), BF16), shape((2, rb, hs), F32), shape((2, rb, hs), F32), shape((2, fb, d), F32), shape((2, d), F32),
        block, block, block, block, shape((4, t2, hh), BF16), shape((4, t2, hh), BF16), shape((td, d), BF16),
    ]
    scratch = [
        pltpu.VMEM((2, d, hh), BF16), pltpu.VMEM((2, d, hh), BF16), pltpu.VMEM((2, hh, d), BF16),
        pltpu.VMEM((2 * rb, hh), F32), pltpu.VMEM((2 * rb, hh), F32), pltpu.VMEM((fb, d), F32),
        pltpu.VMEM((1, t2, d), BF16), pltpu.VMEM((1, t2, d), BF16),
        pltpu.VMEM((t2, hh), BF16), pltpu.VMEM((t2, hh), BF16), pltpu.VMEM((t2, hh), BF16), pltpu.VMEM((t2, hh), BF16),
        pltpu.VMEM((t2, d), F32), pltpu.VMEM((td, d), F32), pltpu.VMEM((3, ch, d), F32),
        pltpu.VMEM((t2, d), BF16), pltpu.VMEM((t2, d), BF16),
        pltpu.VMEM((ch, d), BF16), pltpu.VMEM((ch, d), BF16), pltpu.VMEM((ch, d), BF16), pltpu.VMEM((ch, d), BF16),
        pltpu.VMEM((t2, 128), F32),
        pltpu.VMEM((2, d), F32), pltpu.VMEM((2, d), F32), pltpu.VMEM((2, d), F32), pltpu.VMEM((2, d), F32), pltpu.VMEM((4, 2, d), F32),
        pltpu.SemaphoreType.DMA((NSEM,)), pltpu.SemaphoreType.DMA((NSEM,)), pltpu.SemaphoreType.DMA((NLOC,)),
    ]
    return pl.pallas_call(
        kernel,
        out_shape=outs,
        in_specs=[hbm] * 5 + [vmem],
        out_specs=[hbm] * 4 + [vmem] + [hbm] * 7,
        scratch_shapes=scratch,
        compiler_params=pltpu.CompilerParams(collective_id=0, has_side_effects=True, vmem_limit_bytes=67043328),
    )


def solution(mesh):
    tok_spec = P(("replica", "fsdp"), None)
    wide_spec = P(None, "fsdp", "tensor")
    down_spec = P(None, ("tensor", "fsdp"), None)
    gain_spec = P(None, None)

    def device_fn(x_loc, dy_loc, w_gate, w_up, w_down, norm_gain):
        call = make_call(x_loc.shape[0], x_loc.shape[1], w_gate.shape[1], w_gate.shape[2])
        return tuple(call(x_loc, dy_loc, w_gate, w_up, w_down, norm_gain)[:5])

    return jax.shard_map(device_fn, mesh=mesh, in_specs=(tok_spec, tok_spec, wide_spec, wide_spec, down_spec, gain_spec), out_specs=(tok_spec, wide_spec, wide_spec, down_spec, gain_spec), check_vma=False)
```

time: 2070 us -> 426 us (0.21)
  waiting for transfers between devices: 1850 us -> 0 us
  Pallas kernels: 0 us -> 400 us
  matrix products: 133 us -> 0 us
  other arithmetic: 25.7 us -> 0.01 us
  blocking collectives: 24.2 us -> 0 us
    psum x4 -> x0, waiting for transfers between devices: 824 us -> none  [the longest x1 531 us: device_fn(): lax.psum(lax.psum_scatter(part_gate[layer_idx], 'fsdp', scatter_dimension...]
    reduce_scatter x6 -> x0, waiting for transfers between devices: 700 us -> none  [the longest x2 254 us: device_fn(): lax.psum_scatter(part_down[layer_idx], 'fsdp', scatter_dimension=0, tiled...]
    pallas_call x0 -> x1, Pallas kernels: none -> 400 us  [device_fn(): return tuple(call(x_loc, dy_loc, w_gate, w_up, w_down, norm_gain)[:5])]
    all_gather x6 -> x0, waiting for transfers between devices: 322 us -> none  [the longest x2 108 us: gather_layer(): full_up = lax.all_gather(w_up[layer_idx], 'fsdp', axis=0, tiled=True)]
    dot_general x18 -> x0, matrix products: 133 us -> none  [the longest x2 19.5 us: device_fn(): jnp.einsum('td,tf->df', normed, d_up, preferred_element_type=jnp.float32)]
    psum x1 -> x0, blocking collectives: 24.2 us -> none  [device_fn(): d_gain = lax.psum(jnp.stack(part_gain), ('replica', 'fsdp'))]
  transfers between devices with their start and end apart: 16 -> 0, of which waited for: 16 -> 0; matrix products, arithmetic and copies ran while one was open for 7% -> 0% of each run, Pallas kernels for 0% -> 0%
where the time goes in v1:
time: 426 us; the launch traced here: 422 us
  Pallas kernels  400 us (94%)
  local copies, waits for them, and re-layouts  20.8 us (5%)
    pallas_call x1, Pallas kernels, device_fn(): return tuple(call(x_loc, dy_loc, w_gate, w_up, w_down, norm_gain)[:5])  400 us
    unnamed x13, local copies, waits for them, and re-layouts  20.8 us

profile of v1, /device:TPU:0, one launch (start us, length us, event | category | flops | bytes accessed | tf_op | source)
XLA Modules:
  0.0 421.6 jit_solution(3677885157408942667)
XLA Ops:
  0.6 400.2 %shard_map.101 = (bf16[256,2048]{1,0:T(8,128)(2,1)}, f32[2,512,2048]{2,1,0:T(8,128)}, f32[2,512,2048]{2,1,0:T(8,128)}, f32[2,512,2048]{2,1,0:T(8,128)}, f32[2,20...) custom-call(bf16[256,2048]{1,0:T(8,128)(2,1)} %x_in.1, ...), custom_call_target="tpu_custom_call" | custom-call | tf_op jit(solution)/shard_map/pallas_call | solution.py:634
  400.8 2.3 copy.16
  403.1 0.0 copy-start
  403.1 0.0 slice-start
  403.1 8.9 %copy.17 = f32[2,512,2048]{2,1,0:T(8,128)} copy(f32[2,512,2048]{2,1,0:T(8,128)} %get-tuple-element.21) | data formatting | bytes 16777216
  412.0 0.0 copy-done
  412.0 0.0 slice-start.1
  412.0 4.3 %copy.18 = f32[2,512,2048]{2,1,0:T(8,128)} copy(f32[2,512,2048]{2,1,0:T(8,128)S(1)} %copy-done) | data formatting | bytes 16777216
  416.3 0.0 slice-done
  416.3 1.3 slice-done.1
  417.6 0.0 copy-start.1
  417.6 3.4 copy.19
  421.0 0.0 copy-done.1
  421.0 0.6 copy.20
  (1 shorter events, 0.0 us)
Async XLA Ops:
  403.1 8.9 %copy-start = (f32[2,512,2048]{2,1,0:T(8,128)S(1)}, f32[2,512,2048]{2,1,0:T(8,128)}, u32[]{:S(2)}) copy-start(f32[2,512,2048]{2,1,0:T(8,128)} %get-tuple-element.22) | copy-start | bytes 25165828
  403.1 13.2 %slice-start = ((s8[8388608]{0:T(1024)(128)(4,1)}), s8[4194304]{0:T(1024)(128)(4,1)S(1)}, s32[]{:S(2)}) async-start(s8[8388608]{0:T(1024)(128)(4,1)} %bitcast), calls=%async_computation | async-start | bytes 8388608
  412.0 5.6 %slice-start.1 = ((s8[8388608]{0:T(1024)(128)(4,1)}), s8[4194304]{0:T(1024)(128)(4,1)S(1)}, s32[]{:S(2)}) async-start(s8[8388608]{0:T(1024)(128)(4,1)} %bitcast), calls=%async_computation.1 | async-start | bytes 8388608
  417.6 3.4 copy-start.1

commit v2 on v0

v2 whole, which is shorter than its diff:
```python
import jax
import jax.numpy as jnp
from jax import lax
from jax.experimental import pallas as pl
from jax.experimental.pallas import tpu as pltpu
from jax.sharding import PartitionSpec as P

F32 = jnp.float32
BF16 = jnp.bfloat16
MESH = pl.DeviceIdType.MESH
NSEM = 300
NLOC = 64


def mm(lhs, rhs, ldim, rdim):
    return lax.dot_general(lhs, rhs, (((ldim,), (rdim,)), ((), ())), preferred_element_type=F32)


def kernel(
    x_in, dy_in, wg_in, wu_in, wd_in, gain,
    y_out, dwg_out, dwu_out, dwd_out, dgain_out, n0_buf, n1_buf, o1_buf, o0_buf, a_save, b_save, x_part,
    wg, wu, wd, acc_g, acc_u, acc_d, nb, ob, a_t, b_t, g_t, g_keep, part, from_core, from_z, n_own, o_own,
    x_ch, dy_ch, h1_ch, y_ch, r_own, dg, dg_core, dg_x, dg_y, dg_z, ssem, rsem, lsem,
):
    td, d = x_in.shape
    rb = wg_in.shape[1]
    fb = wg_in.shape[2] // 4
    hh = 2 * fb
    t2, ch, half = 2 * td, td // 4, td // 2
    hc = ch // 2
    tile = min(512, fb)
    z = lax.axis_index("tensor")
    y = lax.axis_index("replica")
    f = lax.axis_index("fsdp")
    x, c = f // 2, f % 2
    xo, yo, co = 1 - x, 1 - y, 1 - c
    q, qx, qy, qd = 2 * y + x, 2 * y + xo, 2 * yo + x, 2 * yo + xo
    cs = (c + y) % 2
    cso = 1 - cs
    to_c, to_x, to_xs, to_y = {"fsdp": 2 * x + co}, {"fsdp": 2 * xo + c}, {"fsdp": 2 * xo + cs}, {"replica": yo}
    inner = ((z + 1) // 2) % 2
    outer = 1 - inner
    up = z // 2
    pair = z + 1 - 2 * (z % 2)
    far_outer, far_inner = 3 - 3 * up, 2 - up
    order = (outer * far_outer + inner * pair, outer * far_inner + inner * far_outer, outer * pair + inner * far_inner, z)

    def at_z(i):
        return {"tensor": i}

    def z_other(k):
        return (z + 4 + k * (1 - 2 * up)) % 4

    def rows(start, size):
        return pl.ds(pl.multiple_of(start, size if size % 16 == 0 else 8), size)

    def cols(start, size):
        return pl.ds(pl.multiple_of(start, 128), size)

    ids, lids, sent = {}, {}, {}

    def sid(key):
        i = ids.setdefault(key, len(ids))
        assert i < NSEM, i
        return i

    def name_of(key):
        return key if isinstance(key, str) else "_".join(map(str, key))

    def copy_of(skey, rkey, src, dst, dev):
        return pltpu.make_async_remote_copy(
            src_ref=src, dst_ref=dst, send_sem=ssem.at[sid(skey)], recv_sem=rsem.at[rkey if not isinstance(rkey, (str, tuple)) else sid(rkey)],
            device_id=dev, device_id_type=MESH,
        )

    def push(key, make, rkey=None):
        copy_of(key, key if rkey is None else rkey, *make()).start()
        sent[key] = make

    def got(key, dst):
        with jax.named_scope("got_" + (name_of(key) if isinstance(key, (str, tuple)) else "dyn")):
            copy_of("none", key, dst, dst, to_c).wait_recv()

    def send_done(key):
        copy_of(key, key, *sent.pop(key)()).wait_send()

    def local(key, src, dst):
        i = lids.setdefault(key, len(lids))
        assert i < NLOC
        return pltpu.make_async_copy(src, dst, lsem.at[i])

    def scoped(fn):
        def run(*args):
            with jax.named_scope(fn.__name__):
                return fn(*args)

        return run

    gu = ((wg_in, wg), (wu_in, wu))
    pieces = (2, 2)

    def wview(m, l, row, xb, k=0, n=1):
        return gu[m][1].at[l, rows(row * rb + k * (rb // n), rb // n), cols(xb * fb, fb)]

    def wsrc(m, l, xb, core, k=0, n=1):
        return gu[m][0].at[l, pl.ds(k * (rb // n), rb // n), cols((2 * xb + core) * fb, fb)]

    def push_w(l):
        n = pieces[l]
        for m in range(2):
            for xb in range(2):
                for k in range(n):
                    push(("wx", l, m, xb, k), lambda m=m, xb=xb, k=k: (wsrc(m, l, xb, cs, k, n), wview(m, l, f, xb, k, n), to_xs))
        for k in range(4):
            r0 = y * (fb // 2) + k * (fb // 8)
            push(("wdx", l, k), lambda r0=r0: (wd_in.at[l, rows(r0, fb // 8)], wd.at[l, rows(x * fb + r0, fb // 8)], to_x))

    def push_wc(l):
        for m in range(2):
            for xb in range(2):
                push(("wc", l, m, xb), lambda m=m, xb=xb: (wsrc(m, l, xb, co), wview(m, l, f, xb), to_c))
                local(("w", l, m, xb), wsrc(m, l, xb, c), wview(m, l, f, xb)).start()
        local(("wd", l), wd_in.at[l], wd.at[l, rows(x * fb, fb)]).start()

    def relay_gu(l, m, xb):
        n = pieces[l]
        for k in range(n):
            ref = lambda k=k: wview(m, l, 2 * xo + cs, xb, k, n)
            got(("wx", l, m, xb, k), ref())
            push(("wy", l, m, xb, k), lambda k=k: (ref(k), ref(k), to_y))

    def relay_d(l, k):
        ref = lambda: wd.at[l, rows(xo * fb + y * (fb // 2) + k * (fb // 8), fb // 8)]
        got(("wdx", l, k), ref())
        push(("wdy", l, k), lambda: (ref(), ref(), to_y))

    def have_gu(l, m, xb):
        n = pieces[l]
        local(("w", l, m, xb), wsrc(m, l, xb, c), wview(m, l, f, xb)).wait()
        got(("wc", l, m, xb), wview(m, l, 2 * x + co, xb))
        for k in range(n):
            got(("wy", l, m, xb, k), wview(m, l, 2 * xo + cso, xb, k, n))

    def have_d_own(l):
        local(("wd", l), wd_in.at[l], wd.at[l, rows(x * fb, fb)]).wait()

    def have_d(l):
        for k in range(4):
            got(("wdy", l, k), wd.at[l, rows(xo * fb + yo * (fb // 2) + k * (fb // 8), fb // 8)])

    def piece(buf, block, core, start, size):
        return buf.at[block, core, pl.ds(start, size)]

    def chunk(buf, block, core, zi):
        return buf.at[block, core, rows(zi * ch, ch)]

    def part_id(a, j):
        base = sid((a, "p", 0))
        for jj in range(3):
            assert sid((a, "p", jj)) == base + jj
        return base + j

    def share(a, j, tag, ref):
        push((a, "s", j, tag), lambda: (ref(), ref(), to_c), (a, "p", j))

    def ag_x(a, buf, src, h):
        push((a, "x", h), lambda: (src().at[pl.ds(h * half, half)], piece(buf, q, c, h * half, half), to_x))

    def ag_y(a, buf, src, h):
        push((a, "y", h), lambda: (src().at[pl.ds(h * half, half)], piece(buf, q, c, h * half, half), to_y))

    def ag_yc(a, buf, src):
        push((a, "yc"), lambda: (src().at[rows(z * ch, ch)], chunk(buf, q, c, z), to_y))

    def zb_id(a, zi):
        base = sid((a, "zb", 0))
        for i in range(4):
            assert sid((a, "zb", i)) == base + i
        return base + zi

    def ag_spread(a, buf):
        got((a, "yc"), chunk(buf, qy, c, z))
        for k in (1, 2, 3):
            push((a, "zs", k), lambda: (chunk(buf, qy, c, z), chunk(buf, qy, c, z), at_z(z_other(k))), zb_id(a, z))

    def ag_spread_got(a, buf, cut):
        for k in (1, 2, 3):
            with jax.named_scope("got_zb_" + a):
                got(zb_id(a, z_other(k)), chunk(buf, qy, c, z_other(k)))
        share(a, 0, 0, lambda: buf.at[qy, c])

    def ag_dx(a, buf, cut):
        push((a, "dx"), lambda: (piece(buf, qy, c, 0, cut), piece(buf, qy, c, 0, cut), to_x))

    def ag_got_y(a, buf, h):
        got((a, "y", h), piece(buf, qy, c, h * half, half))
        share(a, 0, h, lambda: piece(buf, qy, c, h * half, half))
        if h == 0:
            ag_dx(a, buf, half)

    def diag_piece(h, cut):
        start = max(cut, h * half)
        return start, (h + 1) * half - start

    def ag_got_x(a, buf, h, cut):
        got((a, "x", h), piece(buf, qx, c, h * half, half))
        start, size = diag_piece(h, cut)
        if size:
            push((a, "dy", h), lambda: (piece(buf, qx, c, start, size), piece(buf, qx, c, start, size), to_y))
        share(a, 1, h, lambda: piece(buf, qx, c, h * half, half))

    def ag_got_dx(a, buf, cut):
        got((a, "dx"), piece(buf, qd, c, 0, cut))
        share(a, 2, "x", lambda: piece(buf, qd, c, 0, cut))

    def ag_got_dy(a, buf, h, cut):
        start, size = diag_piece(h, cut)
        if size:
            got((a, "dy", h), piece(buf, qd, c, start, size))
            share(a, 2, h, lambda: piece(buf, qd, c, start, size))

    def block_of(j):
        return 2 * ((y + (j + 1) % 2) % 2) + (x + (j + 1) // 2) % 2

    def partner_has(a, buf, j):
        with jax.named_scope("got_p_" + a):
            got(part_id(a, j), buf.at[block_of(j), co])

    for a in ("n0", "o1", "n1", "o0"):
        for j in range(3):
            sid((a, "p", j))
        for i in range(4):
            sid((a, "zb", i))

    def fwd_tile(l, n_ref, g_ref, i):
        w = cols(i * tile, tile)
        a = mm(n_ref[...], wg[l, :, w], 1, 0).astype(BF16)
        b = mm(n_ref[...], wu[l, :, w], 1, 0).astype(BF16)
        a_t[:, w] = a
        b_t[:, w] = b
        if g_ref is not None:
            a_f = a.astype(F32)
            g_ref[:, w] = (a_f * jax.nn.sigmoid(a_f) * b.astype(F32)).astype(BF16)

    @scoped
    def fwd(l, n_ref, g_ref):
        def step(i, carry):
            fwd_tile(l, n_ref, g_ref, i)
            return carry

        lax.fori_loop(0, hh // tile, step, 0)

    @scoped
    def down_rows(l, g_ref, core):
        def step(i, carry):
            w = cols(i * tile, tile)
            part[rows(core * td, td), w] = mm(g_ref[rows(core * td, td), :], wd[l, :, w], 1, 0)
            return carry

        lax.fori_loop(0, d // tile, step, 0)

    @scoped
    def m_rows(l, core):
        r = rows(core * td, td)

        def step(i, carry):
            w = rows(i * tile, tile)
            part[r, cols(i * tile, tile)] = mm(a_t[r, :], wg[l, w], 1, 1) + mm(b_t[r, :], wu[l, w], 1, 1)
            return carry

        lax.fori_loop(0, d // tile, step, 0)

    @scoped
    def bwd_hidden(l, o_ref):
        def step(i, carry):
            w = cols(i * tile, tile)
            q_f = mm(o_ref[...], wd[l, rows(i * tile, tile)], 1, 1).astype(BF16).astype(F32)
            a_f = a_t[:, w].astype(F32)
            b_f = b_t[:, w].astype(F32)
            s = jax.nn.sigmoid(a_f)
            g_t[:, w] = (a_f * s * b_f).astype(BF16)
            a_t[:, w] = (q_f * b_f * s * (1.0 + a_f * (1.0 - s))).astype(BF16)
            b_t[:, w] = (q_f * a_f * s).astype(BF16)
            return carry

        lax.fori_loop(0, hh // tile, step, 0)

    @scoped
    def weight_grads(n_ref, o_ref):
        def step(i, carry):
            w = rows(i * tile, tile)
            n_rows = n_ref[:, cols(x * (2 * rb) + i * tile, tile)]
            acc_g[w, :] += mm(n_rows, a_t[...], 0, 0)
            acc_u[w, :] += mm(n_rows, b_t[...], 0, 0)
            return carry

        lax.fori_loop(0, 2 * rb // tile, step, 0)
        tile_d = min(256, fb)

        def step_d(i, carry):
            acc_d[rows(i * tile_d, tile_d), :] += mm(g_t[:, cols(x * fb + i * tile_d, tile_d)], o_ref[...], 0, 0)
            return carry

        lax.fori_loop(0, fb // tile_d, step_d, 0)

    @scoped
    def zero_acc():
        for ref in (acc_g, acc_u, acc_d):
            def step(i, carry, ref=ref):
                ref[rows(i * 16, 16), :] = jnp.zeros((16, ref.shape[1]), F32)
                return carry

            lax.fori_loop(0, ref.shape[0] // 16, step, 0)

    def rinv(h_f):
        return lax.rsqrt(jnp.mean(h_f * h_f, axis=-1, keepdims=True) + 1e-6)

    def core_push(key):
        for k in range(4):
            push((key, "c", k), lambda k=k: (part.at[rows(co * td + order[k] * ch, ch)], from_core.at[rows(order[k] * ch, ch)], to_c))

    def z_ids(key):
        base = sid((key, "A", 0))
        for h in range(2):
            for i, s in enumerate("ABCD"):
                assert sid((key, s, h)) == base + 4 * h + i
        return base

    def mine(zi, h):
        return part.at[rows(c * td + zi * ch + h * hc, hc)]

    def slot(i, h):
        return from_z.at[i, pl.ds(h * hc, hc)]

    @scoped
    def core_sum_send(key):
        z_ids(key)
        for k in range(4):
            got((key, "c", k), from_core.at[rows(order[k] * ch, ch)])

            def step(i, carry):
                r = order[k] * ch + i * 16
                mine_r = rows(c * td + r, 16)
                part[mine_r, :] = part[mine_r, :] + from_core[rows(r, 16), :]
                return carry

            lax.fori_loop(0, ch // 16, step, 0)
            if k == 0:
                for h in range(2):
                    push((key, "A", h), lambda: (mine(order[0], h), slot(0, h), at_z(pair)))
            elif k < 3:
                @pl.when(outer == 1)
                def _():
                    for h in range(2):
                        copy_of((key, "BC"[k - 1], h), (key, "BC"[k - 1], h), mine(order[k], h), slot(k, h), at_z(pair)).start()

                for h in range(2):
                    sent[(key, "BC"[k - 1], h)] = lambda: (mine(order[k], h), slot(k, h), at_z(pair))

    def z_relay(key, n, h):
        @pl.when(inner == 1)
        def _():
            got((key, "AB"[n], h), slot(n, h))
            zi = (far_outer, far_inner)[n]

            def step(i, carry):
                r = pl.ds(h * hc + i * 8, 8)
                from_z[n, pl.ds(pl.multiple_of(h * hc + i * 8, 8), 8), :] += part[rows(c * td + zi * ch + h * hc + i * 8, 8), :]
                return carry

            lax.fori_loop(0, hc // 8, step, 0)
            if n == 0:
                copy_of((key, "B", h), (key, "B", h), slot(0, h), slot(1, h), at_z(far_outer)).start()
            else:
                copy_of((key, "C", h), (key, "D", h), slot(1, h), slot(3, h), at_z(far_inner)).start()

    def z_got(key):
        base = z_ids(key)
        for h in range(2):
            for i in range(2):
                with jax.named_scope("got_" + key):
                    got(base + 4 * h + 2 * inner + i, slot(2 * inner + i, h))

    def z_sum(i):
        r = rows(i * 16, 16)
        return part[rows(c * td + z * ch + i * 16, 16), :] + from_z[2 * inner, r, :] + from_z[2 * inner + 1, r, :]

    def sum_sends_done(key):
        for k in range(4):
            send_done((key, "c", k))
        for s in "ABC":
            for h in range(2):
                send_done((key, s, h))

    def quarter(ref, core, zi):
        return ref.at[rows(core * td + zi * ch, ch)]

    def zg_id(key, zi):
        base = sid((key, "z", 0))
        for i in range(4):
            assert sid((key, "z", i)) == base + i
        return base + zi

    def z_gather(key, ref):
        for k in (1, 2, 3):
            push((key, "zs", k), lambda: (quarter(ref, c, z), quarter(ref, c, z), at_z(z_other(k))), zg_id(key, z))
        push((key, "s", 0), lambda: (quarter(ref, c, z), quarter(ref, c, z), to_c))

    def z_gathered(key, ref):
        for k in (1, 2, 3):
            with jax.named_scope("got_" + key):
                got(zg_id(key, z_other(k)), quarter(ref, c, z_other(k)))
            push((key, "s", k), lambda: (quarter(ref, c, z_other(k)), quarter(ref, c, z_other(k)), to_c))

    def z_gathered_partner(key, ref):
        got((key, "s", 0), quarter(ref, co, z))
        for k in (1, 2, 3):
            got((key, "s", k), quarter(ref, co, z_other(k)))

    def stage(buf, block, slot_ref, key):
        for core in range(2):
            local((key, core), buf.at[block, core], slot_ref.at[pl.ds(core * td, td)]).start()

    def staged(buf, block, slot_ref, key):
        for core in range(2):
            local((key, core), buf.at[block, core], slot_ref.at[pl.ds(core * td, td)]).wait()

    def save_ab(block):
        return (local("sa", a_t, a_save.at[block]), local("sb", b_t, b_save.at[block]))

    @scoped
    def f0_other(j):
        block = block_of(j)
        partner_has("n0", n0_buf, j)
        stage(n0_buf, block, nb.at[0], "sn")
        staged(n0_buf, block, nb.at[0], "sn")
        fwd(0, nb.at[0], None)
        for s in save_ab(block):
            s.start()
        for s in save_ab(block):
            s.wait()

    def grads_out(l):
        for i, (acc, out) in enumerate(((acc_g, dwg_out), (acc_u, dwu_out))):
            for xb in range(2):
                dst = lambda: out.at[l, :, cols((2 * xb + c) * fb, fb)]
                push(("q", l, i, xb), lambda: (acc.at[rows(co * rb, rb), cols(xb * fb, fb)], dst(), to_c))
                local(("qo", l, i, xb), acc.at[rows(c * rb, rb), cols(xb * fb, fb)], dst()).start()
        local(("qd", l), acc_d, dwd_out.at[l]).start()

    @scoped
    def grads_out_done(l):
        for i, (acc, out) in enumerate(((acc_g, dwg_out), (acc_u, dwu_out))):
            for xb in range(2):
                local(("qo", l, i, xb), acc.at[rows(c * rb, rb), cols(xb * fb, fb)], out.at[l, :, cols((2 * xb + c) * fb, fb)]).wait()
                send_done(("q", l, i, xb))
                got(("q", l, i, xb), out.at[l, :, cols((2 * xb + co) * fb, fb)])
        local(("qd", l), acc_d, dwd_out.at[l]).wait()

    barrier = pltpu.get_barrier_semaphore()
    for dev in (to_c, to_x, {"fsdp": 2 * xo + co}, to_y, at_z((z + 1) % 4), at_z((z + 2) % 4), at_z((z + 3) % 4)):
        pl.semaphore_signal(barrier, inc=1, device_id=dev, device_id_type=MESH)
    x_load = local("x", x_in, n_own.at[pl.ds(0, td)])
    x_load.start()
    with jax.named_scope("barrier"):
        pl.semaphore_wait(barrier, 7)

    dy_src = lambda: dy_in
    n0_src = lambda: n0_buf.at[q, c]
    n1_src = lambda: n_own.at[rows(c * td, td)]
    o0_src = lambda: o_own.at[rows(c * td, td)]
    cut = ch

    push_w(0)
    ag_yc("o1", o1_buf, dy_src)
    push_wc(0)
    x_load.wait()

    def n0_step(i, carry):
        h_f = n_own[rows(i * 16, 16), :].astype(F32)
        nb[0, rows(c * td + i * 16, 16), :] = (h_f * rinv(h_f) * gain[0:1, :]).astype(BF16)
        return carry

    lax.fori_loop(0, td // 16, n0_step, 0)
    n0_mine = lambda: nb.at[0, rows(c * td, td)]
    push("n0p", lambda: (n0_mine(), n0_mine(), to_c))
    keep = local("n0k", n0_mine(), n0_buf.at[q, c])
    keep.start()
    keep.wait()
    ag_yc("n0", n0_buf, n0_src)
    push_w(1)
    ag_x("o1", o1_buf, dy_src, 0)
    push("xp", lambda: (x_in, x_part, to_c))
    push("dyp", lambda: (dy_in, o1_buf.at[q, c], to_c))
    push_wc(1)
    local("xc", x_in.at[rows(z * ch, ch)], x_ch).start()
    local("dyc", dy_in.at[rows(z * ch, ch)], dy_ch).start()
    local("dy_own", dy_in, ob.at[0, rows(c * td, td)]).start()

    relay_gu(0, 0, 0)
    ag_spread("o1", o1_buf)
    ag_spread("n0", n0_buf)
    relay_gu(0, 0, 1)
    relay_gu(0, 1, 0)
    relay_gu(0, 1, 1)
    got("n0p", nb.at[0, rows(co * td, td)])
    keep2 = local("n0k2", nb.at[0, rows(co * td, td)], n0_buf.at[q, co])
    keep2.start()
    have_gu(0, 0, 0)
    have_gu(0, 1, 0)
    with jax.named_scope("fwd_tile0"):
        fwd_tile(0, nb.at[0], g_t, 0)
    relay_d(0, 0)
    relay_d(0, 1)
    have_gu(0, 0, 1)
    have_gu(0, 1, 1)
    with jax.named_scope("fwd_tile1"):
        for i in range(1, hh // tile):
            fwd_tile(0, nb.at[0], g_t, i)
    for s in save_ab(q):
        s.start()
    relay_d(0, 2)
    relay_d(0, 3)
    have_d_own(0)
    have_d(0)
    down_rows(0, g_t, co)
    core_push("d0")
    down_rows(0, g_t, c)
    core_sum_send("d0")
    relay_gu(1, 0, 0)
    z_relay("d0", 0, 0)
    relay_gu(1, 0, 1)
    z_relay("d0", 0, 1)
    keep2.wait()
    send_done("n0p")
    for s in save_ab(q):
        s.wait()
    ag_spread_got("n0", n0_buf, cut)
    ag_spread_got("o1", o1_buf, cut)
    z_relay("d0", 1, 0)
    relay_gu(1, 1, 0)
    z_relay("d0", 1, 1)
    relay_gu(1, 1, 1)

    local("xc", x_in.at[rows(z * ch, ch)], x_ch).wait()
    z_got("d0")
    sum_sends_done("d0")

    @scoped
    def h1_calc():
        def h1_step(i, carry):
            r = rows(i * 16, 16)
            h1 = (x_ch[r, :].astype(F32) + z_sum(i)).astype(BF16)
            h1_ch[r, :] = h1
            h_f = h1.astype(F32)
            n_own[rows(c * td + z * ch + i * 16, 16), :] = (h_f * rinv(h_f) * gain[1:2, :]).astype(BF16)
            return carry

        lax.fori_loop(0, ch // 16, h1_step, 0)

    h1_calc()
    z_gather("n1z", n_own)
    relay_d(1, 0)
    relay_d(1, 1)
    relay_d(1, 2)
    relay_d(1, 3)
    z_gathered("n1z", n_own)
    for h in range(2):
        ag_x("n1", n1_buf, n1_src, h)
    ag_x("o1", o1_buf, dy_src, 1)
    for h in range(2):
        ag_y("n1", n1_buf, n1_src, h)
    got("dyp", o1_buf.at[q, co])
    dy_other = local("dy_other", o1_buf.at[q, co], ob.at[0, rows(co * td, td)])
    dy_other.start()
    z_gathered_partner("n1z", n_own)

    for m in range(2):
        for xb in range(2):
            have_gu(1, m, xb)
    fwd(1, n_own, g_keep)
    local("dy_own", dy_in, ob.at[0, rows(c * td, td)]).wait()
    dy_other.wait()
    have_d_own(1)
    have_d(1)
    bwd_hidden(1, ob.at[0])
    m_rows(1, co)
    core_push("d1")
    m_rows(1, c)
    core_sum_send("d1")
    zero_acc()
    weight_grads(n_own, ob.at[0])
    ag_got_x("o1", o1_buf, 0, cut)
    ag_got_x("n1", n1_buf, 0, half)
    z_relay("d1", 0, 0)
    ag_got_y("n1", n1_buf, 0)
    ag_dx("o1", o1_buf, cut)
    for h in range(2):
        ag_x("n0", n0_buf, n0_src, h)
    ag_dx("n0", n0_buf, cut)
    f0_other(0)
    z_relay("d1", 0, 1)
    ag_got_y("n1", n1_buf, 1)
    ag_got_x("n1", n1_buf, 1, half)
    z_relay("d1", 1, 0)
    local("dyc", dy_in.at[rows(z * ch, ch)], dy_ch).wait()

    @scoped
    def e_calc():
        def e_step(i, dg1):
            r = rows(i * 16, 16)
            m = z_sum(i)
            h_f = h1_ch[r, :].astype(F32)
            r_inv = rinv(h_f)
            xh = h_f * r_inv
            v = m * gain[1:2, :]
            e = dy_ch[r, :].astype(F32) + r_inv * (v - xh * jnp.mean(v * xh, axis=-1, keepdims=True))
            o_own[rows(c * td + z * ch + i * 16, 16), :] = e.astype(BF16)
            return dg1 + jnp.sum(m * xh, axis=0, keepdims=True)

        dg[1:2, :] = lax.fori_loop(0, ch // 16, e_step, jnp.zeros((1, d), F32))

    def at_step(j, k):
        return pl.when(j == k)

    def l1_step(j, carry):
        block = block_of(j)

        @at_step(j, 2)
        def _():
            ag_got_dx("n1", n1_buf, half)
            ag_got_dy("n1", n1_buf, 1, half)
            ag_got_dx("o1", o1_buf, cut)
            for h in range(2):
                ag_got_dy("o1", o1_buf, h, cut)
            down_rows(1, g_keep, co)
            core_push("d2")
            down_rows(1, g_keep, c)

        partner_has("n1", n1_buf, j)
        stage(n1_buf, block, nb.at[0], "sn")
        partner_has("o1", o1_buf, j)
        stage(o1_buf, block, ob.at[0], "so")
        staged(n1_buf, block, nb.at[0], "sn")
        fwd(1, nb.at[0], None)

        @at_step(j, 0)
        def _():
            z_relay("d1", 1, 1)

        @at_step(j, 1)
        def _():
            z_got("d1")
            sum_sends_done("d1")
            e_calc()
            z_gather("o0z", o_own)

        staged(o1_buf, block, ob.at[0], "so")
        bwd_hidden(1, ob.at[0])

        @at_step(j, 0)
        def _():
            ag_got_x("o1", o1_buf, 1, cut)

        @at_step(j, 2)
        def _():
            ag_got_x("n0", n0_buf, 0, cut)
            ag_got_x("n0", n0_buf, 1, cut)

        weight_grads(nb.at[0], ob.at[0])
        return carry

    lax.fori_loop(0, 3, l1_step, 0)
    grads_out(1)
    z_gathered("o0z", o_own)
    for h in range(2):
        ag_x("o0", o0_buf, o0_src, h)
        ag_y("o0", o0_buf, o0_src, h)
    core_sum_send("d2")
    got("xp", x_part)
    xl = [local("xl0", x_in, nb.at[1, rows(c * td, td)]), local("xl1", x_part, nb.at[1, rows(co * td, td)])]
    for s in xl:
        s.start()
    stage(n0_buf, q, nb.at[0], "sn")
    back = lambda block: (local("sa", a_save.at[block], a_t), local("sb", b_save.at[block], b_t))
    for s in back(q):
        s.start()
    for s in xl:
        s.wait()

    def r_step(i, carry):
        h_f = nb[1, rows(i * 16, 16), :].astype(F32)
        r_own[rows(i * 16, 16), :] = jnp.broadcast_to(rinv(h_f), (16, 128))
        return carry

    lax.fori_loop(0, t2 // 16, r_step, 0)
    z_gathered_partner("o0z", o_own)
    for s in back(q):
        s.wait()

    def gz_id(zi):
        base = sid(("gz", 0))
        for i in range(4):
            assert sid(("gz", i)) == base + i
        return base + zi

    def yz_id(zi):
        base = sid(("yz", 0))
        for i in range(4):
            assert sid(("yz", i)) == base + i
        return base + zi

    def y_rows(zi):
        return y_out.at[rows(zi * ch, ch)]

    gz_id(0)
    yz_id(0)

    bwd_hidden(0, o_own)

    @scoped
    def dgain0():
        def dg_step(i, carry):
            w = cols(i * tile, tile)
            m = mm(a_t[...], wg[0, rows(i * tile, tile)], 1, 1) + mm(b_t[...], wu[0, rows(i * tile, tile)], 1, 1)
            xh = nb[1, :, w].astype(F32) * r_own[:, 0:1]
            dg[0:1, w] = jnp.sum(m * xh, axis=0, keepdims=True)
            return carry

        lax.fori_loop(0, d // tile, dg_step, 0)

    dgain0()
    push("gc", lambda: (dg, dg_core, to_c))
    z_relay("d2", 0, 0)
    z_relay("d2", 0, 1)
    staged(n0_buf, q, nb.at[0], "sn")
    grads_out_done(1)
    zero_acc()
    weight_grads(nb.at[0], o_own)
    z_relay("d2", 1, 0)
    ag_got_y("o0", o0_buf, 0)
    z_relay("d2", 1, 1)
    ag_got_dx("n0", n0_buf, cut)
    for h in range(2):
        ag_got_dy("n0", n0_buf, h, cut)

    def f0_step(j, carry):
        f0_other(j)
        return carry

    lax.fori_loop(1, 3, f0_step, 0)
    ag_got_y("o0", o0_buf, 1)
    ag_got_x("o0", o0_buf, 0, half)

    def l0_body(j, carry):
        block = block_of(j)

        @at_step(j, 2)
        def _():
            ag_got_dx("o0", o0_buf, half)
            ag_got_dy("o0", o0_buf, 1, half)

        for s in back(block):
            s.start()
        stage(n0_buf, block, nb.at[0], "sn")
        partner_has("o0", o0_buf, j)
        stage(o0_buf, block, ob.at[0], "so")
        for s in back(block):
            s.wait()
        staged(o0_buf, block, ob.at[0], "so")
        bwd_hidden(0, ob.at[0])

        @at_step(j, 0)
        def _():
            ag_got_x("o0", o0_buf, 1, half)
            got("gc", dg_core)
            copy_of("gc", "gc", dg, dg_core, to_c).wait_send()
            dg[...] = dg[...] + dg_core[...]
            push("gx", lambda: (dg, dg_x, to_x))
            z_got("d2")

            def y_step(i, carry):
                r = rows(i * 16, 16)
                y_ch[r, :] = (h1_ch[r, :].astype(F32) + z_sum(i)).astype(BF16)
                return carry

            lax.fori_loop(0, ch // 16, y_step, 0)
            local("yk", y_ch, y_rows(z)).start()
            for k in (1, 2, 3):
                push(("ys", k), lambda: (y_ch, y_rows(z), at_z(z_other(k))), yz_id(z))

        @at_step(j, 1)
        def _():
            got("gx", dg_x)
            copy_of("gx", "gx", dg, dg_x, to_x).wait_send()
            dg[...] = dg[...] + dg_x[...]
            push("gy", lambda: (dg, dg_y, to_y))

        @at_step(j, 2)
        def _():
            got("gy", dg_y)
            copy_of("gy", "gy", dg, dg_y, to_y).wait_send()
            dg_z[z] = dg[...] + dg_y[...]
            for k in (1, 2, 3):
                push(("gs", k), lambda: (dg_z.at[z], dg_z.at[z], at_z(z_other(k))), gz_id(z))

        staged(n0_buf, block, nb.at[0], "sn")
        weight_grads(nb.at[0], ob.at[0])
        return carry

    lax.fori_loop(0, 3, l0_body, 0)
    grads_out(0)
    for key in ("gc", "gx", "gy"):
        sent.pop(key)
    for k in (1, 2, 3):
        with jax.named_scope("got_gz"):
            got(gz_id(z_other(k)), dg_z.at[z_other(k)])
    dgain_out[...] = dg_z[0] + dg_z[1] + dg_z[2] + dg_z[3]
    for k in (1, 2, 3):
        with jax.named_scope("got_yz"):
            got(yz_id(z_other(k)), y_rows(z_other(k)))
    local("yk", y_ch, y_rows(z)).wait()
    grads_out_done(0)
    for key in list(sent):
        send_done(key)


def make_call(td, d, rb, hs):
    fb = hs // 4
    hh, t2, ch = 2 * fb, 2 * td, td // 4
    shape = jax.ShapeDtypeStruct
    hbm = pl.BlockSpec(memory_space=pl.ANY)
    vmem = pl.BlockSpec(memory_space=pltpu.VMEM)
    block = shape((4, 2, td, d), BF16)
    outs = [
        shape((td, d), BF16), shape((2, rb, hs), F32), shape((2, rb, hs), F32), shape((2, fb, d), F32), shape((2, d), F32),
        block, block, block, block, shape((4, t2, hh), BF16), shape((4, t2, hh), BF16), shape((td, d), BF16),
    ]
    scratch = [
        pltpu.VMEM((2, d, hh), BF16), pltpu.VMEM((2, d, hh), BF16), pltpu.VMEM((2, hh, d), BF16),
        pltpu.VMEM((2 * rb, hh), F32), pltpu.VMEM((2 * rb, hh), F32), pltpu.VMEM((fb, d), F32),
        pltpu.VMEM((2, t2, d), BF16), pltpu.VMEM((1, t2, d), BF16),
        pltpu.VMEM((t2, hh), BF16), pltpu.VMEM((t2, hh), BF16), pltpu.VMEM((t2, hh), BF16), pltpu.VMEM((t2, hh), BF16),
        pltpu.VMEM((t2, d), F32), pltpu.VMEM((td, d), F32), pltpu.VMEM((4, ch, d), F32),
        pltpu.VMEM((t2, d), BF16), pltpu.VMEM((t2, d), BF16),
        pltpu.VMEM((ch, d), BF16), pltpu.VMEM((ch, d), BF16), pltpu.VMEM((ch, d), BF16), pltpu.VMEM((ch, d), BF16),
        pltpu.VMEM((t2, 128), F32),
        pltpu.VMEM((2, d), F32), pltpu.VMEM((2, d), F32), pltpu.VMEM((2, d), F32), pltpu.VMEM((2, d), F32), pltpu.VMEM((4, 2, d), F32),
        pltpu.SemaphoreType.DMA((NSEM,)), pltpu.SemaphoreType.DMA((NSEM,)), pltpu.SemaphoreType.DMA((NLOC,)),
    ]
    return pl.pallas_call(
        kernel,
        out_shape=outs,
        in_specs=[hbm] * 5 + [vmem],
        out_specs=[hbm] * 4 + [vmem] + [hbm] * 7,
        scratch_shapes=scratch,
        compiler_params=pltpu.CompilerParams(collective_id=0, has_side_effects=True, vmem_limit_bytes=67043328),
    )


def solution(mesh):
    tok_spec = P(("replica", "fsdp"), None)
    wide_spec = P(None, "fsdp", "tensor")
    down_spec = P(None, ("tensor", "fsdp"), None)
    gain_spec = P(None, None)

    def device_fn(x_loc, dy_loc, w_gate, w_up, w_down, norm_gain):
        call = make_call(x_loc.shape[0], x_loc.shape[1], w_gate.shape[1], w_gate.shape[2])
        return tuple(call(x_loc, dy_loc, w_gate, w_up, w_down, norm_gain)[:5])

    return jax.shard_map(device_fn, mesh=mesh, in_specs=(tok_spec, tok_spec, wide_spec, wide_spec, down_spec, gain_spec), out_specs=(tok_spec, wide_spec, wide_spec, down_spec, gain_spec), check_vma=False)
```

time: 2070 us -> 343 us (0.17)
  waiting for transfers between devices: 1850 us -> 0 us
  Pallas kernels: 0 us -> 319 us
  matrix products: 133 us -> 0 us
  other arithmetic: 25.7 us -> 0.01 us
  blocking collectives: 24.2 us -> 0 us
    psum x4 -> x0, waiting for transfers between devices: 824 us -> none  [the longest x1 531 us: device_fn(): lax.psum(lax.psum_scatter(part_gate[layer_idx], 'fsdp', scatter_dimension...]
    reduce_scatter x6 -> x0, waiting for transfers between devices: 700 us -> none  [the longest x2 254 us: device_fn(): lax.psum_scatter(part_down[layer_idx], 'fsdp', scatter_dimension=0, tiled...]
    all_gather x6 -> x0, waiting for transfers between devices: 322 us -> none  [the longest x2 108 us: gather_layer(): full_up = lax.all_gather(w_up[layer_idx], 'fsdp', axis=0, tiled=True)]
    pallas_call x0 -> x1, Pallas kernels: none -> 319 us  [device_fn(): return tuple(call(x_loc, dy_loc, w_gate, w_up, w_down, norm_gain)[:5])]
    dot_general x18 -> x0, matrix products: 133 us -> none  [the longest x2 19.5 us: device_fn(): jnp.einsum('td,tf->df', normed, d_up, preferred_element_type=jnp.float32)]
    psum x1 -> x0, blocking collectives: 24.2 us -> none  [device_fn(): d_gain = lax.psum(jnp.stack(part_gain), ('replica', 'fsdp'))]
  transfers between devices with their start and end apart: 16 -> 0, of which waited for: 16 -> 0; matrix products, arithmetic and copies ran while one was open for 7% -> 0% of each run, Pallas kernels for 0% -> 0%
where the time goes in v2:
time: 343 us; the launch traced here: 341 us
  Pallas kernels  319 us (93%)
  local copies, waits for them, and re-layouts  20.8 us (6%)
    pallas_call x1, Pallas kernels, device_fn(): return tuple(call(x_loc, dy_loc, w_gate, w_up, w_down, norm_gain)[:5])  319 us
    unnamed x13, local copies, waits for them, and re-layouts  20.8 us

profile of v2, /device:TPU:0, one launch (start us, length us, event | category | flops | bytes accessed | tf_op | source)
XLA Modules:
  0.0 340.6 jit_solution(6033156594758546331)
XLA Ops:
  0.6 319.2 %shard_map.101 = (bf16[256,2048]{1,0:T(8,128)(2,1)}, f32[2,512,2048]{2,1,0:T(8,128)}, f32[2,512,2048]{2,1,0:T(8,128)}, f32[2,512,2048]{2,1,0:T(8,128)}, f32[2,20...) custom-call(bf16[256,2048]{1,0:T(8,128)(2,1)} %x_in.1, ...), custom_call_target="tpu_custom_call" | custom-call | tf_op jit(solution)/shard_map/pallas_call | solution.py:869
  319.8 2.3 copy.16
  322.1 0.0 copy-start
  322.1 0.0 slice-start
  322.1 8.9 %copy.17 = f32[2,512,2048]{2,1,0:T(8,128)} copy(f32[2,512,2048]{2,1,0:T(8,128)} %get-tuple-element.21) | data formatting | bytes 16777216
  331.0 0.0 copy-done
  331.0 0.0 slice-start.1
  331.0 4.3 %copy.18 = f32[2,512,2048]{2,1,0:T(8,128)} copy(f32[2,512,2048]{2,1,0:T(8,128)S(1)} %copy-done) | data formatting | bytes 16777216
  335.3 0.0 slice-done
  335.3 1.3 slice-done.1
  336.6 0.0 copy-start.1
  336.6 3.4 copy.19
  340.0 0.0 copy-done.1
  340.0 0.6 copy.20
  (1 shorter events, 0.0 us)
Async XLA Ops:
  322.1 8.9 %copy-start = (f32[2,512,2048]{2,1,0:T(8,128)S(1)}, f32[2,512,2048]{2,1,0:T(8,128)}, u32[]{:S(2)}) copy-start(f32[2,512,2048]{2,1,0:T(8,128)} %get-tuple-element.22) | copy-start | bytes 25165828
  322.1 13.2 %slice-start = ((s8[8388608]{0:T(1024)(128)(4,1)}), s8[4194304]{0:T(1024)(128)(4,1)S(1)}, s32[]{:S(2)}) async-start(s8[8388608]{0:T(1024)(128)(4,1)} %bitcast), calls=%async_computation | async-start | bytes 8388608
  331.0 5.6 %slice-start.1 = ((s8[8388608]{0:T(1024)(128)(4,1)}), s8[4194304]{0:T(1024)(128)(4,1)S(1)}, s32[]{:S(2)}) async-start(s8[8388608]{0:T(1024)(128)(4,1)} %bitcast), calls=%async_computation.1 | async-start | bytes 8388608
  336.6 3.4 copy-start.1

commit v3 on v2

v3 whole, which is shorter than its diff:
```python
import jax
import jax.numpy as jnp
from jax import lax
from jax.experimental import pallas as pl
from jax.experimental.pallas import tpu as pltpu
from jax.sharding import PartitionSpec as P

F32 = jnp.float32
BF16 = jnp.bfloat16
MESH = pl.DeviceIdType.MESH
NSEM = 340
NLOC = 96


def mm(lhs, rhs, ldim, rdim):
    return lax.dot_general(lhs, rhs, (((ldim,), (rdim,)), ((), ())), preferred_element_type=F32)


def kernel(
    x_in, dy_in, wg_in, wu_in, wd_in, gain,
    y_out, dwg_out, dwu_out, dwd_out, dgain_out, n0_buf, n1_buf, o1_buf, o0_buf, a_save, b_save, x_part, g_save, core_hbm,
    wg, wu, wd, acc_g, acc_u, acc_d, nb, ob, a_t, b_t, g_t, part, from_z,
    x_ch, h1_ch, r_own, dg, dg_core, dg_x, dg_y, dg_z, ssem, rsem, lsem, credit,
):
    td, d = x_in.shape
    rb = wg_in.shape[1]
    fb = wg_in.shape[2] // 4
    hh = 2 * fb
    t2, ch, half = 2 * td, td // 4, td // 2
    hc = ch // 2
    tile = min(512, fb)
    z = lax.axis_index("tensor")
    y = lax.axis_index("replica")
    f = lax.axis_index("fsdp")
    x, c = f // 2, f % 2
    xo, yo, co = 1 - x, 1 - y, 1 - c
    q, qx, qy, qd = 2 * y + x, 2 * y + xo, 2 * yo + x, 2 * yo + xo
    cs = (c + y) % 2
    cso = 1 - cs
    to_c, to_x, to_xs, to_y = {"fsdp": 2 * x + co}, {"fsdp": 2 * xo + c}, {"fsdp": 2 * xo + cs}, {"replica": yo}
    inner = ((z + 1) // 2) % 2
    outer = 1 - inner
    up = z // 2
    pair = z + 1 - 2 * (z % 2)
    far_outer, far_inner = 3 - 3 * up, 2 - up
    order = (outer * far_outer + inner * pair, outer * far_inner + inner * far_outer, outer * pair + inner * far_inner, z)

    n_own, o_own = nb.at[1], ob.at[1]

    def at_z(i):
        return {"tensor": i}

    def z_other(k):
        return (z + 4 + k * (1 - 2 * up)) % 4

    others = tuple(z_other(k) for k in (1, 2, 3))
    toward = outer * pair + inner * far_inner

    def rows(start, size):
        return pl.ds(start if isinstance(start, int) else pl.multiple_of(start, size if size % 16 == 0 else 8), size)

    def cols(start, size):
        return pl.ds(start if isinstance(start, int) else pl.multiple_of(start, 128), size)

    ids, lids, sent, passed = {}, {}, {}, {}

    def sid(key):
        i = ids.setdefault(key, len(ids))
        assert i < NSEM, i
        return i

    def name_of(key):
        return key if isinstance(key, str) else "_".join(map(str, key))

    def copy_of(skey, rkey, src, dst, dev):
        return pltpu.make_async_remote_copy(
            src_ref=src, dst_ref=dst, send_sem=ssem.at[sid(skey)], recv_sem=rsem.at[rkey if not isinstance(rkey, (str, tuple)) else sid(rkey)],
            device_id=dev, device_id_type=MESH,
        )

    def push(key, make, rkey=None):
        copy_of(key, key if rkey is None else rkey, *make()).start()
        sent[key] = make

    def got(key, dst):
        with jax.named_scope("got_" + (name_of(key) if isinstance(key, (str, tuple)) else "dyn")):
            copy_of("none", key, dst, dst, to_c).wait_recv()

    def send_done(key):
        copy_of(key, key, *sent.pop(key)()).wait_send()

    def local(key, src, dst):
        i = lids.setdefault(key, len(lids))
        assert i < NLOC, i
        return pltpu.make_async_copy(src, dst, lsem.at[i])

    def scoped(fn):
        def run(*args):
            with jax.named_scope(fn.__name__):
                return fn(*args)

        return run

    gu = ((wg_in, wg), (wu_in, wu))
    pieces = (2, 2)

    def wview(m, l, row, xb, k=0, n=1):
        return gu[m][1].at[l, rows(row * rb + k * (rb // n), rb // n), cols(xb * fb, fb)]

    def wsrc(m, l, xb, core, k=0, n=1):
        return gu[m][0].at[l, pl.ds(k * (rb // n), rb // n), cols((2 * xb + core) * fb, fb)]

    def push_w(l, m):
        n = pieces[l]
        for xb in range(2):
            for k in range(n):
                push(("wx", l, m, xb, k), lambda xb=xb, k=k: (wsrc(m, l, xb, cs, k, n), wview(m, l, f, xb, k, n), to_xs))
        for k in range(4 * m):
            r0 = y * (fb // 2) + k * (fb // 8)
            push(("wdx", l, k), lambda r0=r0: (wd_in.at[l, rows(r0, fb // 8)], wd.at[l, rows(x * fb + r0, fb // 8)], to_x))
        if (l, m) == (1, 1):
            r1 = yo * (fb // 2) + 3 * (fb // 8)
            push("wdx_last", lambda: (wd_in.at[l, rows(r1, fb // 8)], wd.at[l, rows(x * fb + r1, fb // 8)], to_x))

    def push_wc(l):
        for m in range(2):
            for xb in range(2):
                push(("wc", l, m, xb), lambda m=m, xb=xb: (wsrc(m, l, xb, co), wview(m, l, f, xb), to_c))
                local(("w", l, m, xb), wsrc(m, l, xb, c), wview(m, l, f, xb)).start()
        local(("wd", l), wd_in.at[l], wd.at[l, rows(x * fb, fb)]).start()

    def relay_gu(l, m, xb):
        n = pieces[l]
        for k in range(n):
            ref = lambda k=k: wview(m, l, 2 * xo + cs, xb, k, n)
            got(("wx", l, m, xb, k), ref())
            push(("wy", l, m, xb, k), lambda k=k: (ref(k), ref(k), to_y))

    def relay_d(l, k):
        ref = lambda: wd.at[l, rows(xo * fb + y * (fb // 2) + k * (fb // 8), fb // 8)]
        got(("wdx", l, k), ref())
        push(("wdy", l, k), lambda: (ref(), ref(), to_y))

    def have_gu(l, m, xb):
        n = pieces[l]
        local(("w", l, m, xb), wsrc(m, l, xb, c), wview(m, l, f, xb)).wait()
        got(("wc", l, m, xb), wview(m, l, 2 * x + co, xb))
        for k in range(n):
            got(("wy", l, m, xb, k), wview(m, l, 2 * xo + cso, xb, k, n))

    def have_d_own(l):
        local(("wd", l), wd_in.at[l], wd.at[l, rows(x * fb, fb)]).wait()

    def have_d(l):
        for k in range(4 - l):
            got(("wdy", l, k), wd.at[l, rows(xo * fb + yo * (fb // 2) + k * (fb // 8), fb // 8)])
        if l == 1:
            got(("wdx", 1, 3), wd.at[1, rows(xo * fb + y * (fb // 2) + 3 * (fb // 8), fb // 8)])
            got("wdx_last", wd.at[1, rows(xo * fb + yo * (fb // 2) + 3 * (fb // 8), fb // 8)])

    def piece(buf, block, core, start, size):
        return buf.at[block, core, pl.ds(start, size)]

    def chunk(buf, block, core, zi):
        return buf.at[block, core, rows(zi * ch, ch)]

    def part_id(a, j):
        base = sid((a, "p", 0))
        for jj in range(3):
            assert sid((a, "p", jj)) == base + jj
        return base + j

    def share(a, j, tag, ref):
        push((a, "s", j, tag), lambda: (ref(), ref(), to_c), (a, "p", j))

    def ag_x(a, buf, src, h):
        push((a, "x", h), lambda: (src().at[pl.ds(h * half, half)], piece(buf, q, c, h * half, half), to_x))

    def ag_y(a, buf, src, h):
        push((a, "y", h), lambda: (src().at[pl.ds(h * half, half)], piece(buf, q, c, h * half, half), to_y))

    def ag_quarter(a, buf, src, axis):
        push((a, axis + "c"), lambda: (src().at[rows(z * ch, ch)], chunk(buf, q, c, z), to_y if axis == "y" else to_x))

    def zb_id(a, axis, zi):
        base = sid((a, axis, "zb", 0))
        for i in range(4):
            assert sid((a, axis, "zb", i)) == base + i
        return base + zi

    def ag_spread(a, buf, axis):
        block = qy if axis == "y" else qx
        got((a, axis + "c"), chunk(buf, block, c, z))
        for k in (1, 2, 3):
            push((a, axis, "zs", k), lambda k=k: (chunk(buf, block, c, z), chunk(buf, block, c, z), at_z(z_other(k))), zb_id(a, axis, z))

    def ag_spread_got(a, buf, axis):
        block = qy if axis == "y" else qx
        for k in (1, 2, 3):
            with jax.named_scope("got_zb_" + a + axis):
                got(zb_id(a, axis, z_other(k)), chunk(buf, block, c, z_other(k)))
        share(a, 0 if axis == "y" else 1, 0, lambda: buf.at[block, c])

    def ag_dx(a, buf, cut):
        push((a, "dx"), lambda: (piece(buf, qy, c, 0, cut), piece(buf, qy, c, 0, cut), to_x))

    def ag_got_y(a, buf, h):
        got((a, "y", h), piece(buf, qy, c, h * half, half))
        share(a, 0, h, lambda: piece(buf, qy, c, h * half, half))
        if h == 0:
            ag_dx(a, buf, half)

    def ag_dy(a, buf, cut):
        push((a, "dy", 0), lambda: (piece(buf, qx, c, cut, td - cut), piece(buf, qx, c, cut, td - cut), to_y))

    def ag_got_dy_whole(a, buf, cut):
        got((a, "dy", 0), piece(buf, qd, c, cut, td - cut))
        share(a, 2, 0, lambda: piece(buf, qd, c, cut, td - cut))

    def diag_piece(h, cut):
        start = max(cut, h * half)
        return start, (h + 1) * half - start

    def ag_got_x(a, buf, h, cut):
        got((a, "x", h), piece(buf, qx, c, h * half, half))
        start, size = diag_piece(h, cut)
        if size:
            push((a, "dy", h), lambda: (piece(buf, qx, c, start, size), piece(buf, qx, c, start, size), to_y))
        share(a, 1, h, lambda: piece(buf, qx, c, h * half, half))

    def ag_got_dx(a, buf, cut):
        got((a, "dx"), piece(buf, qd, c, 0, cut))
        share(a, 2, "x", lambda: piece(buf, qd, c, 0, cut))

    def ag_got_dy(a, buf, h, cut):
        start, size = diag_piece(h, cut)
        if size:
            got((a, "dy", h), piece(buf, qd, c, start, size))
            share(a, 2, h, lambda: piece(buf, qd, c, start, size))

    def block_of(j):
        return 2 * ((y + (j + 1) % 2) % 2) + (x + (j + 1) // 2) % 2

    def partner_has(a, buf, j):
        with jax.named_scope("got_p_" + a):
            got(part_id(a, j), buf.at[block_of(j), co])

    for a in ("n0", "o1", "n1", "o0"):
        for j in range(3):
            sid((a, "p", j))
        for axis in "xy":
            for i in range(4):
                sid((a, axis, "zb", i))

    def fwd_tile(l, n_ref, g_ref, i, a_ref=None, b_ref=None):
        w = cols(i * tile, tile)
        a = mm(n_ref[...], wg[l, :, w], 1, 0).astype(BF16)
        b = mm(n_ref[...], wu[l, :, w], 1, 0).astype(BF16)
        (a_t if a_ref is None else a_ref)[:, w] = a
        (b_t if b_ref is None else b_ref)[:, w] = b
        if g_ref is not None:
            a_f = a.astype(F32)
            g_ref[:, w] = (a_f * jax.nn.sigmoid(a_f) * b.astype(F32)).astype(BF16)

    @scoped
    def fwd(l, n_ref, g_ref, a_ref=None, b_ref=None):
        def step(i, carry):
            fwd_tile(l, n_ref, g_ref, i, a_ref, b_ref)
            return carry

        lax.fori_loop(0, hh // tile, step, 0)

    @scoped
    def down_half(l, g_ref, kb, start, size, add):
        r, k = rows(start, size), pl.ds(pl.multiple_of(kb * fb, fb), fb)

        def step(i, carry):
            w = cols(i * tile, tile)
            new = mm(g_ref[r, k], wd[l, k, w], 1, 0)
            part[r, w] = part[r, w] + new if add else new
            return carry

        lax.fori_loop(0, d // tile, step, 0)

    @scoped
    def down_rows(l, g_ref, core):
        r = rows(core * td, td)

        def step(i, carry):
            w = cols(i * tile, tile)
            part[r, w] = mm(g_ref[r, :], wd[l, :, w], 1, 0)
            return carry

        lax.fori_loop(0, d // tile, step, 0)

    @scoped
    def m_half(l, kb, start, size, add):
        r, k = rows(start, size), pl.ds(pl.multiple_of(kb * fb, fb), fb)

        def step(i, carry):
            w = rows(i * tile, tile)
            new = mm(a_t[r, k], wg[l, w, k], 1, 1) + mm(b_t[r, k], wu[l, w, k], 1, 1)
            o = cols(i * tile, tile)
            part[r, o] = part[r, o] + new if add else new
            return carry

        lax.fori_loop(0, d // tile, step, 0)

    def bwd_tile(l, o_ref, i, a_ref, b_ref):
        w = cols(i * tile, tile)
        q_f = mm(o_ref[...], wd[l, rows(i * tile, tile)], 1, 1).astype(BF16).astype(F32)
        a_f, b_f = a_ref[:, w].astype(F32), b_ref[:, w].astype(F32)
        s = jax.nn.sigmoid(a_f)
        g_t[:, w] = (a_f * s * b_f).astype(BF16)
        a_t[:, w] = (q_f * b_f * s * (1.0 + a_f * (1.0 - s))).astype(BF16)
        b_t[:, w] = (q_f * a_f * s).astype(BF16)

    @scoped
    def bwd_hidden(l, o_ref, a_ref, b_ref):
        for i in range(hh // tile):
            bwd_tile(l, o_ref, i, a_ref, b_ref)

    @scoped
    def weight_grads(n_ref, col, o_ref, between):
        t = min(256, fb)

        def half_rows(core):
            for i in range(rb // t):
                n_rows = n_ref[:, cols(col + core * rb + i * t, t)]
                w = rows(core * rb + i * t, t)
                acc_g[w, :] += mm(n_rows, a_t[...], 0, 0)
                acc_u[w, :] += mm(n_rows, b_t[...], 0, 0)

        half_rows(co)
        if between is not None:
            between()
        half_rows(c)
        for i in range(fb // t):
            acc_d[pl.ds(i * t, t), :] += mm(g_t[:, cols(x * fb + i * t, t)], o_ref[...], 0, 0)

    @scoped
    def zero_acc():
        for ref in (acc_g, acc_u, acc_d):
            def step(i, carry, ref=ref):
                ref[rows(i * 16, 16), :] = jnp.zeros((16, ref.shape[1]), F32)
                return carry

            lax.fori_loop(0, ref.shape[0] // 16, step, 0)

    def rinv(h_f):
        return lax.rsqrt(jnp.mean(h_f * h_f, axis=-1, keepdims=True) + 1e-6)

    def core_land(key):
        return core_hbm if key == "d2" else acc_d

    def core_push(key):
        for k in range(4):
            push((key, "c", k), lambda k=k: (part.at[rows(co * td + order[k] * ch, ch)], core_land(key).at[rows(order[k] * ch, ch)], to_c))

    def z_ids(key):
        base = sid((key, "A", 0))
        for h in range(2):
            for i, s in enumerate("ABCD"):
                assert sid((key, s, h)) == base + 4 * h + i
        return base

    for sum_key in ("d0", "d1", "d2"):
        z_ids(sum_key)

    def mine(zi, h):
        return part.at[rows(c * td + zi * ch + h * hc, hc)]

    def slot(key, i, h):
        return from_z.at[i, pl.ds(h * hc, hc)]

    def core_back(k):
        return local(("cl", k), core_hbm.at[rows(order[k] * ch, ch)], part.at[rows(co * td + order[k] * ch, ch)])

    def core_back_start(key):
        for k in range(4):
            got((key, "c", k), core_land(key).at[rows(order[k] * ch, ch)])
            send_done((key, "c", k))
            core_back(k).start()

    @scoped
    def core_sum_send(key):
        z_ids(key)
        for k in range(4):
            if key == "d2":
                core_back(k).wait()
            else:
                got((key, "c", k), core_land(key).at[rows(order[k] * ch, ch)])

            def step(i, carry):
                r = order[k] * ch + i * 16
                mine_r = rows(c * td + r, 16)
                part[mine_r, :] = part[mine_r, :] + (part[rows(co * td + r, 16), :] if key == "d2" else acc_d[rows(r, 16), :])
                return carry

            lax.fori_loop(0, ch // 16, step, 0)
            if k == 0:
                for h in range(2):
                    push((key, "A", h), lambda h=h: (mine(order[0], h), slot(key, 0, h), at_z(pair)))
            elif k < 3:
                @pl.when(outer == 1)
                def _():
                    for h in range(2):
                        copy_of((key, "BC"[k - 1], h), (key, "BC"[k - 1], h), mine(order[k], h), slot(key, k, h), at_z(pair)).start()


    def z_relay(key, n, h):
        @pl.when(inner == 1)
        def _():
            got((key, "AB"[n], h), slot(key, n, h))
            zi = (far_outer, far_inner)[n]
            work = slot(key, n, h)

            def step(i, carry):
                r = rows(i * 8, 8)
                work[r, :] = work[r, :] + part[rows(c * td + zi * ch + h * hc + i * 8, 8), :]
                return carry

            lax.fori_loop(0, hc // 8, step, 0)
            if n == 0:
                copy_of((key, "B", h), (key, "B", h), work, slot(key, 1, h), at_z(far_outer)).start()
            else:
                copy_of((key, "C", h), (key, "D", h), work, slot(key, 3, h), at_z(far_inner)).start()

    def z_got(key):
        base = z_ids(key)
        for h in range(2):
            for i in range(2):
                with jax.named_scope("got_" + key):
                    got(base + 4 * h + 2 * inner + i, slot(key, 2 * inner + i, h))

    def z_sum(key, i):
        r = rows(i * 16, 16)
        return part[rows(c * td + z * ch + i * 16, 16), :] + from_z[2 * inner, r, :] + from_z[2 * inner + 1, r, :]

    def relay_sends_done(key):
        @pl.when(inner == 1)
        def _():
            for s in "BC":
                for h in range(2):
                    copy_of((key, s, h), (key, s, h), mine(0, h), slot(key, 0, h), at_z(pair)).wait_send()

    def sum_sends_done(key):
        for part_key in [(key, "c", k) for k in range(4)] + [(key, "A", h) for h in range(2)]:
            send_done(part_key)

        @pl.when(outer == 1)
        def _():
            for s in "BC":
                for h in range(2):
                    copy_of((key, s, h), (key, s, h), mine(0, h), slot(key, 0, h), at_z(pair)).wait_send()

    def quarter(ref, core, zi):
        return ref.at[rows(core * td + zi * ch, ch)]

    def zg_id(key, zi):
        base = sid((key, "z", 0))
        for i in range(4):
            assert sid((key, "z", i)) == base + i
        return base + zi

    relayed = ("n1z",)

    def takes(key):
        return (pair, far_inner, far_outer) if key in relayed else others

    def z_push(key, make, zi):
        for k, dev in enumerate((toward,) if key in relayed else others):
            push((key, "zs", k), lambda dev=dev: (*make(zi), at_z(dev)), zg_id(key, zi))
        if key in relayed:
            z_forward(key, 3, make(zi)[1], zg_id(key, zi), pair)
            passed[(key, "fw", 3)] = lambda: make(z)[1]

    def z_forward(key, i, ref, rkey, dev):
        @pl.when(inner == 1)
        def _():
            copy_of((key, "fw", i), rkey, ref, ref, at_z(dev)).start()

    def z_pass(key, make, i):
        zi = takes(key)[i]
        with jax.named_scope("got_%s_%d" % (key, i)):
            got(zg_id(key, zi), make(zi)[1])
        if key in relayed:
            z_forward(key, i, make(zi)[1], zg_id(key, zi), (far_inner, pair, pair)[i])
            passed[(key, "fw", i)] = lambda: make(zi)[1]

    def passed_done(which):
        @pl.when(inner == 1)
        def _():
            for key in [k1 for k1 in passed if k1[0] == which]:
                ref = passed.pop(key)
                copy_of(key, key, ref(), ref(), to_c).wait_send()

    def z_gather(key, ref):
        z_push(key, lambda zi: (quarter(ref, c, zi), quarter(ref, c, zi)), z)
        push((key, "s", 0), lambda: (quarter(ref, c, z), quarter(ref, c, z), to_c))

    def z_take(key, ref, i):
        z_pass(key, lambda zi: (quarter(ref, c, zi), quarter(ref, c, zi)), i)
        push((key, "s", 1 + i), lambda: (quarter(ref, c, takes(key)[i]), quarter(ref, c, takes(key)[i]), to_c))

    def z_gathered_partner(key, ref):
        got((key, "s", 0), quarter(ref, co, z))
        for i in range(3):
            got((key, "s", 1 + i), quarter(ref, co, takes(key)[i]))

    def stage(buf, block, slot_ref, key):
        for core in range(2):
            local((key, core), buf.at[block, core], slot_ref.at[pl.ds(core * td, td)]).start()

    def staged(buf, block, slot_ref, key):
        for core in range(2):
            local((key, core), buf.at[block, core], slot_ref.at[pl.ds(core * td, td)]).wait()

    def save_ab(block):
        return (local("sa", a_t, a_save.at[block]), local("sb", b_t, b_save.at[block]))

    @scoped
    def f0_other(j, slot):
        fwd(0, nb.at[slot], None)
        for s in save_ab(block_of(j)):
            s.start()

    def saves_done(block):
        for s in save_ab(block):
            s.wait()

    def a_kept(k):
        return wg.at[1, rows(k * t2, t2)]

    def b_kept(k):
        return wd.at[1, rows((k // 2) * t2, t2), cols((k % 2) * hh, hh)]

    def load_ab(block, k):
        return (local(("la", k), a_save.at[block], a_kept(k)), local(("lb", k), b_save.at[block], b_kept(k)))

    def grads_push(l):
        for i, (acc, out) in enumerate(((acc_g, dwg_out), (acc_u, dwu_out))):
            for xb in range(2):
                push(("q", l, i, xb), lambda acc=acc, out=out, xb=xb: (acc.at[rows(co * rb, rb), cols(xb * fb, fb)], out.at[l, :, cols((2 * xb + c) * fb, fb)], to_c))

    def grads_out(l):
        for i, (acc, out) in enumerate(((acc_g, dwg_out), (acc_u, dwu_out))):
            for xb in range(2):
                local(("qo", l, i, xb), acc.at[rows(c * rb, rb), cols(xb * fb, fb)], out.at[l, :, cols((2 * xb + c) * fb, fb)]).start()
        local(("qd", l), acc_d, dwd_out.at[l]).start()

    @scoped
    def grads_out_done(l):
        for i, (acc, out) in enumerate(((acc_g, dwg_out), (acc_u, dwu_out))):
            for xb in range(2):
                local(("qo", l, i, xb), acc.at[rows(c * rb, rb), cols(xb * fb, fb)], out.at[l, :, cols((2 * xb + c) * fb, fb)]).wait()
                send_done(("q", l, i, xb))
                got(("q", l, i, xb), out.at[l, :, cols((2 * xb + co) * fb, fb)])
        local(("qd", l), acc_d, dwd_out.at[l]).wait()

    barrier = pltpu.get_barrier_semaphore()
    for dev in (to_c, to_x, {"fsdp": 2 * xo + co}, to_y, at_z((z + 1) % 4), at_z((z + 2) % 4), at_z((z + 3) % 4)):
        pl.semaphore_signal(barrier, inc=1, device_id=dev, device_id_type=MESH)
    x_load = local("x", x_in, nb.at[1, pl.ds(0, td)])
    x_load.start()
    with jax.named_scope("barrier"):
        pl.semaphore_wait(barrier, 7)

    dy_src = lambda: dy_in
    n0_src = lambda: n0_buf.at[q, c]
    n1_src = lambda: n_own.at[rows(c * td, td)]
    o0_src = lambda: o_own.at[rows(c * td, td)]
    cut_n, cut_o = ch, ch

    push_w(0, 0)
    push_wc(0)
    x_load.wait()

    def n0_step(i, carry):
        h_f = n_own[rows(i * 16, 16), :].astype(F32)
        r_inv = rinv(h_f)
        nb[0, rows(c * td + i * 16, 16), :] = (h_f * r_inv * gain[0:1, :]).astype(BF16)
        r_own[rows(c * td + i * 16, 16), :] = jnp.broadcast_to(r_inv, (16, 128))
        return carry

    lax.fori_loop(0, td // 16, n0_step, 0)
    n0_mine = lambda: nb.at[0, rows(c * td, td)]
    push("n0p", lambda: (n0_mine(), n0_mine(), to_c))
    r_mine = lambda: r_own.at[rows(c * td, td)]
    push("rp", lambda: (r_mine(), r_mine(), to_c))
    keep = local("n0k", n0_mine(), n0_buf.at[q, c])
    keep.start()
    keep.wait()
    ag_quarter("n0", n0_buf, n0_src, "y")
    ag_quarter("n0", n0_buf, n0_src, "x")
    ag_quarter("o1", o1_buf, dy_src, "y")
    push_w(0, 1)
    push_w(1, 0)
    push_w(1, 1)
    ag_x("o1", o1_buf, dy_src, 0)
    push("xp", lambda: (x_in, x_part, to_c))
    push("dyp", lambda: (dy_in, o1_buf.at[q, c], to_c))
    push_wc(1)
    local("xc", x_in.at[rows(z * ch, ch)], x_ch).start()
    local("dy_own", dy_in, ob.at[0, rows(c * td, td)]).start()

    @scoped
    def h1_calc():
        def h1_step(i, carry):
            r = rows(i * 16, 16)
            h1 = (x_ch[r, :].astype(F32) + z_sum("d0", i)).astype(BF16)
            h1_ch[r, :] = h1
            h_f = h1.astype(F32)
            n_own[rows(c * td + z * ch + i * 16, 16), :] = (h_f * rinv(h_f) * gain[1:2, :]).astype(BF16)
            return carry

        lax.fori_loop(0, ch // 16, h1_step, 0)

    def h1_done():
        z_got("d0")
        relay_sends_done("d0")
        h1_calc()
        z_gather("n1z", n_own)

    relay_gu(0, 0, 0)
    ag_spread("n0", n0_buf, "y")
    ag_spread("o1", o1_buf, "y")
    relay_gu(0, 0, 1)
    ag_spread("n0", n0_buf, "x")
    relay_gu(0, 1, 0)
    relay_gu(0, 1, 1)
    got("n0p", nb.at[0, rows(co * td, td)])
    got("rp", r_own.at[rows(co * td, td)])
    keep2 = local("n0k2", nb.at[0, rows(co * td, td)], n0_buf.at[q, co])
    keep2.start()
    have_gu(0, 0, 0)
    have_gu(0, 1, 0)
    with jax.named_scope("fwd_tile0"):
        fwd_tile(0, nb.at[0], g_t, 0)
    relay_d(0, 0)
    relay_d(0, 1)
    have_gu(0, 0, 1)
    have_gu(0, 1, 1)
    with jax.named_scope("fwd_tile1"):
        for i in range(1, hh // tile):
            fwd_tile(0, nb.at[0], g_t, i)
    for s in save_ab(q):
        s.start()
    have_d_own(0)
    relay_d(0, 2)
    down_half(0, g_t, x, 0, t2, False)
    relay_d(0, 3)
    ag_spread_got("n0", n0_buf, "y")
    have_d(0)
    down_half(0, g_t, xo, co * td, td, True)
    core_push("d0")
    down_half(0, g_t, xo, c * td, td, True)
    core_sum_send("d0")
    keep2.wait()
    send_done("n0p")
    saves_done(q)
    partner_has("n0", n0_buf, 0)
    stage(n0_buf, block_of(0), nb.at[0], "sn")
    relay_gu(1, 0, 0)
    staged(n0_buf, block_of(0), nb.at[0], "sn")
    f0_other(0, 0)
    z_relay("d0", 0, 0)
    relay_gu(1, 0, 1)
    z_relay("d0", 0, 1)
    ag_spread_got("n0", n0_buf, "x")
    ag_spread_got("o1", o1_buf, "y")
    partner_has("n0", n0_buf, 1)
    stage(n0_buf, block_of(1), nb.at[0], "sn")
    z_relay("d0", 1, 0)
    relay_gu(1, 1, 0)
    z_relay("d0", 1, 1)
    local("xc", x_in.at[rows(z * ch, ch)], x_ch).wait()

    @pl.when(outer == 1)
    def _():
        h1_done()

    relay_gu(1, 1, 1)

    @pl.when(inner == 1)
    def _():
        h1_done()

    local("dyc", dy_in.at[rows(z * ch, ch)], x_ch).start()
    relay_d(1, 0)
    z_take("n1z", n_own, 0)
    z_take("n1z", n_own, 1)
    relay_d(1, 1)
    z_take("n1z", n_own, 2)
    relay_d(1, 2)
    saves_done(block_of(0))
    for h in range(2):
        ag_x("n1", n1_buf, n1_src, h)
    ag_x("o1", o1_buf, dy_src, 1)
    for h in range(2):
        ag_y("n1", n1_buf, n1_src, h)
    got("dyp", o1_buf.at[q, co])
    dy_other = local("dy_other", o1_buf.at[q, co], ob.at[0, rows(co * td, td)])
    dy_other.start()
    z_gathered_partner("n1z", n_own)

    for m in range(2):
        for xb in range(2):
            have_gu(1, m, xb)
    fwd(1, n_own, g_t)
    local("dy_own", dy_in, ob.at[0, rows(c * td, td)]).wait()
    dy_other.wait()
    have_d_own(1)
    bwd_tile(1, ob.at[0], x, a_t, b_t)
    sum_sends_done("d0")
    m_half(1, x, 0, t2, False)
    have_d(1)
    bwd_tile(1, ob.at[0], xo, a_t, b_t)
    g_keep = local("gk", g_t, g_save)
    g_keep.start()
    m_half(1, xo, co * td, td, True)
    core_push("d1")
    m_half(1, xo, c * td, td, True)
    core_sum_send("d1")
    zero_acc()
    g_keep.wait()
    local("dyc", dy_in.at[rows(z * ch, ch)], x_ch).wait()

    @scoped
    def e_calc():
        def e_step(i, dg1):
            r = rows(i * 16, 16)
            m = z_sum("d1", i)
            h_f = h1_ch[r, :].astype(F32)
            r_inv = rinv(h_f)
            xh = h_f * r_inv
            v = m * gain[1:2, :]
            e = x_ch[r, :].astype(F32) + r_inv * (v - xh * jnp.mean(v * xh, axis=-1, keepdims=True))
            o_own[rows(c * td + z * ch + i * 16, 16), :] = e.astype(BF16)
            return dg1 + jnp.sum(m * xh, axis=0, keepdims=True)

        dg[1:2, :] = lax.fori_loop(0, ch // 16, e_step, jnp.zeros((1, d), F32))

    def at_step(k, n):
        return pl.when(k == n)

    def stage_n(buf, block, slot):
        stage(buf, block, nb.at[slot], ("n", slot))

    def staged_n(buf, block, slot):
        staged(buf, block, nb.at[slot], ("n", slot))

    def stage_o(buf, block, slot):
        stage(buf, block, ob.at[slot], ("o", slot))

    def staged_o(buf, block, slot):
        staged(buf, block, ob.at[slot], ("o", slot))

    xl = lambda: [local("xl0", x_in, nb.at[0, rows(c * td, td)]), local("xl1", x_part, nb.at[0, rows(co * td, td)])]

    def n_half(slot):
        return wu.at[1, rows(slot * t2, t2)]

    def n_half_copies(block, slot):
        return [local(("nh", slot, core), n0_buf.at[block, core, :, cols(2 * x * rb, 2 * rb)], wu.at[1, rows(slot * t2 + core * td, td)]) for core in range(2)]

    def load_n_half(block, slot):
        for s in n_half_copies(block, slot):
            s.start()

    own_g = nb.at[1, :, pl.ds(0, hh)]

    def e_done():
        z_got("d1")
        relay_sends_done("d1")
        e_calc()
        z_gather("o0z", o_own)
        for dev in others:
            pl.semaphore_signal(credit, inc=1, device_id=at_z(dev), device_id_type=MESH)

    def l1_step(k, carry):
        slot = 1 - (k + 3) // 4

        @pl.when(k > 0)
        def _():
            @at_step(k, 1)
            def _():
                partner_has("o1", o1_buf, 0)
                stage_o(o1_buf, block_of(0), 0)

            @pl.when(k * inner == 2)
            def _():
                e_done()

            @at_step(k, 2)
            def _():
                ag_got_x("o1", o1_buf, 1, cut_o)
                ag_dy("n0", n0_buf, cut_n)

            staged_n(n1_buf, block_of(k - 1), 0)
            fwd(1, nb.at[0], None)

            @pl.when(k > 1)
            def _():
                partner_has("o1", o1_buf, k - 1)
                stage_o(o1_buf, block_of(k - 1), 0)

            @at_step(k, 1)
            def _():
                z_relay("d1", 1, 0)
                ag_got_x("n1", n1_buf, 1, half)

            @at_step(k, 3)
            def _():
                for i in range(3):
                    z_take("o0z", o_own, i)
                for h in range(2):
                    ag_x("o0", o0_buf, o0_src, h)
                    ag_y("o0", o0_buf, o0_src, h)
                z_relay("d2", 0, 0)

            staged_o(o1_buf, block_of(k - 1), 0)
            bwd_hidden(1, ob.at[0], a_t, b_t)

            @at_step(k, 1)
            def _():
                z_relay("d1", 1, 1)

                @pl.when(outer == 1)
                def _():
                    e_done()

                partner_has("n1", n1_buf, 1)

            @at_step(k, 2)
            def _():
                local("gl", g_save, own_g).wait()
                sum_sends_done("d1")
                down_rows(1, own_g, co)
                core_push("d2")
                ag_got_dx("n1", n1_buf, half)
                ag_got_dy("n1", n1_buf, 1, half)
                down_rows(1, own_g, c)
                core_back_start("d2")

            @at_step(k, 1)
            def _():
                for key in [("n1z", "zs", 0)] + [("n1z", "s", i) for i in range(4)] + [("n1", axis, h) for axis in "xy" for h in range(2)]:
                    send_done(key)
                passed_done("n1z")
                local("gl", g_save, own_g).start()

            @at_step(k, 3)
            def _():
                z_relay("d2", 0, 1)
                for key in [k1 for k1 in sent if k1[0] in ("wy", "wdy") and k1[1] == 1]:
                    send_done(key)
                for i in range(3):
                    for s in load_ab(block_of(i - 1) if i else q, i):
                        s.start()
                    load_n_half(block_of(i - 1) if i else q, i)

        weight_grads(nb.at[slot], 2 * x * rb, ob.at[0], None)

        @at_step(k, 1)
        def _():
            stage_n(n1_buf, block_of(1), 0)

        @at_step(k, 2)
        def _():
            ag_got_dx("o1", o1_buf, cut_o)
            for h in range(2):
                ag_got_dy("o1", o1_buf, h, cut_o)
            partner_has("n1", n1_buf, 2)
            stage_n(n1_buf, block_of(2), 0)
            pl.semaphore_wait(credit, 3)
            core_sum_send("d2")

        @at_step(k, 0)
        def _():
            staged(n0_buf, block_of(1), nb.at[0], "sn")
            f0_other(1, 0)
            ag_got_x("o1", o1_buf, 0, cut_o)
            ag_got_x("n1", n1_buf, 0, half)
            z_relay("d1", 0, 0)
            ag_got_y("n1", n1_buf, 0)
            ag_dx("o1", o1_buf, cut_o)
            ag_dx("n0", n0_buf, cut_n)
            z_relay("d1", 0, 1)
            ag_got_y("n1", n1_buf, 1)
            partner_has("n1", n1_buf, 0)
            stage_n(n1_buf, block_of(0), 0)
            saves_done(block_of(1))

        return carry

    lax.fori_loop(0, 4, l1_step, 0)
    got("xp", x_part)
    for s in xl():
        s.start()
    for s in load_ab(q, 0):
        s.wait()
    z_gathered_partner("o0z", o_own)
    grads_push(1)
    grads_out(1)

    def gz_id(zi):
        base = sid(("gz", 0))
        for i in range(4):
            assert sid(("gz", i)) == base + i
        return base + zi

    def y_rows(zi):
        return y_out.at[rows(zi * ch, ch)]

    gz_id(0)
    zg_id("y", 0)

    @scoped
    def dgain0():
        def dg_step(i, carry):
            w = cols(i * tile, tile)
            m = mm(a_t[...], wg[0, rows(i * tile, tile)], 1, 1) + mm(b_t[...], wu[0, rows(i * tile, tile)], 1, 1)
            xh = nb[0, :, w].astype(F32) * r_own[:, 0:1]
            dg[0:1, w] = jnp.sum(m * xh, axis=0, keepdims=True)
            return carry

        lax.fori_loop(0, d // tile, dg_step, 0)

    def y_done():
        z_got("d2")

        def y_step(i, carry):
            r = rows(i * 16, 16)
            x_ch[r, :] = (h1_ch[r, :].astype(F32) + z_sum("d2", i)).astype(BF16)
            return carry

        lax.fori_loop(0, ch // 16, y_step, 0)
        local("yk", x_ch, y_rows(z)).start()
        z_push("y", lambda zi: (x_ch, y_rows(zi)), z)

    def l0_step(k, carry):
        oslot = (k + 1) % 2

        @pl.when(k > 0)
        def _():
            staged_o_any(k)

        bwd_hidden(0, ob.at[oslot], a_kept(k), b_kept(k))

        @at_step(k, 0)
        def _():
            for s in xl():
                s.wait()
            ag_got_dx("n0", n0_buf, cut_n)
            ag_got_dy_whole("n0", n0_buf, cut_n)
            z_relay("d2", 1, 0)
            dgain0()
            dg_z[z] = dg[...]
            for i in range(3):
                push(("gs", i), lambda i=i: (dg_z.at[z], dg_z.at[z], at_z(others[i])), gz_id(z))
            z_relay("d2", 1, 1)
            partner_has("n0", n0_buf, 2)
            stage_n(n0_buf, block_of(2), 0)
            load_n_half(block_of(2), 3)
            ag_got_y("o0", o0_buf, 0)
            grads_out_done(1)
            zero_acc()
            for i in range(4):
                for s in n_half_copies(block_of(i - 1) if i else q, i):
                    s.wait()
            for i in range(1, 3):
                for s in load_ab(block_of(i - 1), i):
                    s.wait()

        @at_step(k, 1)
        def _():
            @pl.when(inner == 1)
            def _():
                y_done()

            partner_has("o0", o0_buf, 1)
            for key in [("o0z", "zs", i) for i in range(3)] + [("o0z", "s", i) for i in range(4)] + [("o0", axis, h) for axis in "xy" for h in range(2)]:
                send_done(key)
            stage_o(o0_buf, block_of(1), 1)
            for i in range(3):
                with jax.named_scope("got_gz"):
                    got(gz_id(others[i]), dg_z.at[others[i]])
                send_done(("gs", i))
            dg[...] = dg_z[0] + dg_z[1] + dg_z[2] + dg_z[3]
            push("gc", lambda: (dg, dg_core, to_c))

        @at_step(k, 2)
        def _():
            got("gc", dg_core)
            copy_of("gc", "gc", dg, dg_core, to_c).wait_send()
            dg[...] = dg[...] + dg_core[...]
            push("gx", lambda: (dg, dg_x, to_x))
            ag_got_dx("o0", o0_buf, half)
            ag_got_dy("o0", o0_buf, 1, half)
            partner_has("o0", o0_buf, 2)
            stage_o(o0_buf, block_of(2), 0)

        @at_step(k, 3)
        def _():
            got("gx", dg_x)
            copy_of("gx", "gx", dg, dg_x, to_x).wait_send()
            dg[...] = dg[...] + dg_x[...]
            push("gy", lambda: (dg, dg_y, to_y))

        def between():
            @at_step(k, 3)
            def _():
                grads_push(0)

        weight_grads(n_half(k), 0, ob.at[oslot], between)

        @at_step(k, 0)
        def _():
            staged_n(n0_buf, block_of(2), 0)
            with jax.named_scope("f0_last"):
                fwd(0, nb.at[0], None, a_kept(3), b_kept(3))

            @pl.when(outer == 1)
            def _():
                y_done()

            ag_got_x("o0", o0_buf, 0, half)
            ag_got_y("o0", o0_buf, 1)
            ag_got_x("o0", o0_buf, 1, half)
            partner_has("o0", o0_buf, 0)
            stage_o(o0_buf, block_of(0), 0)

        return carry

    def staged_o_any(k):
        for n, slot in ((1, 0), (2, 1), (3, 0)):
            @at_step(k, n)
            def _(n=n, slot=slot):
                staged_o(o0_buf, block_of(n - 1), slot)

    lax.fori_loop(0, 4, l0_step, 0)
    grads_out(0)
    for key in ("gc", "gx", "gy"):
        sent.pop(key)
    got("gy", dg_y)
    copy_of("gy", "gy", dg, dg_y, to_y).wait_send()
    dgain_out[...] = dg[...] + dg_y[...]
    for i in range(3):
        with jax.named_scope("got_y"):
            z_pass("y", lambda zi: (x_ch, y_rows(zi)), i)
    local("yk", x_ch, y_rows(z)).wait()
    grads_out_done(0)
    for key in list(sent):
        send_done(key)
    for s in "BC":
        for h in range(2):
            copy_of(("d2", s, h), ("d2", s, h), mine(0, h), slot("d2", 0, h), at_z(pair)).wait_send()

    assert not passed


def make_call(td, d, rb, hs):
    fb = hs // 4
    hh, t2, ch = 2 * fb, 2 * td, td // 4
    shape = jax.ShapeDtypeStruct
    hbm = pl.BlockSpec(memory_space=pl.ANY)
    vmem = pl.BlockSpec(memory_space=pltpu.VMEM)
    block = shape((4, 2, td, d), BF16)
    outs = [
        shape((td, d), BF16), shape((2, rb, hs), F32), shape((2, rb, hs), F32), shape((2, fb, d), F32), shape((2, d), F32),
        block, block, block, block, shape((4, t2, hh), BF16), shape((4, t2, hh), BF16), shape((td, d), BF16), shape((t2, hh), BF16), shape((td, d), F32),
    ]
    scratch = [
        pltpu.VMEM((2, d, hh), BF16), pltpu.VMEM((2, d, hh), BF16), pltpu.VMEM((2, hh, d), BF16),
        pltpu.VMEM((2 * rb, hh), F32), pltpu.VMEM((2 * rb, hh), F32), pltpu.VMEM((fb, d), F32),
        pltpu.VMEM((2, t2, d), BF16), pltpu.VMEM((2, t2, d), BF16),
        pltpu.VMEM((t2, hh), BF16), pltpu.VMEM((t2, hh), BF16), pltpu.VMEM((t2, hh), BF16),
        pltpu.VMEM((t2, d), F32), pltpu.VMEM((4, ch, d), F32),
        pltpu.VMEM((ch, d), BF16), pltpu.VMEM((ch, d), BF16),
        pltpu.VMEM((t2, 128), F32),
        pltpu.VMEM((2, d), F32), pltpu.VMEM((2, d), F32), pltpu.VMEM((2, d), F32), pltpu.VMEM((2, d), F32), pltpu.VMEM((4, 2, d), F32),
        pltpu.SemaphoreType.DMA((NSEM,)), pltpu.SemaphoreType.DMA((NSEM,)), pltpu.SemaphoreType.DMA((NLOC,)), pltpu.SemaphoreType.REGULAR,
    ]
    return pl.pallas_call(
        kernel,
        out_shape=outs,
        in_specs=[hbm] * 5 + [vmem],
        out_specs=[hbm] * 4 + [vmem] + [hbm] * 9,
        scratch_shapes=scratch,
        compiler_params=pltpu.CompilerParams(collective_id=0, has_side_effects=True, vmem_limit_bytes=67043328),
    )


def solution(mesh):
    tok_spec = P(("replica", "fsdp"), None)
    wide_spec = P(None, "fsdp", "tensor")
    down_spec = P(None, ("tensor", "fsdp"), None)
    gain_spec = P(None, None)

    def device_fn(x_loc, dy_loc, w_gate, w_up, w_down, norm_gain):
        call = make_call(x_loc.shape[0], x_loc.shape[1], w_gate.shape[1], w_gate.shape[2])
        return tuple(call(x_loc, dy_loc, w_gate, w_up, w_down, norm_gain)[:5])

    return jax.shard_map(device_fn, mesh=mesh, in_specs=(tok_spec, tok_spec, wide_spec, wide_spec, down_spec, gain_spec), out_specs=(tok_spec, wide_spec, wide_spec, down_spec, gain_spec), check_vma=False)
```

time: 343 us -> 315 us (0.918)
  Pallas kernels: 319 us -> 292 us
    pallas_call x1, Pallas kernels: 319 us -> 292 us  [device_fn(): return tuple(call(x_loc, dy_loc, w_gate, w_up, w_down, norm_gain)[:5])]
where the time goes in v3:
time: 315 us; the launch traced here: 314 us
  Pallas kernels  292 us (93%)
  local copies, waits for them, and re-layouts  20.8 us (7%)
    pallas_call x1, Pallas kernels, device_fn(): return tuple(call(x_loc, dy_loc, w_gate, w_up, w_down, norm_gain)[:5])  292 us
    unnamed x13, local copies, waits for them, and re-layouts  20.8 us

profile of v3, /device:TPU:0, one launch (start us, length us, event | category | flops | bytes accessed | tf_op | source)
XLA Modules:
  0.0 313.6 jit_solution(7706512829470015473)
XLA Ops:
  0.6 292.2 %shard_map.101 = (bf16[256,2048]{1,0:T(8,128)(2,1)}, f32[2,512,2048]{2,1,0:T(8,128)}, f32[2,512,2048]{2,1,0:T(8,128)}, f32[2,512,2048]{2,1,0:T(8,128)}, f32[2,20...) custom-call(bf16[256,2048]{1,0:T(8,128)(2,1)} %x_in.1, ...), custom_call_target="tpu_custom_call" | custom-call | tf_op jit(solution)/shard_map/pallas_call | solution.py:1103
  292.8 2.3 copy.16
  295.1 0.0 copy-start
  295.1 0.0 slice-start
  295.1 8.9 %copy.17 = f32[2,512,2048]{2,1,0:T(8,128)} copy(f32[2,512,2048]{2,1,0:T(8,128)} %get-tuple-element.21) | data formatting | bytes 16777216
  304.0 0.0 copy-done
  304.0 0.0 slice-start.1
  304.0 4.3 %copy.18 = f32[2,512,2048]{2,1,0:T(8,128)} copy(f32[2,512,2048]{2,1,0:T(8,128)S(1)} %copy-done) | data formatting | bytes 16777216
  308.3 0.0 slice-done
  308.3 1.3 slice-done.1
  309.6 0.0 copy-start.1
  309.6 3.4 %copy.19 = f32[2,512,2048]{2,1,0:T(8,128)} copy(f32[2,512,2048]{2,1,0:T(8,128)S(1)} %bitcast.1) | data formatting | bytes 16777216
  313.0 0.0 copy-done.1
  313.0 0.6 copy.20
  (1 shorter events, 0.0 us)
Async XLA Ops:
  295.1 8.9 %copy-start = (f32[2,512,2048]{2,1,0:T(8,128)S(1)}, f32[2,512,2048]{2,1,0:T(8,128)}, u32[]{:S(2)}) copy-start(f32[2,512,2048]{2,1,0:T(8,128)} %get-tuple-element.22) | copy-start | bytes 25165828
  295.1 13.2 %slice-start = ((s8[8388608]{0:T(1024)(128)(4,1)}), s8[4194304]{0:T(1024)(128)(4,1)S(1)}, s32[]{:S(2)}) async-start(s8[8388608]{0:T(1024)(128)(4,1)} %bitcast), calls=%async_computation | async-start | bytes 8388608
  304.0 5.6 %slice-start.1 = ((s8[8388608]{0:T(1024)(128)(4,1)}), s8[4194304]{0:T(1024)(128)(4,1)S(1)}, s32[]{:S(2)}) async-start(s8[8388608]{0:T(1024)(128)(4,1)} %bitcast), calls=%async_computation.1 | async-start | bytes 8388608
  309.6 3.4 %copy-start.1 = (f32[2,2048]{1,0:T(2,128)S(1)}, f32[2,2048]{1,0:T(2,128)}, u32[]{:S(2)}) copy-start(f32[2,2048]{1,0:T(2,128)} %get-tuple-element.24) | copy-start | bytes 49156

commit v4 on v3

--- a/solution.py
+++ b/solution.py
@@ -8,8 +8,11 @@
 F32 = jnp.float32
 BF16 = jnp.bfloat16
 MESH = pl.DeviceIdType.MESH
-NSEM = 340
-NLOC = 96
+NSEND = 174
+NRECV = 176
+NLOC = 55
+VLIM = 67043328 - 16 * 2**20 - 2**17
+VLIM2 = 14 * 2**20
 
 
 def mm(lhs, rhs, ldim, rdim):
@@ -18,8 +21,8 @@
 
 def kernel(
     x_in, dy_in, wg_in, wu_in, wd_in, gain,
-    y_out, dwg_out, dwu_out, dwd_out, dgain_out, n0_buf, n1_buf, o1_buf, o0_buf, a_save, b_save, x_part, g_save, core_hbm,
-    wg, wu, wd, acc_g, acc_u, acc_d, nb, ob, a_t, b_t, g_t, part, from_z,
+    y_out, dwg1, dwu1, dwd1, dgain_out, acc_g, acc_u, acc_d, part, n0_buf, n1_buf, o1_buf, o0_buf, a_save, b_save, x_part, g_save, core_hbm,
+    wg, wu, wd, nb, ob, a_t, b_t, g_t, from_z,
     x_ch, h1_ch, r_own, dg, dg_core, dg_x, dg_y, dg_z, ssem, rsem, lsem, credit,
 ):
     td, d = x_in.shape
@@ -62,21 +65,23 @@
     def cols(start, size):
         return pl.ds(start if isinstance(start, int) else pl.multiple_of(start, 128), size)
 
-    ids, lids, sent, passed = {}, {}, {}, {}
+    ids, sids, lids, sent, passed = {}, {}, {}, {}, {}
+
+    def numbered(table, key, limit):
+        i = table.setdefault(key, len(table))
+        assert i < limit, i
+        return i
 
     def sid(key):
-        i = ids.setdefault(key, len(ids))
-        assert i < NSEM, i
-        return i
+        return numbered(ids, key, NRECV)
 
     def name_of(key):
         return key if isinstance(key, str) else "_".join(map(str, key))
 
     def copy_of(skey, rkey, src, dst, dev):
-        return pltpu.make_async_remote_copy(
-            src_ref=src, dst_ref=dst, send_sem=ssem.at[sid(skey)], recv_sem=rsem.at[rkey if not isinstance(rkey, (str, tuple)) else sid(rkey)],
-            device_id=dev, device_id_type=MESH,
-        )
+        send = 0 if skey is None else numbered(sids, skey, NSEND)
+        recv = sid(rkey) if isinstance(rkey, (str, tuple)) else rkey
+        return pltpu.make_async_remote_copy(src_ref=src, dst_ref=dst, send_sem=ssem.at[send], recv_sem=rsem.at[recv], device_id=dev, device_id_type=MESH)
 
     def push(key, make, rkey=None):
         copy_of(key, key if rkey is None else rkey, *make()).start()
@@ -84,14 +89,19 @@
 
     def got(key, dst):
         with jax.named_scope("got_" + (name_of(key) if isinstance(key, (str, tuple)) else "dyn")):
-            copy_of("none", key, dst, dst, to_c).wait_recv()
+            copy_of(None, key, dst, dst, to_c).wait_recv()
 
     def send_done(key):
-        copy_of(key, key, *sent.pop(key)()).wait_send()
+        copy_of(key, 0, *sent.pop(key)()).wait_send()
+
+    def flush(heads, layer=None):
+        for key in list(sent):
+            parts = (key,) if isinstance(key, str) else key
+            if parts[0] in heads and (layer is None or parts[0][0] != "w" or parts[1] == layer):
+                send_done(key)
 
     def local(key, src, dst):
-        i = lids.setdefault(key, len(lids))
-        assert i < NLOC, i
+        i = numbered(lids, key, NLOC)
         return pltpu.make_async_copy(src, dst, lsem.at[i])
 
     def scoped(fn):
@@ -248,9 +258,9 @@
     for a in ("n0", "o1", "n1", "o0"):
         for j in range(3):
             sid((a, "p", j))
-        for axis in "xy":
-            for i in range(4):
-                sid((a, axis, "zb", i))
+    for a, axis in (("n0", "y"), ("n0", "x"), ("o1", "y")):
+        for i in range(4):
+            sid((a, axis, "zb", i))
 
     def fwd_tile(l, n_ref, g_ref, i, a_ref=None, b_ref=None):
         w = cols(i * tile, tile)
@@ -442,7 +452,7 @@
         def _():
             for s in "BC":
                 for h in range(2):
-                    copy_of((key, s, h), (key, s, h), mine(0, h), slot(key, 0, h), at_z(pair)).wait_send()
+                    copy_of((key, s, h), 0, mine(0, h), slot(key, 0, h), at_z(pair)).wait_send()
 
     def sum_sends_done(key):
         for part_key in [(key, "c", k) for k in range(4)] + [(key, "A", h) for h in range(2)]:
@@ -452,7 +462,7 @@
         def _():
             for s in "BC":
                 for h in range(2):
-                    copy_of((key, s, h), (key, s, h), mine(0, h), slot(key, 0, h), at_z(pair)).wait_send()
+                    copy_of((key, s, h), 0, mine(0, h), slot(key, 0, h), at_z(pair)).wait_send()
 
     def quarter(ref, core, zi):
         return ref.at[rows(core * td + zi * ch, ch)]
@@ -493,7 +503,7 @@
         def _():
             for key in [k1 for k1 in passed if k1[0] == which]:
                 ref = passed.pop(key)
-                copy_of(key, key, ref(), ref(), to_c).wait_send()
+                copy_of(key, 0, ref(), ref(), to_c).wait_send()
 
     def z_gather(key, ref):
         z_push(key, lambda zi: (quarter(ref, c, zi), quarter(ref, c, zi)), z)
@@ -538,25 +548,35 @@
     def load_ab(block, k):
         return (local(("la", k), a_save.at[block], a_kept(k)), local(("lb", k), b_save.at[block], b_kept(k)))
 
+    def grad_piece(i, xb, core):
+        return (acc_g, acc_u)[i].at[rows(core * rb, rb), cols(xb * fb, fb)]
+
+    def grad_land(l, i, xb, core):
+        if l == 1:
+            return (dwg1, dwu1)[i].at[:, cols((2 * xb + core) * fb, fb)]
+        return part.at[:, cols(i * hh + xb * fb, fb)]
+
     def grads_push(l):
-        for i, (acc, out) in enumerate(((acc_g, dwg_out), (acc_u, dwu_out))):
+        for i in range(2):
             for xb in range(2):
-                push(("q", l, i, xb), lambda acc=acc, out=out, xb=xb: (acc.at[rows(co * rb, rb), cols(xb * fb, fb)], out.at[l, :, cols((2 * xb + c) * fb, fb)], to_c))
-
-    def grads_out(l):
-        for i, (acc, out) in enumerate(((acc_g, dwg_out), (acc_u, dwu_out))):
+                push(("q", l, i, xb), lambda i=i, xb=xb: (grad_piece(i, xb, co), grad_land(l, i, xb, c), to_c))
+
+    def grads_out():
+        for i in range(2):
             for xb in range(2):
-                local(("qo", l, i, xb), acc.at[rows(c * rb, rb), cols(xb * fb, fb)], out.at[l, :, cols((2 * xb + c) * fb, fb)]).start()
-        local(("qd", l), acc_d, dwd_out.at[l]).start()
+                local(("qo", i, xb), grad_piece(i, xb, c), grad_land(1, i, xb, c)).start()
+        local("qd", acc_d, dwd1).start()
 
     @scoped
     def grads_out_done(l):
-        for i, (acc, out) in enumerate(((acc_g, dwg_out), (acc_u, dwu_out))):
+        for i in range(2):
             for xb in range(2):
-                local(("qo", l, i, xb), acc.at[rows(c * rb, rb), cols(xb * fb, fb)], out.at[l, :, cols((2 * xb + c) * fb, fb)]).wait()
+                if l == 1:
+                    local(("qo", i, xb), grad_piece(i, xb, c), grad_land(1, i, xb, c)).wait()
                 send_done(("q", l, i, xb))
-                got(("q", l, i, xb), out.at[l, :, cols((2 * xb + co) * fb, fb)])
-        local(("qd", l), acc_d, dwd_out.at[l]).wait()
+                got(("q", l, i, xb), grad_land(l, i, xb, co))
+        if l == 1:
+            local("qd", acc_d, dwd1).wait()
 
     barrier = pltpu.get_barrier_semaphore()
     for dev in (to_c, to_x, {"fsdp": 2 * xo + co}, to_y, at_z((z + 1) % 4), at_z((z + 2) % 4), at_z((z + 3) % 4)):
@@ -570,7 +590,7 @@
     n0_src = lambda: n0_buf.at[q, c]
     n1_src = lambda: n_own.at[rows(c * td, td)]
     o0_src = lambda: o_own.at[rows(c * td, td)]
-    cut_n, cut_o = ch, ch
+    cut_n, cut_o = ch, half
 
     push_w(0, 0)
     push_wc(0)
@@ -687,6 +707,7 @@
         h1_done()
 
     local("dyc", dy_in.at[rows(z * ch, ch)], x_ch).start()
+    flush(("wx", "wdx", "wc", "wy", "wdy", "xp", "dyp", "rp"), 0)
     relay_d(1, 0)
     z_take("n1z", n_own, 0)
     z_take("n1z", n_own, 1)
@@ -788,27 +809,32 @@
                 partner_has("o1", o1_buf, 0)
                 stage_o(o1_buf, block_of(0), 0)
 
+            staged_n(n1_buf, block_of(k - 1), 0)
+            with jax.named_scope("fwd_a"):
+                fwd_tile(1, nb.at[0], None, 0)
+
+            @at_step(k, 2)
+            def _():
+                ag_got_x("o1", o1_buf, 1, cut_o)
+
+            @at_step(k, 3)
+            def _():
+                ag_got_dx("o1", o1_buf, cut_o)
+                for h in range(2):
+                    ag_got_dy("o1", o1_buf, h, cut_o)
+
+            with jax.named_scope("fwd_b"):
+                for i in range(1, hh // tile):
+                    fwd_tile(1, nb.at[0], None, i)
+
             @pl.when(k * inner == 2)
             def _():
                 e_done()
-
-            @at_step(k, 2)
-            def _():
-                ag_got_x("o1", o1_buf, 1, cut_o)
-                ag_dy("n0", n0_buf, cut_n)
-
-            staged_n(n1_buf, block_of(k - 1), 0)
-            fwd(1, nb.at[0], None)
 
             @pl.when(k > 1)
             def _():
                 partner_has("o1", o1_buf, k - 1)
                 stage_o(o1_buf, block_of(k - 1), 0)
-
-            @at_step(k, 1)
-            def _():
-                z_relay("d1", 1, 0)
-                ag_got_x("n1", n1_buf, 1, half)
 
             @at_step(k, 3)
             def _():
@@ -817,7 +843,11 @@
                 for h in range(2):
                     ag_x("o0", o0_buf, o0_src, h)
                     ag_y("o0", o0_buf, o0_src, h)
-                z_relay("d2", 0, 0)
+
+            @at_step(k, 1)
+            def _():
+                z_relay("d1", 1, 0)
+                ag_got_x("n1", n1_buf, 1, half)
 
             staged_o(o1_buf, block_of(k - 1), 0)
             bwd_hidden(1, ob.at[0], a_t, b_t)
@@ -852,7 +882,7 @@
 
             @at_step(k, 3)
             def _():
-                z_relay("d2", 0, 1)
+                z_relay("d2", 0, 0)
                 for key in [k1 for k1 in sent if k1[0] in ("wy", "wdy") and k1[1] == 1]:
                     send_done(key)
                 for i in range(3):
@@ -868,9 +898,6 @@
 
         @at_step(k, 2)
         def _():
-            ag_got_dx("o1", o1_buf, cut_o)
-            for h in range(2):
-                ag_got_dy("o1", o1_buf, h, cut_o)
             partner_has("n1", n1_buf, 2)
             stage_n(n1_buf, block_of(2), 0)
             pl.semaphore_wait(credit, 3)
@@ -886,6 +913,7 @@
             ag_got_y("n1", n1_buf, 0)
             ag_dx("o1", o1_buf, cut_o)
             ag_dx("n0", n0_buf, cut_n)
+            ag_dy("n0", n0_buf, cut_n)
             z_relay("d1", 0, 1)
             ag_got_y("n1", n1_buf, 1)
             partner_has("n1", n1_buf, 0)
@@ -901,8 +929,9 @@
     for s in load_ab(q, 0):
         s.wait()
     z_gathered_partner("o0z", o_own)
+    z_relay("d2", 0, 1)
     grads_push(1)
-    grads_out(1)
+    grads_out()
 
     def gz_id(zi):
         base = sid(("gz", 0))
@@ -979,6 +1008,10 @@
             def _():
                 y_done()
 
+            for h in range(2):
+                send_done(("d2", "A", h))
+                for s in "BC":
+                    copy_of(("d2", s, h), 0, mine(0, h), slot("d2", 0, h), at_z(pair)).wait_send()
             partner_has("o0", o0_buf, 1)
             for key in [("o0z", "zs", i) for i in range(3)] + [("o0z", "s", i) for i in range(4)] + [("o0", axis, h) for axis in "xy" for h in range(2)]:
                 send_done(key)
@@ -993,7 +1026,7 @@
         @at_step(k, 2)
         def _():
             got("gc", dg_core)
-            copy_of("gc", "gc", dg, dg_core, to_c).wait_send()
+            copy_of("gc", 0, dg, dg_core, to_c).wait_send()
             dg[...] = dg[...] + dg_core[...]
             push("gx", lambda: (dg, dg_x, to_x))
             ag_got_dx("o0", o0_buf, half)
@@ -1004,7 +1037,7 @@
         @at_step(k, 3)
         def _():
             got("gx", dg_x)
-            copy_of("gx", "gx", dg, dg_x, to_x).wait_send()
+            copy_of("gx", 0, dg, dg_x, to_x).wait_send()
             dg[...] = dg[...] + dg_x[...]
             push("gy", lambda: (dg, dg_y, to_y))
 
@@ -1028,6 +1061,7 @@
             ag_got_x("o0", o0_buf, 0, half)
             ag_got_y("o0", o0_buf, 1)
             ag_got_x("o0", o0_buf, 1, half)
+            flush(("wx", "wdx", "wdx_last", "wc", "n0", "o1", "n1"))
             partner_has("o0", o0_buf, 0)
             stage_o(o0_buf, block_of(0), 0)
 
@@ -1040,11 +1074,10 @@
                 staged_o(o0_buf, block_of(n - 1), slot)
 
     lax.fori_loop(0, 4, l0_step, 0)
-    grads_out(0)
     for key in ("gc", "gx", "gy"):
         sent.pop(key)
     got("gy", dg_y)
-    copy_of("gy", "gy", dg, dg_y, to_y).wait_send()
+    copy_of("gy", 0, dg, dg_y, to_y).wait_send()
     dgain_out[...] = dg[...] + dg_y[...]
     for i in range(3):
         with jax.named_scope("got_y"):
@@ -1053,11 +1086,39 @@
     grads_out_done(0)
     for key in list(sent):
         send_done(key)
-    for s in "BC":
-        for h in range(2):
-            copy_of(("d2", s, h), ("d2", s, h), mine(0, h), slot("d2", 0, h), at_z(pair)).wait_send()
-
     assert not passed
+
+
+def finish(acc_g, acc_u, acc_d, other, g1, u1, d1, y_in, g_out, u_out, d_out, y_out, buf, ybuf, sem_in, sem_out):
+    rb, hh = other.shape[0], acc_g.shape[1]
+    fb = hh // 2
+    f = lax.axis_index("fsdp")
+    c = f % 2
+    ins = [pltpu.make_async_copy(src, buf.at[i], sem_in.at[i]) for i, src in enumerate((g1, u1, d1))]
+    ins.append(pltpu.make_async_copy(y_in, ybuf, sem_in.at[3]))
+    for copy in ins:
+        copy.start()
+    outs = []
+
+    def out(src, dst):
+        copy = pltpu.make_async_copy(src, dst, sem_out.at[len(outs)])
+        copy.start()
+        outs.append(copy)
+
+    for i, (acc, dst) in enumerate(((acc_g, g_out), (acc_u, u_out))):
+        for xb in range(2):
+            own = pl.ds(pl.multiple_of((2 * xb + c) * fb, 128), fb)
+            out(acc.at[pl.ds(pl.multiple_of(c * rb, rb), rb), pl.ds(xb * fb, fb)], dst.at[0, :, own])
+            theirs = pl.ds(pl.multiple_of((2 * xb + 1 - c) * fb, 128), fb)
+            out(other.at[:, pl.ds(i * hh + xb * fb, fb)], dst.at[0, :, theirs])
+    out(acc_d, d_out.at[0])
+    for i, dst in enumerate((g_out, u_out, d_out)):
+        ins[i].wait()
+        out(buf.at[i], dst.at[1])
+    ins[3].wait()
+    out(ybuf, y_out)
+    for copy in outs:
+        copy.wait()
 
 
 def make_call(td, d, rb, hs):
@@ -1068,28 +1129,45 @@
     vmem = pl.BlockSpec(memory_space=pltpu.VMEM)
     block = shape((4, 2, td, d), BF16)
     outs = [
-        shape((td, d), BF16), shape((2, rb, hs), F32), shape((2, rb, hs), F32), shape((2, fb, d), F32), shape((2, d), F32),
+        shape((td, d), BF16), shape((rb, hs), F32), shape((rb, hs), F32), shape((fb, d), F32), shape((2, d), F32),
+        pltpu.VMEM((2 * rb, hh), F32), pltpu.VMEM((2 * rb, hh), F32), pltpu.VMEM((fb, d), F32), pltpu.VMEM((t2, d), F32),
         block, block, block, block, shape((4, t2, hh), BF16), shape((4, t2, hh), BF16), shape((td, d), BF16), shape((t2, hh), BF16), shape((td, d), F32),
     ]
     scratch = [
         pltpu.VMEM((2, d, hh), BF16), pltpu.VMEM((2, d, hh), BF16), pltpu.VMEM((2, hh, d), BF16),
-        pltpu.VMEM((2 * rb, hh), F32), pltpu.VMEM((2 * rb, hh), F32), pltpu.VMEM((fb, d), F32),
         pltpu.VMEM((2, t2, d), BF16), pltpu.VMEM((2, t2, d), BF16),
         pltpu.VMEM((t2, hh), BF16), pltpu.VMEM((t2, hh), BF16), pltpu.VMEM((t2, hh), BF16),
-        pltpu.VMEM((t2, d), F32), pltpu.VMEM((4, ch, d), F32),
+        pltpu.VMEM((4, ch, d), F32),
         pltpu.VMEM((ch, d), BF16), pltpu.VMEM((ch, d), BF16),
         pltpu.VMEM((t2, 128), F32),
         pltpu.VMEM((2, d), F32), pltpu.VMEM((2, d), F32), pltpu.VMEM((2, d), F32), pltpu.VMEM((2, d), F32), pltpu.VMEM((4, 2, d), F32),
-        pltpu.SemaphoreType.DMA((NSEM,)), pltpu.SemaphoreType.DMA((NSEM,)), pltpu.SemaphoreType.DMA((NLOC,)), pltpu.SemaphoreType.REGULAR,
+        pltpu.SemaphoreType.DMA((NSEND,)), pltpu.SemaphoreType.DMA((NRECV,)), pltpu.SemaphoreType.DMA((NLOC,)), pltpu.SemaphoreType.REGULAR,
     ]
-    return pl.pallas_call(
+    step = pl.pallas_call(
         kernel,
         out_shape=outs,
         in_specs=[hbm] * 5 + [vmem],
-        out_specs=[hbm] * 4 + [vmem] + [hbm] * 9,
+        out_specs=[hbm] * 4 + [vmem] * 5 + [hbm] * 9,
         scratch_shapes=scratch,
-        compiler_params=pltpu.CompilerParams(collective_id=0, has_side_effects=True, vmem_limit_bytes=67043328),
+        compiler_params=pltpu.CompilerParams(collective_id=0, has_side_effects=True, vmem_limit_bytes=VLIM),
     )
+    end = pl.pallas_call(
+        finish,
+        out_shape=[shape((2, rb, hs), F32), shape((2, rb, hs), F32), shape((2, fb, d), F32), shape((td, d), BF16)],
+        in_specs=[vmem] * 4 + [hbm] * 4,
+        out_specs=[hbm] * 4,
+        scratch_shapes=[pltpu.VMEM((3, rb, hs), F32), pltpu.VMEM((td, d), BF16), pltpu.SemaphoreType.DMA((4,)), pltpu.SemaphoreType.DMA((13,))],
+        compiler_params=pltpu.CompilerParams(vmem_limit_bytes=VLIM2),
+    )
+
+    def call(*args):
+        y, g1, u1, d1, dgain, acc_g, acc_u, acc_d, other = step(*args)[:9]
+        kept = [pltpu.with_memory_space_constraint(v, pltpu.VMEM) for v in (acc_g, acc_u, acc_d, other)]
+        stored = [pltpu.with_memory_space_constraint(v, pltpu.HBM) for v in (g1, u1, d1, y)]
+        g, u, dd, y = end(*kept, *stored)
+        return y, g, u, dd, dgain
+
+    return call
 
 
 def solution(mesh):
@@ -1100,6 +1178,6 @@
 
     def device_fn(x_loc, dy_loc, w_gate, w_up, w_down, norm_gain):
         call = make_call(x_loc.shape[0], x_loc.shape[1], w_gate.shape[1], w_gate.shape[2])
-        return tuple(call(x_loc, dy_loc, w_gate, w_up, w_down, norm_gain)[:5])
+        return call(x_loc, dy_loc, w_gate, w_up, w_down, norm_gain)
 
     return jax.shard_map(device_fn, mesh=mesh, in_specs=(tok_spec, tok_spec, wide_spec, wide_spec, down_spec, gain_spec), out_specs=(tok_spec, wide_spec, wide_spec, down_spec, gain_spec), check_vma=False)

time: 315 us -> 303 us (0.962)
  local copies, waits for them, and re-layouts: 20.8 us -> 0.61 us
  Pallas kernels: 292 us -> 302 us
    unnamed x13 -> x3, local copies, waits for them, and re-layouts: 20.8 us -> 0.61 us
    pallas_call x1 -> x2, Pallas kernels: 292 us -> 302 us  [the longest x1 289 us: call(): y, g1, u1, d1, dgain, acc_g, acc_u, acc_d, other = step(*args)[:9]]
where the time goes in v4:
time: 303 us
  Pallas kernels  302 us (100%)
    pallas_call x1, Pallas kernels, call(): y, g1, u1, d1, dgain, acc_g, acc_u, acc_d, other = step(*args)[:9]  289 us
    pallas_call x1, Pallas kernels, call(): g, u, dd, y = end(*kept, *stored)  13.1 us

profile of v4, /device:TPU:0, one launch (start us, length us, event | category | flops | bytes accessed | tf_op | source)
XLA Modules:
  0.0 303.2 jit_solution(11599050552985103558)
XLA Ops:
  0.6 288.8 %shard_map.101 = (bf16[256,2048]{1,0:T(8,128)(2,1)}, f32[512,2048]{1,0:T(8,128)}, f32[512,2048]{1,0:T(8,128)}, f32[512,2048]{1,0:T(8,128)}, f32[2,2048]{1,0:T(2,...) custom-call(bf16[256,2048]{1,0:T(8,128)(2,1)} %x_in.1, ...), custom_call_target="tpu_custom_call" | custom-call | tf_op jit(solution)/shard_map/pallas_call | solution.py:1164
  289.4 0.0 copy-start
  289.4 13.1 %shard_map.102 = (f32[2,512,2048]{2,1,0:T(8,128)}, f32[2,512,2048]{2,1,0:T(8,128)}, f32[2,512,2048]{2,1,0:T(8,128)}, bf16[256,2048]{1,0:T(8,128)(2,1)}) custom-call(f32[1024,1024]{1,0:T(8,128)S(1)} %get-tuple-element.18.acc_g, f32[1024,1024]{1,0:T(8,128)S(1)} %get-tuple-element.19.acc_u, f32[512,2048]{1,0:T(8,128)S(1)} %get-tuple-element.20.acc_d, ...), custom_call_target="tpu_custom_call" | custom-call | tf_op jit(solution)/shard_map/pallas_call | solution.py:1167
  302.6 0.0 copy-done
  302.6 0.6 copy.12
Async XLA Ops:
  289.4 13.2 %copy-start = (f32[2,2048]{1,0:T(2,128)S(1)}, f32[2,2048]{1,0:T(2,128)}, u32[]{:S(2)}) copy-start(f32[2,2048]{1,0:T(2,128)} %get-tuple-element.40) | copy-start | bytes 49156

commit v5 on v4

--- a/solution.py
+++ b/solution.py
@@ -1,5 +1,6 @@
 import jax
 import jax.numpy as jnp
+import numpy as np
 from jax import lax
 from jax.experimental import pallas as pl
 from jax.experimental.pallas import tpu as pltpu
@@ -8,8 +9,8 @@
 F32 = jnp.float32
 BF16 = jnp.bfloat16
 MESH = pl.DeviceIdType.MESH
-NSEND = 174
-NRECV = 176
+NSEND = 62
+NRECV = 129
 NLOC = 55
 VLIM = 67043328 - 16 * 2**20 - 2**17
 VLIM2 = 14 * 2**20
@@ -65,7 +66,7 @@
     def cols(start, size):
         return pl.ds(start if isinstance(start, int) else pl.multiple_of(start, 128), size)
 
-    ids, sids, lids, sent, passed = {}, {}, {}, {}, {}
+    ids, sids, lids, sent, passed, groups = {}, {}, {}, {}, {}, {}
 
     def numbered(table, key, limit):
         i = table.setdefault(key, len(table))
@@ -83,9 +84,19 @@
         recv = sid(rkey) if isinstance(rkey, (str, tuple)) else rkey
         return pltpu.make_async_remote_copy(src_ref=src, dst_ref=dst, send_sem=ssem.at[send], recv_sem=rsem.at[recv], device_id=dev, device_id_type=MESH)
 
-    def push(key, make, rkey=None):
-        copy_of(key, key if rkey is None else rkey, *make()).start()
-        sent[key] = make
+    def push(key, make, rkey=None, group=None):
+        src, dst, dev = make()
+        copy_of(group or key, key if rkey is None else rkey, src, dst, dev).start()
+        if group is None:
+            sent[key] = make
+        else:
+            groups.setdefault(group, {})[key] = int(np.prod(src.shape))
+
+    def group_done(group):
+        n = sum(groups.pop(group).values()) // d
+        assert n % 2 == 0 and n <= 2 * hh, n
+        view = wd.at[:, pl.ds(0, n // 2)]
+        copy_of(group, 0, view, view, to_c).wait_send()
 
     def got(key, dst):
         with jax.named_scope("got_" + (name_of(key) if isinstance(key, (str, tuple)) else "dyn")):
@@ -94,11 +105,9 @@
     def send_done(key):
         copy_of(key, 0, *sent.pop(key)()).wait_send()
 
-    def flush(heads, layer=None):
-        for key in list(sent):
-            parts = (key,) if isinstance(key, str) else key
-            if parts[0] in heads and (layer is None or parts[0][0] != "w" or parts[1] == layer):
-                send_done(key)
+    def flush(keys):
+        for key in keys:
+            send_done(key)
 
     def local(key, src, dst):
         i = numbered(lids, key, NLOC)
@@ -124,18 +133,18 @@
         n = pieces[l]
         for xb in range(2):
             for k in range(n):
-                push(("wx", l, m, xb, k), lambda xb=xb, k=k: (wsrc(m, l, xb, cs, k, n), wview(m, l, f, xb, k, n), to_xs))
+                push(("wx", l, m, xb, k), lambda xb=xb, k=k: (wsrc(m, l, xb, cs, k, n), wview(m, l, f, xb, k, n), to_xs), group=("W", l))
         for k in range(4 * m):
             r0 = y * (fb // 2) + k * (fb // 8)
-            push(("wdx", l, k), lambda r0=r0: (wd_in.at[l, rows(r0, fb // 8)], wd.at[l, rows(x * fb + r0, fb // 8)], to_x))
+            push(("wdx", l, k), lambda r0=r0: (wd_in.at[l, rows(r0, fb // 8)], wd.at[l, rows(x * fb + r0, fb // 8)], to_x), group=("W", l))
         if (l, m) == (1, 1):
             r1 = yo * (fb // 2) + 3 * (fb // 8)
-            push("wdx_last", lambda: (wd_in.at[l, rows(r1, fb // 8)], wd.at[l, rows(x * fb + r1, fb // 8)], to_x))
+            push("wdx_last", lambda: (wd_in.at[l, rows(r1, fb // 8)], wd.at[l, rows(x * fb + r1, fb // 8)], to_x), group=("W", l))
 
     def push_wc(l):
         for m in range(2):
             for xb in range(2):
-                push(("wc", l, m, xb), lambda m=m, xb=xb: (wsrc(m, l, xb, co), wview(m, l, f, xb), to_c))
+                push(("wc", l, m, xb), lambda m=m, xb=xb: (wsrc(m, l, xb, co), wview(m, l, f, xb), to_c), ("wc", l, xb * (1 - l)), group=("W", l))
                 local(("w", l, m, xb), wsrc(m, l, xb, c), wview(m, l, f, xb)).start()
         local(("wd", l), wd_in.at[l], wd.at[l, rows(x * fb, fb)]).start()
 
@@ -144,26 +153,26 @@
         for k in range(n):
             ref = lambda k=k: wview(m, l, 2 * xo + cs, xb, k, n)
             got(("wx", l, m, xb, k), ref())
-            push(("wy", l, m, xb, k), lambda k=k: (ref(k), ref(k), to_y))
+            push(("wy", l, m, xb, k), lambda k=k: (ref(k), ref(k), to_y), ("wy", l, xb * (1 - l)), group=("W", l))
 
     def relay_d(l, k):
         ref = lambda: wd.at[l, rows(xo * fb + y * (fb // 2) + k * (fb // 8), fb // 8)]
         got(("wdx", l, k), ref())
-        push(("wdy", l, k), lambda: (ref(), ref(), to_y))
-
-    def have_gu(l, m, xb):
-        n = pieces[l]
-        local(("w", l, m, xb), wsrc(m, l, xb, c), wview(m, l, f, xb)).wait()
-        got(("wc", l, m, xb), wview(m, l, 2 * x + co, xb))
-        for k in range(n):
-            got(("wy", l, m, xb, k), wview(m, l, 2 * xo + cso, xb, k, n))
+        push(("wdy", l, k), lambda: (ref(), ref(), to_y), ("wdy", l), group=("W", l))
+
+    def have_gu(l, xbs):
+        for m in range(2):
+            for xb in xbs:
+                local(("w", l, m, xb), wsrc(m, l, xb, c), wview(m, l, f, xb)).wait()
+        whole = wd.at[0, pl.ds(0, 2 * len(xbs) * rb // 4)]
+        got(("wc", l, xbs[-1] * (1 - l)), whole)
+        got(("wy", l, xbs[-1] * (1 - l)), whole)
 
     def have_d_own(l):
         local(("wd", l), wd_in.at[l], wd.at[l, rows(x * fb, fb)]).wait()
 
     def have_d(l):
-        for k in range(4 - l):
-            got(("wdy", l, k), wd.at[l, rows(xo * fb + yo * (fb // 2) + k * (fb // 8), fb // 8)])
+        got(("wdy", l), wd.at[l, pl.ds(0, (4 - l) * (fb // 8))])
         if l == 1:
             got(("wdx", 1, 3), wd.at[1, rows(xo * fb + y * (fb // 2) + 3 * (fb // 8), fb // 8)])
             got("wdx_last", wd.at[1, rows(xo * fb + yo * (fb // 2) + 3 * (fb // 8), fb // 8)])
@@ -181,38 +190,30 @@
         return base + j
 
     def share(a, j, tag, ref):
-        push((a, "s", j, tag), lambda: (ref(), ref(), to_c), (a, "p", j))
+        push((a, "s", j, tag), lambda: (ref(), ref(), to_c), (a, "p", j), group=("S", a))
 
     def ag_x(a, buf, src, h):
-        push((a, "x", h), lambda: (src().at[pl.ds(h * half, half)], piece(buf, q, c, h * half, half), to_x))
+        push((a, "x", h), lambda: (src().at[pl.ds(h * half, half)], piece(buf, q, c, h * half, half), to_x), group=("X", a))
 
     def ag_y(a, buf, src, h):
-        push((a, "y", h), lambda: (src().at[pl.ds(h * half, half)], piece(buf, q, c, h * half, half), to_y))
+        push((a, "y", h), lambda: (src().at[pl.ds(h * half, half)], piece(buf, q, c, h * half, half), to_y), group=("X", a))
 
     def ag_quarter(a, buf, src, axis):
-        push((a, axis + "c"), lambda: (src().at[rows(z * ch, ch)], chunk(buf, q, c, z), to_y if axis == "y" else to_x))
-
-    def zb_id(a, axis, zi):
-        base = sid((a, axis, "zb", 0))
-        for i in range(4):
-            assert sid((a, axis, "zb", i)) == base + i
-        return base + zi
+        push((a, axis + "c"), lambda: (src().at[rows(z * ch, ch)], chunk(buf, q, c, z), to_y if axis == "y" else to_x), group=("S", a))
 
     def ag_spread(a, buf, axis):
         block = qy if axis == "y" else qx
         got((a, axis + "c"), chunk(buf, block, c, z))
         for k in (1, 2, 3):
-            push((a, axis, "zs", k), lambda k=k: (chunk(buf, block, c, z), chunk(buf, block, c, z), at_z(z_other(k))), zb_id(a, axis, z))
+            push((a, axis, "zs", k), lambda k=k: (chunk(buf, block, c, z), chunk(buf, block, c, z), at_z(z_other(k))), (a, axis, "zb"), group=("S", a))
 
     def ag_spread_got(a, buf, axis):
         block = qy if axis == "y" else qx
-        for k in (1, 2, 3):
-            with jax.named_scope("got_zb_" + a + axis):
-                got(zb_id(a, axis, z_other(k)), chunk(buf, block, c, z_other(k)))
+        got((a, axis, "zb"), buf.at[block, c, pl.ds(0, 3 * ch)])
         share(a, 0 if axis == "y" else 1, 0, lambda: buf.at[block, c])
 
     def ag_dx(a, buf, cut):
-        push((a, "dx"), lambda: (piece(buf, qy, c, 0, cut), piece(buf, qy, c, 0, cut), to_x))
+        push((a, "dx"), lambda: (piece(buf, qy, c, 0, cut), piece(buf, qy, c, 0, cut), to_x), group=("S", a))
 
     def ag_got_y(a, buf, h):
         got((a, "y", h), piece(buf, qy, c, h * half, half))
@@ -221,7 +222,7 @@
             ag_dx(a, buf, half)
 
     def ag_dy(a, buf, cut):
-        push((a, "dy", 0), lambda: (piece(buf, qx, c, cut, td - cut), piece(buf, qx, c, cut, td - cut), to_y))
+        push((a, "dy", 0), lambda: (piece(buf, qx, c, cut, td - cut), piece(buf, qx, c, cut, td - cut), to_y), group=("S", a))
 
     def ag_got_dy_whole(a, buf, cut):
         got((a, "dy", 0), piece(buf, qd, c, cut, td - cut))
@@ -235,7 +236,7 @@
         got((a, "x", h), piece(buf, qx, c, h * half, half))
         start, size = diag_piece(h, cut)
         if size:
-            push((a, "dy", h), lambda: (piece(buf, qx, c, start, size), piece(buf, qx, c, start, size), to_y))
+            push((a, "dy", h), lambda: (piece(buf, qx, c, start, size), piece(buf, qx, c, start, size), to_y), group=("S", a))
         share(a, 1, h, lambda: piece(buf, qx, c, h * half, half))
 
     def ag_got_dx(a, buf, cut):
@@ -258,9 +259,6 @@
     for a in ("n0", "o1", "n1", "o0"):
         for j in range(3):
             sid((a, "p", j))
-    for a, axis in (("n0", "y"), ("n0", "x"), ("o1", "y")):
-        for i in range(4):
-            sid((a, axis, "zb", i))
 
     def fwd_tile(l, n_ref, g_ref, i, a_ref=None, b_ref=None):
         w = cols(i * tile, tile)
@@ -480,7 +478,7 @@
 
     def z_push(key, make, zi):
         for k, dev in enumerate((toward,) if key in relayed else others):
-            push((key, "zs", k), lambda dev=dev: (*make(zi), at_z(dev)), zg_id(key, zi))
+            push((key, "zs", k), lambda dev=dev: (*make(zi), at_z(dev)), zg_id(key, zi), group=("X", key[:2]))
         if key in relayed:
             z_forward(key, 3, make(zi)[1], zg_id(key, zi), pair)
             passed[(key, "fw", 3)] = lambda: make(z)[1]
@@ -507,16 +505,14 @@
 
     def z_gather(key, ref):
         z_push(key, lambda zi: (quarter(ref, c, zi), quarter(ref, c, zi)), z)
-        push((key, "s", 0), lambda: (quarter(ref, c, z), quarter(ref, c, z), to_c))
+        push((key, "s", 0), lambda: (quarter(ref, c, z), quarter(ref, c, z), to_c), (key, "s"), group=("X", key[:2]))
 
     def z_take(key, ref, i):
         z_pass(key, lambda zi: (quarter(ref, c, zi), quarter(ref, c, zi)), i)
-        push((key, "s", 1 + i), lambda: (quarter(ref, c, takes(key)[i]), quarter(ref, c, takes(key)[i]), to_c))
+        push((key, "s", 1 + i), lambda: (quarter(ref, c, takes(key)[i]), quarter(ref, c, takes(key)[i]), to_c), (key, "s"), group=("X", key[:2]))
 
     def z_gathered_partner(key, ref):
-        got((key, "s", 0), quarter(ref, co, z))
-        for i in range(3):
-            got((key, "s", 1 + i), quarter(ref, co, takes(key)[i]))
+        got((key, "s"), ref.at[rows(co * td, td)])
 
     def stage(buf, block, slot_ref, key):
         for core in range(2):
@@ -559,7 +555,7 @@
     def grads_push(l):
         for i in range(2):
             for xb in range(2):
-                push(("q", l, i, xb), lambda i=i, xb=xb: (grad_piece(i, xb, co), grad_land(l, i, xb, c), to_c))
+                push(("q", l, i, xb), lambda i=i, xb=xb: (grad_piece(i, xb, co), grad_land(l, i, xb, c), to_c), ("q", l))
 
     def grads_out():
         for i in range(2):
@@ -574,7 +570,7 @@
                 if l == 1:
                     local(("qo", i, xb), grad_piece(i, xb, c), grad_land(1, i, xb, c)).wait()
                 send_done(("q", l, i, xb))
-                got(("q", l, i, xb), grad_land(l, i, xb, co))
+        got(("q", l), acc_d)
         if l == 1:
             local("qd", acc_d, dwd1).wait()
 
@@ -653,14 +649,12 @@
     got("rp", r_own.at[rows(co * td, td)])
     keep2 = local("n0k2", nb.at[0, rows(co * td, td)], n0_buf.at[q, co])
     keep2.start()
-    have_gu(0, 0, 0)
-    have_gu(0, 1, 0)
+    have_gu(0, (0,))
     with jax.named_scope("fwd_tile0"):
         fwd_tile(0, nb.at[0], g_t, 0)
     relay_d(0, 0)
     relay_d(0, 1)
-    have_gu(0, 0, 1)
-    have_gu(0, 1, 1)
+    have_gu(0, (1,))
     with jax.named_scope("fwd_tile1"):
         for i in range(1, hh // tile):
             fwd_tile(0, nb.at[0], g_t, i)
@@ -707,7 +701,8 @@
         h1_done()
 
     local("dyc", dy_in.at[rows(z * ch, ch)], x_ch).start()
-    flush(("wx", "wdx", "wc", "wy", "wdy", "xp", "dyp", "rp"), 0)
+    group_done(("W", 0))
+    flush(("xp", "dyp", "rp"))
     relay_d(1, 0)
     z_take("n1z", n_own, 0)
     z_take("n1z", n_own, 1)
@@ -725,9 +720,7 @@
     dy_other.start()
     z_gathered_partner("n1z", n_own)
 
-    for m in range(2):
-        for xb in range(2):
-            have_gu(1, m, xb)
+    have_gu(1, (0, 1))
     fwd(1, n_own, g_t)
     local("dy_own", dy_in, ob.at[0, rows(c * td, td)]).wait()
     dy_other.wait()
@@ -875,16 +868,14 @@
 
             @at_step(k, 1)
             def _():
-                for key in [("n1z", "zs", 0)] + [("n1z", "s", i) for i in range(4)] + [("n1", axis, h) for axis in "xy" for h in range(2)]:
-                    send_done(key)
+                group_done(("X", "n1"))
                 passed_done("n1z")
                 local("gl", g_save, own_g).start()
 
             @at_step(k, 3)
             def _():
                 z_relay("d2", 0, 0)
-                for key in [k1 for k1 in sent if k1[0] in ("wy", "wdy") and k1[1] == 1]:
-                    send_done(key)
+                group_done(("W", 1))
                 for i in range(3):
                     for s in load_ab(block_of(i - 1) if i else q, i):
                         s.start()
@@ -933,16 +924,9 @@
     grads_push(1)
     grads_out()
 
-    def gz_id(zi):
-        base = sid(("gz", 0))
-        for i in range(4):
-            assert sid(("gz", i)) == base + i
-        return base + zi
-
     def y_rows(zi):
         return y_out.at[rows(zi * ch, ch)]
 
-    gz_id(0)
     zg_id("y", 0)
 
     @scoped
@@ -970,6 +954,11 @@
 
     def l0_step(k, carry):
         oslot = (k + 1) % 2
+
+        @at_step(k, 2)
+        def _():
+            ag_got_dx("o0", o0_buf, half)
+            ag_got_dy("o0", o0_buf, 1, half)
 
         @pl.when(k > 0)
         def _():
@@ -987,7 +976,7 @@
             dgain0()
             dg_z[z] = dg[...]
             for i in range(3):
-                push(("gs", i), lambda i=i: (dg_z.at[z], dg_z.at[z], at_z(others[i])), gz_id(z))
+                push(("gs", i), lambda i=i: (dg_z.at[z], dg_z.at[z], at_z(others[i])), "gz")
             z_relay("d2", 1, 1)
             partner_has("n0", n0_buf, 2)
             stage_n(n0_buf, block_of(2), 0)
@@ -1013,12 +1002,10 @@
                 for s in "BC":
                     copy_of(("d2", s, h), 0, mine(0, h), slot("d2", 0, h), at_z(pair)).wait_send()
             partner_has("o0", o0_buf, 1)
-            for key in [("o0z", "zs", i) for i in range(3)] + [("o0z", "s", i) for i in range(4)] + [("o0", axis, h) for axis in "xy" for h in range(2)]:
-                send_done(key)
+            group_done(("X", "o0"))
             stage_o(o0_buf, block_of(1), 1)
+            got("gz", dg_z.at[pl.ds(0, 3)])
             for i in range(3):
-                with jax.named_scope("got_gz"):
-                    got(gz_id(others[i]), dg_z.at[others[i]])
                 send_done(("gs", i))
             dg[...] = dg_z[0] + dg_z[1] + dg_z[2] + dg_z[3]
             push("gc", lambda: (dg, dg_core, to_c))
@@ -1029,8 +1016,6 @@
             copy_of("gc", 0, dg, dg_core, to_c).wait_send()
             dg[...] = dg[...] + dg_core[...]
             push("gx", lambda: (dg, dg_x, to_x))
-            ag_got_dx("o0", o0_buf, half)
-            ag_got_dy("o0", o0_buf, 1, half)
             partner_has("o0", o0_buf, 2)
             stage_o(o0_buf, block_of(2), 0)
 
@@ -1051,17 +1036,21 @@
         @at_step(k, 0)
         def _():
             staged_n(n0_buf, block_of(2), 0)
-            with jax.named_scope("f0_last"):
-                fwd(0, nb.at[0], None, a_kept(3), b_kept(3))
-
-            @pl.when(outer == 1)
-            def _():
-                y_done()
-
+            with jax.named_scope("f0_a"):
+                fwd_tile(0, nb.at[0], None, 0, a_kept(3), b_kept(3))
             ag_got_x("o0", o0_buf, 0, half)
             ag_got_y("o0", o0_buf, 1)
             ag_got_x("o0", o0_buf, 1, half)
-            flush(("wx", "wdx", "wdx_last", "wc", "n0", "o1", "n1"))
+            with jax.named_scope("f0_b"):
+                for i in range(1, hh // tile):
+                    fwd_tile(0, nb.at[0], None, i, a_kept(3), b_kept(3))
+
+            @pl.when(outer == 1)
+            def _():
+                y_done()
+
+            for a in ("n0", "o1", "n1"):
+                group_done(("S", a))
             partner_has("o0", o0_buf, 0)
             stage_o(o0_buf, block_of(0), 0)
 
@@ -1086,6 +1075,8 @@
     grads_out_done(0)
     for key in list(sent):
         send_done(key)
+    for group in list(groups):
+        group_done(group)
     assert not passed
 
 

time: 303 us -> 299 us (0.987)
  Pallas kernels: 302 us -> 298 us
    pallas_call x1, Pallas kernels: 289 us -> 285 us  [call(): y, g1, u1, d1, dgain, acc_g, acc_u, acc_d, other = step(*args)[:9]]
where the time goes in v5:
time: 299 us
  Pallas kernels  298 us (100%)
    pallas_call x1, Pallas kernels, call(): y, g1, u1, d1, dgain, acc_g, acc_u, acc_d, other = step(*args)[:9]  285 us
    pallas_call x1, Pallas kernels, call(): g, u, dd, y = end(*kept, *stored)  13.1 us

profile of v5, /device:TPU:0, one launch (start us, length us, event | category | flops | bytes accessed | tf_op | source)
XLA Modules:
  0.0 299.1 jit_solution(1487163557340614499)
XLA Ops:
  0.6 284.7 %shard_map.101 = (bf16[256,2048]{1,0:T(8,128)(2,1)}, f32[512,2048]{1,0:T(8,128)}, f32[512,2048]{1,0:T(8,128)}, f32[512,2048]{1,0:T(8,128)}, f32[2,2048]{1,0:T(2,...) custom-call(bf16[256,2048]{1,0:T(8,128)(2,1)} %x_in.1, ...), custom_call_target="tpu_custom_call" | custom-call | tf_op jit(solution)/shard_map/pallas_call | solution.py:1155
  285.3 0.0 copy-start
  285.3 13.1 %shard_map.102 = (f32[2,512,2048]{2,1,0:T(8,128)}, f32[2,512,2048]{2,1,0:T(8,128)}, f32[2,512,2048]{2,1,0:T(8,128)}, bf16[256,2048]{1,0:T(8,128)(2,1)}) custom-call(f32[1024,1024]{1,0:T(8,128)S(1)} %get-tuple-element.18.acc_g, f32[1024,1024]{1,0:T(8,128)S(1)} %get-tuple-element.19.acc_u, f32[512,2048]{1,0:T(8,128)S(1)} %get-tuple-element.20.acc_d, ...), custom_call_target="tpu_custom_call" | custom-call | tf_op jit(solution)/shard_map/pallas_call | solution.py:1158
  298.5 0.0 copy-done
  298.5 0.6 copy.12
Async XLA Ops:
  285.3 13.2 %copy-start = (f32[2,2048]{1,0:T(2,128)S(1)}, f32[2,2048]{1,0:T(2,128)}, u32[]{:S(2)}) copy-start(f32[2,2048]{1,0:T(2,128)} %get-tuple-element.40) | copy-start | bytes 49156

commit v6 on v5

--- a/solution.py
+++ b/solution.py
@@ -9,8 +9,8 @@
 F32 = jnp.float32
 BF16 = jnp.bfloat16
 MESH = pl.DeviceIdType.MESH
-NSEND = 62
-NRECV = 129
+NSEND = 65
+NRECV = 130
 NLOC = 55
 VLIM = 67043328 - 16 * 2**20 - 2**17
 VLIM2 = 14 * 2**20
@@ -329,7 +329,7 @@
             bwd_tile(l, o_ref, i, a_ref, b_ref)
 
     @scoped
-    def weight_grads(n_ref, col, o_ref, between):
+    def weight_grads(n_ref, col, o_ref, theirs):
         t = min(256, fb)
 
         def half_rows(core):
@@ -339,9 +339,13 @@
                 acc_g[w, :] += mm(n_rows, a_t[...], 0, 0)
                 acc_u[w, :] += mm(n_rows, b_t[...], 0, 0)
 
-        half_rows(co)
-        if between is not None:
-            between()
+        if theirs is None:
+            half_rows(co)
+        else:
+            @pl.when(theirs)
+            def _():
+                half_rows(co)
+
         half_rows(c)
         for i in range(fb // t):
             acc_d[pl.ds(i * t, t), :] += mm(g_t[:, cols(x * fb + i * t, t)], o_ref[...], 0, 0)
@@ -573,6 +577,13 @@
         got(("q", l), acc_d)
         if l == 1:
             local("qd", acc_d, dwd1).wait()
+        else:
+            got("dab", nb.at[0])
+            for i in range(2):
+                w = pl.ds(i * hh, hh)
+                part[:, w] += mm(n_half(3)[:, rows(c * rb, rb)], their_d(i)[...], 0, 0)
+            for i in range(2):
+                send_done(("dab", i))
 
     barrier = pltpu.get_barrier_semaphore()
     for dev in (to_c, to_x, {"fsdp": 2 * xo + co}, to_y, at_z((z + 1) % 4), at_z((z + 2) % 4), at_z((z + 3) % 4)):
@@ -613,7 +624,7 @@
     push_w(0, 1)
     push_w(1, 0)
     push_w(1, 1)
-    ag_x("o1", o1_buf, dy_src, 0)
+    ag_x("o1", o1_buf, dy_src, 1)
     push("xp", lambda: (x_in, x_part, to_c))
     push("dyp", lambda: (dy_in, o1_buf.at[q, c], to_c))
     push_wc(1)
@@ -710,9 +721,9 @@
     z_take("n1z", n_own, 2)
     relay_d(1, 2)
     saves_done(block_of(0))
-    for h in range(2):
+    for h in (1, 0):
         ag_x("n1", n1_buf, n1_src, h)
-    ag_x("o1", o1_buf, dy_src, 1)
+    ag_x("o1", o1_buf, dy_src, 0)
     for h in range(2):
         ag_y("n1", n1_buf, n1_src, h)
     got("dyp", o1_buf.at[q, co])
@@ -808,7 +819,7 @@
 
             @at_step(k, 2)
             def _():
-                ag_got_x("o1", o1_buf, 1, cut_o)
+                ag_got_x("o1", o1_buf, 0, cut_o)
 
             @at_step(k, 3)
             def _():
@@ -834,13 +845,13 @@
                 for i in range(3):
                     z_take("o0z", o_own, i)
                 for h in range(2):
-                    ag_x("o0", o0_buf, o0_src, h)
+                    ag_x("o0", o0_buf, o0_src, 1 - h)
                     ag_y("o0", o0_buf, o0_src, h)
 
             @at_step(k, 1)
             def _():
                 z_relay("d1", 1, 0)
-                ag_got_x("n1", n1_buf, 1, half)
+                ag_got_x("n1", n1_buf, 0, half)
 
             staged_o(o1_buf, block_of(k - 1), 0)
             bwd_hidden(1, ob.at[0], a_t, b_t)
@@ -898,8 +909,8 @@
         def _():
             staged(n0_buf, block_of(1), nb.at[0], "sn")
             f0_other(1, 0)
-            ag_got_x("o1", o1_buf, 0, cut_o)
-            ag_got_x("n1", n1_buf, 0, half)
+            ag_got_x("o1", o1_buf, 1, cut_o)
+            ag_got_x("n1", n1_buf, 1, half)
             z_relay("d1", 0, 0)
             ag_got_y("n1", n1_buf, 0)
             ag_dx("o1", o1_buf, cut_o)
@@ -950,7 +961,19 @@
 
         lax.fori_loop(0, ch // 16, y_step, 0)
         local("yk", x_ch, y_rows(z)).start()
-        z_push("y", lambda zi: (x_ch, y_rows(zi)), z)
+        for i, dev in enumerate((far_inner, pair)):
+            push(("y", i), lambda dev=dev: (x_ch, y_rows(z), at_z(dev)), zg_id("y", z), group=("X", "y"))
+
+        @pl.when(outer == 1)
+        def _():
+            copy_of(("y", 2), zg_id("y", z), x_ch, y_rows(z), at_z(far_outer)).start()
+
+    def y_pass():
+        got(zg_id("y", far_inner), y_rows(far_inner))
+        copy_of(("y", 2), zg_id("y", far_inner), y_rows(far_inner), y_rows(far_inner), at_z(pair)).start()
+
+    def their_d(i):
+        return nb.at[0, :, pl.ds(i * hh, hh)]
 
     def l0_step(k, carry):
         oslot = (k + 1) % 2
@@ -982,6 +1005,7 @@
             stage_n(n0_buf, block_of(2), 0)
             load_n_half(block_of(2), 3)
             ag_got_y("o0", o0_buf, 0)
+            ag_got_x("o0", o0_buf, 1, half)
             grads_out_done(1)
             zero_acc()
             for i in range(4):
@@ -1026,33 +1050,41 @@
             dg[...] = dg[...] + dg_x[...]
             push("gy", lambda: (dg, dg_y, to_y))
 
-        def between():
-            @at_step(k, 3)
-            def _():
-                grads_push(0)
-
-        weight_grads(n_half(k), 0, ob.at[oslot], between)
+            @pl.when(inner == 1)
+            def _():
+                y_pass()
+
+        @at_step(k, 3)
+        def _():
+            for i in range(2):
+                push(("dab", i), lambda i=i: ((a_t, b_t)[i], their_d(i), to_c), "dab")
+
+        weight_grads(n_half(k), 0, ob.at[oslot], k < 3)
+
+        @at_step(k, 2)
+        def _():
+            grads_push(0)
 
         @at_step(k, 0)
         def _():
             staged_n(n0_buf, block_of(2), 0)
             with jax.named_scope("f0_a"):
                 fwd_tile(0, nb.at[0], None, 0, a_kept(3), b_kept(3))
+            ag_got_y("o0", o0_buf, 1)
             ag_got_x("o0", o0_buf, 0, half)
-            ag_got_y("o0", o0_buf, 1)
-            ag_got_x("o0", o0_buf, 1, half)
             with jax.named_scope("f0_b"):
                 for i in range(1, hh // tile):
                     fwd_tile(0, nb.at[0], None, i, a_kept(3), b_kept(3))
 
+            partner_has("o0", o0_buf, 0)
+            stage_o(o0_buf, block_of(0), 0)
+
             @pl.when(outer == 1)
             def _():
                 y_done()
 
             for a in ("n0", "o1", "n1"):
                 group_done(("S", a))
-            partner_has("o0", o0_buf, 0)
-            stage_o(o0_buf, block_of(0), 0)
 
         return carry
 
@@ -1068,11 +1100,17 @@
     got("gy", dg_y)
     copy_of("gy", 0, dg, dg_y, to_y).wait_send()
     dgain_out[...] = dg[...] + dg_y[...]
-    for i in range(3):
-        with jax.named_scope("got_y"):
-            z_pass("y", lambda zi: (x_ch, y_rows(zi)), i)
+    grads_out_done(0)
+    with jax.named_scope("got_y"):
+        got(zg_id("y", pair), y_rows(pair))
+        got(zg_id("y", far_outer), y_rows(far_outer))
+
+        @pl.when(outer == 1)
+        def _():
+            got(zg_id("y", far_inner), y_rows(far_inner))
+
+        copy_of(("y", 2), 0, x_ch, x_ch, to_c).wait_send()
     local("yk", x_ch, y_rows(z)).wait()
-    grads_out_done(0)
     for key in list(sent):
         send_done(key)
     for group in list(groups):
@@ -1080,7 +1118,7 @@
     assert not passed
 
 
-def finish(acc_g, acc_u, acc_d, other, g1, u1, d1, y_in, g_out, u_out, d_out, y_out, buf, ybuf, sem_in, sem_out):
+def finish(acc_g, acc_u, acc_d, other, gain_in, g1, u1, d1, y_in, g_out, u_out, d_out, y_out, gain_out, buf, ybuf, sem_in, sem_out):
     rb, hh = other.shape[0], acc_g.shape[1]
     fb = hh // 2
     f = lax.axis_index("fsdp")
@@ -1103,6 +1141,7 @@
             theirs = pl.ds(pl.multiple_of((2 * xb + 1 - c) * fb, 128), fb)
             out(other.at[:, pl.ds(i * hh + xb * fb, fb)], dst.at[0, :, theirs])
     out(acc_d, d_out.at[0])
+    out(gain_in, gain_out)
     for i, dst in enumerate((g_out, u_out, d_out)):
         ins[i].wait()
         out(buf.at[i], dst.at[1])
@@ -1120,7 +1159,7 @@
     vmem = pl.BlockSpec(memory_space=pltpu.VMEM)
     block = shape((4, 2, td, d), BF16)
     outs = [
-        shape((td, d), BF16), shape((rb, hs), F32), shape((rb, hs), F32), shape((fb, d), F32), shape((2, d), F32),
+        shape((td, d), BF16), shape((rb, hs), F32), shape((rb, hs), F32), shape((fb, d), F32), pltpu.VMEM((2, d), F32),
         pltpu.VMEM((2 * rb, hh), F32), pltpu.VMEM((2 * rb, hh), F32), pltpu.VMEM((fb, d), F32), pltpu.VMEM((t2, d), F32),
         block, block, block, block, shape((4, t2, hh), BF16), shape((4, t2, hh), BF16), shape((td, d), BF16), shape((t2, hh), BF16), shape((td, d), F32),
     ]
@@ -1144,18 +1183,18 @@
     )
     end = pl.pallas_call(
         finish,
-        out_shape=[shape((2, rb, hs), F32), shape((2, rb, hs), F32), shape((2, fb, d), F32), shape((td, d), BF16)],
-        in_specs=[vmem] * 4 + [hbm] * 4,
-        out_specs=[hbm] * 4,
-        scratch_shapes=[pltpu.VMEM((3, rb, hs), F32), pltpu.VMEM((td, d), BF16), pltpu.SemaphoreType.DMA((4,)), pltpu.SemaphoreType.DMA((13,))],
+        out_shape=[shape((2, rb, hs), F32), shape((2, rb, hs), F32), shape((2, fb, d), F32), shape((td, d), BF16), shape((2, d), F32)],
+        in_specs=[vmem] * 5 + [hbm] * 4,
+        out_specs=[hbm] * 5,
+        scratch_shapes=[pltpu.VMEM((3, rb, hs), F32), pltpu.VMEM((td, d), BF16), pltpu.SemaphoreType.DMA((4,)), pltpu.SemaphoreType.DMA((14,))],
         compiler_params=pltpu.CompilerParams(vmem_limit_bytes=VLIM2),
     )
 
     def call(*args):
         y, g1, u1, d1, dgain, acc_g, acc_u, acc_d, other = step(*args)[:9]
-        kept = [pltpu.with_memory_space_constraint(v, pltpu.VMEM) for v in (acc_g, acc_u, acc_d, other)]
+        kept = [pltpu.with_memory_space_constraint(v, pltpu.VMEM) for v in (acc_g, acc_u, acc_d, other, dgain)]
         stored = [pltpu.with_memory_space_constraint(v, pltpu.HBM) for v in (g1, u1, d1, y)]
-        g, u, dd, y = end(*kept, *stored)
+        g, u, dd, y, dgain = end(*kept, *stored)
         return y, g, u, dd, dgain
 
     return call

time: 299 us -> 298 us (level)
  no operation moved by 1% of the time
where the time goes in v6:
time: 298 us; the launch traced here: 297 us
  Pallas kernels  296 us (99%)
    pallas_call x1, Pallas kernels, call(): y, g1, u1, d1, dgain, acc_g, acc_u, acc_d, other = step(*args)[:9]  283 us
    pallas_call x1, Pallas kernels, call(): g, u, dd, y, dgain = end(*kept, *stored)  13.1 us

profile of v6, /device:TPU:0, one launch (start us, length us, event | category | flops | bytes accessed | tf_op | source)
XLA Modules:
  0.0 296.9 jit_solution(17045618056918661528)
XLA Ops:
  0.6 283.0 %shard_map.101 = (bf16[256,2048]{1,0:T(8,128)(2,1)}, f32[512,2048]{1,0:T(8,128)}, f32[512,2048]{1,0:T(8,128)}, f32[512,2048]{1,0:T(8,128)}, f32[2,2048]{1,0:T(2,...) custom-call(bf16[256,2048]{1,0:T(8,128)(2,1)} %x_in.1, ...), custom_call_target="tpu_custom_call" | custom-call | tf_op jit(solution)/shard_map/pallas_call | solution.py:1194
  283.6 13.1 %shard_map.102 = (f32[2,512,2048]{2,1,0:T(8,128)}, f32[2,512,2048]{2,1,0:T(8,128)}, f32[2,512,2048]{2,1,0:T(8,128)}, bf16[256,2048]{1,0:T(8,128)(2,1)}, f32[2,2048]{1,0:T(2,128)}) custom-call(f32[1024,1024]{1,0:T(8,128)S(1)} %get-tuple-element.19.acc_g, f32[1024,1024]{1,0:T(8,128)S(1)} %get-tuple-element.20.acc_u, f32[512,2048]{1,0:T(8,128)S(1)} %get-tuple-element.21.acc_d, ...), custom_call_target="tpu_custom_call" | custom-call | tf_op jit(solution)/shard_map/pallas_call | solution.py:1197

commit v7 on v6

--- a/solution.py
+++ b/solution.py
@@ -987,6 +987,10 @@
         def _():
             staged_o_any(k)
 
+        @pl.when(k * inner == 3)
+        def _():
+            y_pass()
+
         bwd_hidden(0, ob.at[oslot], a_kept(k), b_kept(k))
 
         @at_step(k, 0)
@@ -1049,10 +1053,6 @@
             copy_of("gx", 0, dg, dg_x, to_x).wait_send()
             dg[...] = dg[...] + dg_x[...]
             push("gy", lambda: (dg, dg_y, to_y))
-
-            @pl.when(inner == 1)
-            def _():
-                y_pass()
 
         @at_step(k, 3)
         def _():

time: 298 us -> 298 us (level)
  no operation moved by 1% of the time
where the time goes in v7:
time: 298 us; the launch traced here: 297 us
  Pallas kernels  296 us (99%)
    pallas_call x1, Pallas kernels, call(): y, g1, u1, d1, dgain, acc_g, acc_u, acc_d, other = step(*args)[:9]  283 us
    pallas_call x1, Pallas kernels, call(): g, u, dd, y, dgain = end(*kept, *stored)  13.1 us

profile of v7, /device:TPU:0, one launch (start us, length us, event | category | flops | bytes accessed | tf_op | source)
XLA Modules:
  0.0 296.9 jit_solution(16114261196577196650)
XLA Ops:
  0.6 283.0 %shard_map.101 = (bf16[256,2048]{1,0:T(8,128)(2,1)}, f32[512,2048]{1,0:T(8,128)}, f32[512,2048]{1,0:T(8,128)}, f32[512,2048]{1,0:T(8,128)}, f32[2,2048]{1,0:T(2,...) custom-call(bf16[256,2048]{1,0:T(8,128)(2,1)} %x_in.1, ...), custom_call_target="tpu_custom_call" | custom-call | tf_op jit(solution)/shard_map/pallas_call | solution.py:1194
  283.6 13.1 %shard_map.102 = (f32[2,512,2048]{2,1,0:T(8,128)}, f32[2,512,2048]{2,1,0:T(8,128)}, f32[2,512,2048]{2,1,0:T(8,128)}, bf16[256,2048]{1,0:T(8,128)(2,1)}, f32[2,2048]{1,0:T(2,128)}) custom-call(f32[1024,1024]{1,0:T(8,128)S(1)} %get-tuple-element.19.acc_g, f32[1024,1024]{1,0:T(8,128)S(1)} %get-tuple-element.20.acc_u, f32[512,2048]{1,0:T(8,128)S(1)} %get-tuple-element.21.acc_d, ...), custom_call_target="tpu_custom_call" | custom-call | tf_op jit(solution)/shard_map/pallas_call | solution.py:1197
